TPU v7x, 128 devices: a whole 4x4x4 slice. The times are simulated.
128 devices in a mesh: mem: 4 (over y_lo, core), lat: 4 (over z), lon: 8 (over y_hi, x).
Axes of the slice: x: 4, y: 4 (y_hi: 2, y_lo: 2; y = y_hi * 2 + y_lo), z: 4, core: 2. Of those that a mesh axis runs over, the one named last changes fastest.
Arguments:
- fields: bfloat16 [4, 2, 96, 384, 512], P('mem', None, 'lat', 'lon'), may hold values from -6 to 6
- region: int32 [96, 384], P('lat', 'lon'), may hold values from 0 to 2
- gain_attn: float32 [512], replicated, may hold values from 0.1 to 1.9
- w_qkv: bfloat16 [512, 1536], P(None, ('mem', 'lat', 'lon')), may hold values from -1 to 1
- w_proj: bfloat16 [512, 512], P(None, ('mem', 'lat', 'lon')), may hold values from -0.25 to 0.25
- gain_mlp: float32 [512], replicated, may hold values from 0.1 to 1.9
- w_up: bfloat16 [512, 2048], P(None, ('mem', 'lat', 'lon')), may hold values from -0.25 to 0.25
- w_down: bfloat16 [2048, 512], P(None, ('mem', 'lat', 'lon')), may hold values from -0.125 to 0.125
Outputs:
- updated: bfloat16 [4, 2, 96, 384, 512], P('mem', None, 'lat', 'lon')
All inputs are finite; a program needn't handle non-finite values.
Results may differ from a plain program's by a relative error of at most 0.011.
Values may be sent and summed in bfloat16 or wider, within the bound.
No kernel may reach another device: no remote copies, remote signals or barrier semaphores. Data moves between devices by JAX's collectives and lax.ppermute only.
A program may use at most 192 MiB of HBM per device.

v0:
```python
import jax
import jax.numpy as jnp
from jax import lax
from jax.sharding import PartitionSpec as P

HEADS = 16
HDIM = 32
WLAT = 6
WLON = 12
SH = 3
SL = 6


eps = 1e-05


def in_order(pieces, dim):
    pieces = jnp.moveaxis(pieces, 0, dim)
    shape = pieces.shape
    return pieces.reshape(*shape[:dim], shape[dim] * shape[dim + 1], *shape[dim + 2 :])


def one_gather(arrays, axis, dims):
    flat = jnp.concatenate([a.reshape(-1) for a in arrays])
    lines, at, gathered = (lax.all_gather(flat, axis), 0, [])
    for a, dim in zip(arrays, dims):
        pieces = lines[:, at : at + a.size].reshape(-1, *a.shape)
        gathered.append(in_order(pieces, dim))
        at += a.size
    return tuple(gathered)


def shifted_2(block, axis, distance):
    devices = range(lax.axis_size(axis))
    route = [((i - distance) % len(devices), i) for i in devices]
    return lax.ppermute(block, axis, route)


def layer_norm(values, gain_vec):
    values = values.astype(jnp.float32)
    average = jnp.mean(values, axis=-1, keepdims=True)
    centred = values - average
    variance = jnp.mean(centred * centred, axis=-1, keepdims=True)
    return (centred * lax.rsqrt(variance + eps) * gain_vec).astype(jnp.bfloat16)


def attend(qkv_all, region_ids, north_side, height):
    levels, row_count, col_count, width3 = qkv_all.shape
    width = width3 // 3
    band_count = row_count // height
    win_count = col_count // WLON
    win_tok = levels * height * WLON
    windowed = qkv_all.reshape(levels, band_count, height, win_count, WLON, width3)
    windowed = windowed.transpose(1, 3, 0, 2, 4, 5).reshape(
        band_count * win_count, win_tok, 3, HEADS, width // HEADS
    )
    ids_full = jnp.broadcast_to(region_ids[None], (levels, row_count, col_count))
    ids_full = ids_full.reshape(levels, band_count, height, win_count, WLON).transpose(
        1, 3, 0, 2, 4
    )
    ids_full = ids_full.reshape(band_count * win_count, win_tok)
    north_full = jnp.broadcast_to(north_side[None, :, None], (levels, row_count, col_count))
    north_full = north_full.reshape(levels, band_count, height, win_count, WLON).transpose(
        1, 3, 0, 2, 4
    )
    north_full = north_full.reshape(band_count * win_count, win_tok)
    scores = jnp.einsum(
        "wqhd,wkhd->whqk", windowed[:, :, 0], windowed[:, :, 1], preferred_element_type=jnp.float32
    )
    scores = scores * (1.0 / HDIM**0.5)
    allow = (ids_full[:, :, None] == ids_full[:, None, :]) & (
        north_full[:, :, None] == north_full[:, None, :]
    )
    scores = jnp.where(allow[:, None], scores, -1000000000.0)
    attn_probs = jax.nn.softmax(scores, axis=-1).astype(jnp.bfloat16)
    mixed_heads = jnp.einsum(
        "whqk,wkhd->wqhd", attn_probs, windowed[:, :, 2], preferred_element_type=jnp.float32
    )
    mixed_heads = mixed_heads.astype(jnp.bfloat16).reshape(
        band_count, win_count, levels, height, WLON, width
    )
    return mixed_heads.transpose(2, 0, 3, 1, 4, 5).reshape(levels, row_count, col_count, width)


def body(fields, region, gain_attn, w_qkv, w_proj, gain_mlp, w_up, w_down):
    gathered = one_gather((w_qkv, w_proj, w_up, w_down), ("mem", "lat", "lon"), (1, 1, 1, 1))
    member = fields[0]
    levels, clat, clon, width = member.shape
    normed = layer_norm(member, gain_attn)
    region_ids = region.astype(jnp.bfloat16)
    lat_pos = lax.axis_index("lat")
    nlat_all = clat * lax.axis_size("lat")
    row_ids = jnp.arange(clat, dtype=jnp.int32)
    north_side = (lat_pos * clat + SH + row_ids) % nlat_all < SH
    arrived, arrived_ids = shifted_2((normed[:, :SH], region_ids[:SH]), "lat", -1)
    lat_band = jnp.concatenate([normed[:, SH:], arrived], axis=1)
    band_ids = jnp.concatenate([region_ids[SH:], arrived_ids], axis=0)
    strip, strip_ids = shifted_2((lat_band[:, :, :SL], band_ids[:, :SL]), "lon", -1)
    shifted = jnp.concatenate([lat_band[:, :, SL:], strip], axis=2)
    shifted_ids = jnp.concatenate([band_ids[:, SL:], strip_ids], axis=1)
    qkv_all = (
        jnp.dot(shifted.reshape(-1, width), gathered[0], preferred_element_type=jnp.float32)
        .astype(jnp.bfloat16)
        .reshape(levels, clat, clon, 3 * width)
    )
    mixed_heads = attend(qkv_all, shifted_ids, north_side, WLAT)
    attn_out = (
        jnp.dot(mixed_heads.reshape(-1, width), gathered[1], preferred_element_type=jnp.float32)
        .astype(jnp.bfloat16)
        .reshape(levels, clat, clon, width)
    )
    arrived_cols = shifted_2(attn_out[:, :, clon - SL :], "lon", 1)
    attn_out = jnp.concatenate([arrived_cols, attn_out[:, :, : clon - SL]], axis=2)
    arrived_rows = shifted_2(attn_out[:, clat - SH :], "lat", 1)
    attn_out = jnp.concatenate([arrived_rows, attn_out[:, : clat - SH]], axis=1)
    resid = (member.astype(jnp.float32) + attn_out.astype(jnp.float32)).astype(jnp.bfloat16)
    normed2 = layer_norm(resid, gain_mlp).reshape(-1, width)
    pre_act = jnp.dot(normed2, gathered[2], preferred_element_type=jnp.float32)
    hidden = jax.nn.gelu(pre_act, approximate=False).astype(jnp.bfloat16)
    delta = jnp.dot(hidden, gathered[3], preferred_element_type=jnp.float32).reshape(
        levels, clat, clon, width
    )
    updated = (resid.astype(jnp.float32) + delta).astype(jnp.bfloat16)
    return updated[None]


def solution(mesh):
    in_specs = (
        P("mem", None, "lat", "lon", None),
        P("lat", "lon"),
        P(),
        P(None, ("mem", "lat", "lon")),
        P(None, ("mem", "lat", "lon")),
        P(),
        P(None, ("mem", "lat", "lon")),
        P(None, ("mem", "lat", "lon")),
    )
    out_specs = P("mem", None, "lat", "lon", None)
    return jax.shard_map(body, mesh=mesh, in_specs=in_specs, out_specs=out_specs, check_vma=False)
```

profile of v0, /device:TPU:1, one launch (start us, length us, event | category | flops | bytes accessed | tf_op | source)
XLA Modules:
  0.0 644.1 jit_solution(7595094467053468557)
XLA Ops:
  6.5 1.0 copy.49
  9.8 1.0 copy.52
  13.0 4.6 collective-permute-start.2
  17.6 2.0 convert_reduce_fusion.1
  19.7 1.0 fusion.22
  20.7 0.9 fusion.24
  21.7 1.4 copy-done.3
  23.3 1.7 slice.76
  25.3 5.2 collective-permute-start.3
  31.7 5.4 collective-permute-start.1
  38.7 4.6 collective-permute-done.1
  43.3 1.8 pad_maximum_fusion
  45.0 276.8 %all-gather.3.cloned.1.call-done = bf16[3145728]{0:T(1024)(128)(2,1)} async-done(((bf16[24576]{0:T(1024)(128)(2,1)}), bf16[3145728]{0:T(1024)(128)(2,1)}) %all-gather.3.cloned.1.call-update) | async-done | bytes 6291472 | tf_op jit(solution)/shard_map/all_gather | solution.py:25
  321.8 8.8 %reshape.169 = bf16[128,24576]{1,0:T(8,128)(2,1)} reshape(bf16[3145728]{0:T(1024)(128)(2,1)} %all-gather.3.cloned.1.call-done) | data formatting | bytes 12582912 | tf_op jit(solution)/shard_map/all_gather | solution.py:25
  330.6 1.2 slice.88
  333.6 1.6 copy.53
  335.2 2.3 reshape.158
  337.5 3.6 copy.54
  341.1 2.5 reshape.159
  343.6 7.6 %convolution_convert_fusion = bf16[2304,1536]{1,0:T(8,128)(2,1)} fusion(bf16[2304,512]{1,0:T(8,128)(2,1)} %bitcast.115, bf16[512,1536]{0,1:T(8,128)(2,1)S(1)} %reshape.159), kind=kOutput, calls=%fused_computation.29 | convolution fusion | flops 3627417600 | bytes 11010048 | tf_op jit(solution)/shard_map/dot_general | solution.py:102
  351.2 11.3 %reshape_reshape.6 = bf16[2,4,6,4,12,1536]{5,4,3,2,1,0:T(8,128)(2,1)} reshape(bf16[2304,1536]{1,0:T(8,128)(2,1)} %convolution_convert_fusion) | data formatting | bytes 14155776 | tf_op jit(solution)/shard_map/reshape;reshape | solution.py:53
  362.5 12.0 %copy.55 = bf16[4,4,2,6,12,1536]{5,1,0,4,3,2:T(4,128)(2,1)} copy(bf16[4,4,2,6,12,1536]{5,4,1,3,0,2:T(8,128)(2,1)} %bitcast.103) | data formatting | bytes 14155776 | tf_op jit(solution)/shard_map/transpose | solution.py:54
  374.5 32.6 %reshape.160 = bf16[16,144,3,16,32]{4,3,2,0,1:T(8,128)(2,1)} reshape(bf16[4,4,2,6,12,1536]{5,1,0,4,3,2:T(4,128)(2,1)} %copy.55) | data formatting | bytes 14155776 | tf_op jit(solution)/shard_map/reshape | solution.py:54
  407.1 24.0 %fusion.52 = (bf16[16,144,1,16,32]{4,3,2,0,1:T(8,128)(2,1)}, bf16[16,144,1,16,32]{4,3,2,0,1:T(8,128)(2,1)}, bf16[16,144,1,16,32]{4,3,2,0,1:T(8,128)(2,1)}) fusion(bf16[16,144,3,16,32]{4,3,2,0,1:T(8,128)(2,1)} %reshape.160), kind=kLoop, calls=%fused_computation.82 | loop fusion | bytes 14155776 | tf_op jit(solution)/shard_map/slice | solution.py:77
  431.1 12.3 %copy.73 = bf16[16,144,1,16,32]{1,4,3,0,2:T(8,128)(2,1)} copy(bf16[16,144,1,16,32]{4,3,2,0,1:T(8,128)(2,1)} %get-tuple-element.5) | data formatting | bytes 4718592
  443.4 12.3 %copy.74 = bf16[16,144,1,16,32]{1,4,3,0,2:T(8,128)(2,1)} copy(bf16[16,144,1,16,32]{4,3,2,0,1:T(8,128)(2,1)} %get-tuple-element.6) | data formatting | bytes 4718592
  455.7 12.3 %copy.75 = bf16[16,144,1,16,32]{1,4,3,0,2:T(8,128)(2,1)} copy(bf16[16,144,1,16,32]{4,3,2,0,1:T(8,128)(2,1)} %get-tuple-element.7) | data formatting | bytes 4718592
  468.0 19.9 %fusion.54 = (f32[16,16,144]{2,1,0:T(8,128)S(1)}, f32[16,16,144,144]{2,3,1,0:T(8,128)}) fusion(pred[16,144,144]{1,2,0:T(8,128)(4,1)S(1)} %compare_and_fusion, bf16[16,144,1,16,32]{1,4,3,0,2:T(8,128)(2,1)} %copy.75, bf16[16,144,1,16,32]{1,4,3,0,2:T(8,128)(2,1)} %copy.74), kind=kOutput, calls=%fused_computation.84 | convolution fusion | flops 360972416 | bytes 26431488 | tf_op jit(solution)/shard_map/sub | solution.py:75
  487.8 16.4 %convert_bitcast_fusion.1 = bf16[16,144,16,32]{1,3,2,0:T(8,128)(2,1)} fusion(f32[16,16,144,144]{2,3,1,0:T(8,128)} %get-tuple-element.11, f32[16,16,144]{2,1,0:T(8,128)S(1)} %get-tuple-element.10, bf16[16,144,1,16,32]{1,4,3,0,2:T(8,128)(2,1)} %copy.73), kind=kOutput, calls=%fused_computation.56 | convolution fusion | flops 351535104 | bytes 26099712 | tf_op jit(solution)/shard_map/whqk,wkhd->wqhd/dot_general | solution.py:76
  504.3 11.5 %copy.61 = bf16[16,144,16,32]{3,2,0,1:T(8,128)(2,1)} copy(bf16[16,144,16,32]{1,3,2,0:T(8,128)(2,1)} %convert_bitcast_fusion.1) | data formatting | bytes 4718592 | tf_op jit(solution)/shard_map/convert_element_type | solution.py:79
  515.8 12.2 %reshape.161 = bf16[4,4,2,6,12,512]{5,1,0,4,3,2:T(4,128)(2,1)S(1)} reshape(bf16[16,144,16,32]{3,2,0,1:T(8,128)(2,1)} %copy.61) | data formatting | bytes 4718592 | tf_op jit(solution)/shard_map/reshape | solution.py:79
  528.0 3.8 copy.62
  531.8 5.1 reshape_reshape.7
  536.9 3.2 convolution_convert_fusion.1
  540.3 1.9 collective-permute-start.4
  542.1 12.5 %collective-permute-done.4 = bf16[2,24,6,512]{3,2,1,0:T(8,128)(2,1)S(1)} collective-permute-done((bf16[2,24,6,512]{3,2,1,0:T(8,128)(2,1)S(1)}, bf16[2,24,6,512]{3,2,1,0:T(8,128)(2,1)S(1)}, u32[]{:S(2)}, u32[]{:S(2)}) %collective-permute-start.4) | collective-permute-done | bytes 294944 | tf_op jit(solution)/shard_map/ppermute | solution.py:36
  554.7 1.6 collective-permute-start.5
  556.3 2.2 fusion.53
  558.5 3.2 copy.67
  561.7 4.0 copy.68
  565.7 4.1 reshape.168
  569.8 2.4 copy.65
  572.3 5.1 copy.66
  577.4 2.8 pad_maximum_fusion.1
  580.9 1.3 fusion.28
  582.3 1.1 multiply_convert_fusion
  583.8 45.8 %fusion.4 = bf16[2304,2048]{1,0:T(8,128)(2,1)S(1)} fusion(bf16[2304,512]{1,0:T(8,128)(2,1)S(1)} %bitcast.116, bf16[512,2048]{0,1:T(8,128)(2,1)S(1)} %bitcast.117), kind=kOutput, calls=%fused_computation.8 | convolution fusion | flops 5138546688 | bytes 13893632 | tf_op jit(solution)/shard_map/dot_general | solution.py:118
  629.6 7.2 %fusion.44 = bf16[1,2,24,48,512]{4,3,2,1,0:T(8,128)(2,1)} fusion(bf16[2,24,48,2048]{3,2,1,0:T(8,128)(2,1)S(1)} %bitcast.119, bf16[2048,512]{0,1:T(8,128)(2,1)S(1)} %copy-done.5, bf16[2,21,48,512]{3,2,1,0:T(8,128)(2,1)S(1)} %pad_maximum_fusion.1, bf16[2,3,48,512]{3,2,1,0:T(8,128)(2,1)S(1)} %collective-permute-done.5, ...), kind=kOutput, calls=%fused_computation.57 | convolution fusion | flops 4841275392 | bytes 18612224 | tf_op jit(solution)/shard_map/dot_general | solution.py:120
  (67 shorter events, 10.7 us)
Async XLA Ops:
  6.5 13.1 %copy-start = (bf16[1,2,24,48,512]{4,3,2,1,0:T(8,128)(2,1)S(1)}, bf16[1,2,24,48,512]{4,3,2,1,0:T(8,128)(2,1)}, u32[]{:S(2)}) copy-start(bf16[1,2,24,48,512]{4,3,2,1,0:T(8,128)(2,1)} %param.8) | copy-start | bytes 7077892
  6.5 14.2 %copy-start.8 = (f32[512]{0:T(512)S(1)}, f32[512]{0:T(512)}, u32[]{:S(2)}) copy-start(f32[512]{0:T(512)} %param.10) | copy-start | bytes 6148
  6.5 315.3 %all-gather.3.cloned.1.call-start = ((), (), s32[]{:S(2)}) async-start(), calls=%async_computation | async-start | bytes 6340608 | tf_op jit(solution)/shard_map/all_gather | solution.py:25
  13.0 12.2 %collective-permute-start.2 = (bf16[3,48]{1,0:T(4,128)(2,1)S(1)}, bf16[3,48]{1,0:T(4,128)(2,1)S(1)}, u32[]{:S(2)}, u32[]{:S(2)}) collective-permute-start(bf16[3,48]{1,0:T(4,128)(2,1)S(1)} %slice.83), channel_id=1, source_target_pairs={{8,0},{16,8},{24,16},{0,24},{9,1},{17,9},{25,17},{1,25},{10,2},{18... | collective-permute-start | bytes 872 | tf_op jit(solution)/shard_map/ppermute | solution.py:36
  21.7 1.4 copy-start.3
  23.1 8.6 %collective-permute-start = (bf16[2,3,48,512]{3,2,1,0:T(8,128)(2,1)S(1)}, bf16[2,3,48,512]{3,2,1,0:T(8,128)(2,1)S(1)}, u32[]{:S(2)}, u32[]{:S(2)}) collective-permute-start(bf16[2,3,48,512]{3,2,1,0:T(8,128)(2,1)S(1)} %slice.77), channel_id=1, source_target_pairs={{8,0},{16,8},{24,16},{0,24},{9,1},{17,9},{25,17},{1,25},{10,2},{18... | collective-permute-start | bytes 884744 | tf_op jit(solution)/shard_map/ppermute | solution.py:36
  25.3 6.0 collective-permute-start.3
  31.7 11.5 %collective-permute-start.1 = (bf16[2,24,6,512]{3,2,1,0:T(8,128)(2,1)S(1)}, bf16[2,24,6,512]{3,2,1,0:T(8,128)(2,1)S(1)}, u32[]{:S(2)}, u32[]{:S(2)}) collective-permute-start(bf16[2,24,6,512]{3,2,1,0:T(8,128)(2,1)S(1)} %pad_maximum_fusion.2), channel_id=1, source_target_pairs={{1,0},{2,1},{3,2},{4,3},{5,4},{6,5},{7,6},{0,7},{9,8},{10,9},{11,1... | collective-permute-start | bytes 884744 | tf_op jit(solution)/shard_map/ppermute | solution.py:36
  330.6 3.0 slice-start.2
  528.0 8.9 %copy-start.7 = (bf16[512,512]{0,1:T(8,128)(2,1)S(1)}, bf16[512,512]{0,1:T(8,128)(2,1)}, u32[]{:S(2)}) copy-start(bf16[512,512]{0,1:T(8,128)(2,1)} %reshape.163) | copy-start | bytes 1572868
  531.8 24.5 %slice-start = ((s8[6291456]{0:T(1024)(128)(4,1)}), s8[2097152]{0:T(1024)(128)(4,1)S(1)}, s32[]{:S(2)}) async-start(s8[6291456]{0:T(1024)(128)(4,1)} %bitcast.105), calls=%async_computation.1 | async-start | bytes 4194304
  536.9 19.4 %slice-start.1 = ((s8[6291456]{0:T(1024)(128)(4,1)}), s8[4194304]{0:T(1024)(128)(4,1)S(1)}, s32[]{:S(2)}) async-start(s8[6291456]{0:T(1024)(128)(4,1)} %bitcast.105), calls=%async_computation.2 | async-start | bytes 8388608
  540.1 14.5 %copy-start.2 = (bf16[2304,512]{1,0:T(8,128)(2,1)}, bf16[2304,512]{1,0:T(8,128)(2,1)S(1)}, u32[]{:S(2)}) copy-start(bf16[2304,512]{1,0:T(8,128)(2,1)S(1)} %convolution_convert_fusion.1) | copy-start | bytes 7077892
  540.3 14.3 %collective-permute-start.4 = (bf16[2,24,6,512]{3,2,1,0:T(8,128)(2,1)S(1)}, bf16[2,24,6,512]{3,2,1,0:T(8,128)(2,1)S(1)}, u32[]{:S(2)}, u32[]{:S(2)}) collective-permute-start(bf16[2,24,6,512]{3,2,1,0:T(8,128)(2,1)S(1)} %slice.89), channel_id=1, source_target_pairs={{7,0},{0,1},{1,2},{2,3},{3,4},{4,5},{5,6},{6,7},{15,8},{8,9},{9,10... | collective-permute-start | bytes 884744 | tf_op jit(solution)/shard_map/ppermute | solution.py:36
  554.7 25.4 %collective-permute-start.5 = (bf16[2,3,48,512]{3,2,1,0:T(8,128)(2,1)S(1)}, bf16[2,3,48,512]{3,2,1,0:T(8,128)(2,1)S(1)}, u32[]{:S(2)}, u32[]{:S(2)}) collective-permute-start(bf16[2,3,48,512]{3,2,1,0:T(8,128)(2,1)S(1)} %pad_maximum_fusion.3), channel_id=1, source_target_pairs={{24,0},{0,8},{8,16},{16,24},{25,1},{1,9},{9,17},{17,25},{26,2},{2,... | collective-permute-start | bytes 884744 | tf_op jit(solution)/shard_map/ppermute | solution.py:36
  565.7 4.1 copy-start.4
  572.3 7.9 %copy-start.1 = (bf16[1,2,24,48,512]{4,3,2,1,0:T(8,128)(2,1)S(1)}, bf16[1,2,24,48,512]{4,3,2,1,0:T(8,128)(2,1)}, u32[]{:S(2)}) copy-start(bf16[1,2,24,48,512]{4,3,2,1,0:T(8,128)(2,1)} %param.8) | copy-start | bytes 7077892
  580.1 2.1 copy-start.9
  582.2 1.6 copy-start.6
  583.8 45.8 %copy-start.5 = (bf16[2048,512]{0,1:T(8,128)(2,1)S(1)}, bf16[2048,512]{0,1:T(8,128)(2,1)}, u32[]{:S(2)}) copy-start(bf16[2048,512]{0,1:T(8,128)(2,1)} %reshape.168) | copy-start | bytes 6291460
Sparse Core Ops, SparseCore 0:
  12.4 309.3 all-gather.2
where the time goes:
time: 652 us; the launch traced here: 644 us
  waiting for transfers between devices  295 us (45%)
  local copies, waits for them, and re-layouts  201 us (31%)
  matrix products  100 us (15%)
  starting transfers between devices  18.8 us (3%)
  other arithmetic  14.9 us (2%)
  between operations  14.2 us (2%)
    all_gather x1, waiting for transfers between devices, one_gather(): lines, at, gathered = (lax.all_gather(flat, axis), 0, [])  277 us
    dot_general x1, matrix products, body(): pre_act = jnp.dot(normed2, gathered[2], preferred_element_type=jnp.float32)  45.8 us
    unnamed x31, local copies, waits for them, and re-layouts  42.4 us
    reshape x1, local copies, waits for them, and re-layouts, attend(): windowed.transpose(1, 3, 0, 2, 4, 5)  32.6 us
    slice x1, local copies, waits for them, and re-layouts, attend(): windowed[:, :, 2]  24 us
    sub x1, matrix products, attend(): attn_probs = jax.nn.softmax(scores, axis=-1).astype(jnp.bfloat16)  19.9 us
    ppermute x6, starting transfers between devices, shifted_2(): return lax.ppermute(block, axis, route)  18.8 us
    ppermute x6, waiting for transfers between devices, shifted_2(): return lax.ppermute(block, axis, route)  18 us
  transfers between devices with their start and end apart: 7, of which 5 were waited for; matrix products, arithmetic and copies ran while one was open for 5% of the time, Pallas kernels for 0%

commit v1 on v0

v1 whole, which is shorter than its diff:
```python
import functools
import math

import jax
import jax.numpy as jnp
import numpy as np
from jax import lax
from jax.experimental import pallas as pl
from jax.experimental.pallas import tpu as pltpu
from jax.sharding import PartitionSpec as P

D = 512
HDIM = 32
FF = 2048
SH = 3
SL = 6
TOK = 144
EDGE = 7
INNER = 9
AXES = ("mem", "lat", "lon")
MASKED = -1e30
EXP2_SCALE = math.log2(math.e) / math.sqrt(HDIM)
BF16 = jnp.bfloat16
F32 = jnp.float32
NT = (((1,), (1,)), ((), ()))

eps = 1e-05


def place(j):
    return j & 3, ((j >> 2) & 1) * 2 + ((j >> 6) & 1), (j >> 3) & 3, (j >> 5) & 1


def flat(x, y, z, core):
    return ((y & 1) << 6) | (core << 5) | (z << 3) | ((y >> 1) << 2) | x


def send(block, source_of):
    pairs = [(flat(*source_of(*place(j))), j) for j in range(128)]
    return lax.ppermute(block, AXES, pairs)


def along_x(block, d):
    return send(block, lambda x, y, z, c: ((x + d) % 4, y, z, c))


def along_first(block, d):
    return send(block, lambda x, y, z, c: (x, (y + d * (1 - c)) % 4, (z + d * c) % 4, c))


def along_second(block, d):
    return send(block, lambda x, y, z, c: (x, (y + d * c) % 4, (z + d * (1 - c)) % 4, c))


def other_core(block):
    return send(block, lambda x, y, z, c: (x, y, z, 1 - c))


def from_grid(block, dlat, dlon):
    pairs = []
    for j in range(128):
        mem, lat, lon = j >> 5, (j >> 3) & 3, j & 7
        pairs.append((mem * 32 + ((lat + dlat) % 4) * 8 + (lon + dlon) % 8, j))
    return lax.ppermute(block, AXES, pairs)


def norm(values, gain):
    average = jnp.mean(values, axis=-1, keepdims=True)
    centred = values - average
    variance = jnp.mean(centred * centred, axis=-1, keepdims=True)
    return (centred * lax.rsqrt(variance + eps) * gain).astype(BF16)


def prep_kernel(ext_ref, ids_ref, gain_ref, f_ref, x_ref, xq_ref, bias_ref):
    i = pl.program_id(0)
    k = i - EDGE
    wi = jnp.where(i < 4, 3, jnp.where(i < EDGE, i - 4, k // 3))
    wj = jnp.where(i < 4, i, jnp.where(i < EDGE, 3, k % 3))
    base = jnp.where(wj < 2, 0, jnp.where(wj == 2, 16, 32))
    off = 12 * wj + SL - base
    col = lax.broadcasted_iota(jnp.int32, (1, 384), 1)
    seg = col // 32
    cc = col - seg * 32 - off
    lev = (seg >= 6).astype(jnp.int32)
    r = seg - 6 * lev
    rh = (r >= 3).astype(jnp.int32)
    ch = (cc >= 6).astype(jnp.int32)
    quad = jnp.where(wj == 3, ch * 2 + rh, rh * 2 + ch)
    row = quad * 36 + lev * 18 + (r - 3 * rh) * 6 + cc - 6 * ch
    row = jnp.where((cc >= 0) & (cc < 12), row, -1)
    pick = (lax.broadcasted_iota(jnp.int32, (TOK, 384), 0) == row).astype(F32).astype(BF16)
    start = pl.multiple_of(base, 16)
    tokens = jnp.concatenate(
        [ext_ref[s // 6, 6 * wi + SH + s % 6, pl.ds(start, 32), :] for s in range(12)], axis=0
    )
    marks = jnp.concatenate([ids_ref[6 * wi + SH + s % 6, pl.ds(start, 32), :] for s in range(12)], axis=0)
    f = jnp.dot(pick, tokens, preferred_element_type=F32)
    idk = jnp.dot(pick, marks, preferred_element_type=F32)
    f_ref[0] = f.astype(BF16)
    x = norm(f, gain_ref[...])
    x_ref[0] = x
    xq_ref[0, 0:128] = x[0:128]
    for t in range(8):
        xq_ref[0, 128 + 16 * t : 144 + 16 * t] = x[128:144]
    idq = jnp.concatenate([idk[0:128]] + [idk[128:144]] * 8, axis=0).T[0:1]
    both = jnp.concatenate([idk, idk], axis=1)
    bias_ref[0] = jnp.where(both == idq, 0.0, MASKED).astype(BF16)


def prep(ext, ids, gain):
    n = EDGE + INNER
    whole = lambda a: pl.BlockSpec(a.shape, lambda i: (0,) * a.ndim)
    out = lambda *s: (jax.ShapeDtypeStruct((n, *s), BF16), pl.BlockSpec((1, *s), lambda i: (i, 0, 0)))
    shapes, specs = zip(out(TOK, D), out(TOK, D), out(256, D), out(TOK, 256))
    return pl.pallas_call(
        prep_kernel,
        grid=(n,),
        in_specs=[whole(ext), whole(ids), whole(gain)],
        out_specs=specs,
        out_shape=shapes,
        name="prep",
        cost_estimate=pl.CostEstimate(flops=3_000_000_000, bytes_accessed=16_000_000, transcendentals=0),
    )(ext, ids, gain)


def block_rows(pos_ref, side, d2, d3):
    core = pos_ref[2]
    core = core if side == 0 else 1 - core
    dy = jnp.where(core == 0, d2, d3)
    dz = jnp.where(core == 0, d3, d2)
    y = (pos_ref[0] + dy) % 4
    z = (pos_ref[1] + dz) % 4
    return (y % 2) * 16 + core * 8 + z * 2 + y // 2


def attn_kernel(count, pos_ref, x_ref, xq_ref, bias_ref, *refs):
    pieces, out_ref, (w, kall, qt, vt, mt) = refs[:8], refs[8], refs[9:]
    i = pl.program_id(0)

    @pl.when(i == 0)
    def _():
        for p in range(8):
            for d2 in range(4):
                b = block_rows(pos_ref, p // 4, d2, p % 4)
                w[pl.ds(pl.multiple_of(b * 48, 16), 48), :] = pieces[p][d2]
        keys = lax.dot_general(
            x_ref[...].reshape(count * TOK, D), w[D : 2 * D, :], NT, preferred_element_type=F32
        )
        kall[...] = keys.astype(BF16)

    xq = xq_ref[0]
    qt[...] = lax.dot_general(w[0:D, :], xq, NT, preferred_element_type=F32).astype(BF16)
    vt[...] = lax.dot_general(w[2 * D : 3 * D, :], xq, NT, preferred_element_type=F32).astype(BF16)
    krow = pl.multiple_of(i * TOK, 16)
    ones = jnp.ones((16, TOK), BF16)
    bias = bias_ref[0].astype(F32)

    def soften(s):
        m = jnp.max(s, axis=0, keepdims=True)
        return jnp.exp2((s - m) * EXP2_SCALE).astype(BF16)

    for g in range(4):
        zeros = jnp.zeros((32, 128), BF16)
        heads = []
        for h in range(4):
            q = qt[128 * g + 32 * h : 128 * g + 32 * h + 32, 0:128]
            heads.append(jnp.concatenate([zeros] * h + [q] + [zeros] * (3 - h), axis=0))
        kg = kall[pl.ds(krow, TOK), 128 * g : 128 * g + 128]
        for pair in range(2):
            s = jnp.dot(
                kg, jnp.concatenate(heads[2 * pair : 2 * pair + 2], axis=1), preferred_element_type=F32
            )
            s = s + jnp.concatenate([bias[:, 0:128]] * 2, axis=1)
            p = soften(s)
            at = 128 * g + 64 * pair
            lhs = jnp.concatenate([vt[at : at + 64, 0:TOK], ones], axis=0)
            o = jnp.dot(lhs, p, preferred_element_type=F32)
            inv = 1.0 / o[64:65]
            mt[at : at + 32, 0:128] = o[0:32, 0:128] * inv[:, 0:128]
            mt[at + 32 : at + 64, 0:128] = o[32:64, 128:256] * inv[:, 128:256]
    own = (
        lax.broadcasted_iota(jnp.int32, (256, 128), 0) // 32
        == lax.broadcasted_iota(jnp.int32, (256, 128), 1) // 16
    )
    fold = (
        lax.broadcasted_iota(jnp.int32, (128, 128), 0) % 16 == lax.broadcasted_iota(jnp.int32, (128, 128), 1)
    ).astype(F32).astype(BF16)
    for a in range(2):
        q = jnp.where(own, qt[256 * a : 256 * a + 256, 128:256].astype(F32), 0.0).astype(BF16)
        s = jnp.dot(kall[pl.ds(krow, TOK), 256 * a : 256 * a + 256], q, preferred_element_type=F32)
        p = soften(s + bias[:, 128:256])
        lhs = jnp.concatenate([vt[256 * a : 256 * a + 256, 0:TOK], ones], axis=0)
        o = jnp.dot(lhs, p, preferred_element_type=F32)
        o = jnp.where(own, o[0:256] * (1.0 / o[256:257]), 0.0).astype(BF16)
        mt[256 * a : 256 * a + 256, 128:256] = jnp.dot(o, fold, preferred_element_type=F32)
    out_ref[0] = mt[...].T[0:TOK].astype(BF16)


def attend(pos, x, xq, bias, pieces, first, count):
    whole = lambda a: pl.BlockSpec(a.shape, lambda i: (0,) * a.ndim, pipeline_mode=pl.Buffered(1))
    one = lambda *s: pl.BlockSpec((1, *s), lambda i: (i + first, 0, 0))
    return pl.pallas_call(
        functools.partial(attn_kernel, count),
        grid=(count,),
        in_specs=[
            pl.BlockSpec(memory_space=pltpu.SMEM),
            whole(x),
            one(256, D),
            one(TOK, 256),
            *[whole(p) for p in pieces],
        ],
        out_specs=pl.BlockSpec((1, TOK, D), lambda i: (i, 0, 0)),
        out_shape=jax.ShapeDtypeStruct((count, TOK, D), BF16),
        scratch_shapes=[
            pltpu.VMEM((3 * D, D), BF16),
            pltpu.VMEM((count * TOK, D), BF16),
            pltpu.VMEM((D, 256), BF16),
            pltpu.VMEM((D, 256), BF16),
            pltpu.VMEM((D, 256), F32),
        ],
        name=f"attend_{first}",
        cost_estimate=pl.CostEstimate(
            flops=count * 1_000_000_000, bytes_accessed=count * 600_000, transcendentals=count * 400_000
        ),
    )(pos, x, xq, bias, *pieces)


def mlp_kernel(pos_ref, mixed_ref, f_ref, gain_ref, *refs):
    pieces, out_ref, (wp, wu, wd) = refs[:8], refs[8], refs[9:]

    @pl.when(pl.program_id(0) == 0)
    def _():
        for p in range(8):
            for d2 in range(4):
                b = block_rows(pos_ref, p // 4, d2, p % 4)
                wp[pl.ds(pl.multiple_of(b * 16, 16), 16), :] = pieces[p][d2, 0:16]
                wu[pl.ds(pl.multiple_of(b * 64, 16), 64), :] = pieces[p][d2, 16:80]
                for c in range(4):
                    wd[c, pl.ds(pl.multiple_of(b * 16, 16), 16), :] = pieces[p][d2, 80 + 16 * c : 96 + 16 * c]

    attn = lax.dot_general(mixed_ref[...], wp[...], NT, preferred_element_type=F32).astype(BF16)
    resid = (f_ref[...].astype(F32) + attn.astype(F32)).astype(BF16)
    normed = norm(resid.astype(F32), gain_ref[...])
    total = resid.astype(F32)
    for c in range(4):
        pre = lax.dot_general(normed, wu[512 * c : 512 * c + 512, :], NT, preferred_element_type=F32)
        hidden = (0.5 * pre * (1.0 + lax.erf(pre * math.sqrt(0.5)))).astype(BF16)
        total = total + lax.dot_general(hidden, wd[c], NT, preferred_element_type=F32)
    out_ref[...] = total.astype(BF16)


def mlp(pos, mixed, f, gain, pieces, first, rows, tile):
    whole = lambda a: pl.BlockSpec(a.shape, lambda i: (0,) * a.ndim, pipeline_mode=pl.Buffered(1))
    return pl.pallas_call(
        mlp_kernel,
        grid=(rows // tile,),
        in_specs=[
            pl.BlockSpec(memory_space=pltpu.SMEM),
            pl.BlockSpec((tile, D), lambda i: (i, 0)),
            pl.BlockSpec((pl.Element(tile), pl.Element(D)), lambda i: (pl.multiple_of(first + i * tile, 16), 0)),
            whole(gain),
            *[whole(p) for p in pieces],
        ],
        out_specs=pl.BlockSpec((tile, D), lambda i: (i, 0)),
        out_shape=jax.ShapeDtypeStruct((rows, D), BF16),
        scratch_shapes=[
            pltpu.VMEM((D, D), BF16),
            pltpu.VMEM((FF, D), BF16),
            pltpu.VMEM((4, D, D), BF16),
        ],
        name=f"mlp_{first}",
        cost_estimate=pl.CostEstimate(
            flops=rows * 5_000_000, bytes_accessed=rows * 3072 + 5_000_000, transcendentals=rows * 2048
        ),
    )(pos, mixed, f, gain, *pieces)


def place_matrices():
    top = np.zeros((288, 368), np.float32)
    mid = np.zeros((576, 656), np.float32)
    for lev in range(2):
        for rr in range(3):
            for c in range(48):
                o = lev * 144 + rr * 48 + c
                at = lev * 18 + rr * 6
                wj, cc = (c - 6) // 12, (c - 6) % 12
                ch, c1 = cc // 6, cc % 6
                if c < 6:
                    top[o, 320 + 12 + at + c] = 1
                    for rh in range(2):
                        mid[rh * 288 + o, 576 + 8 + 36 * rh + at + c] = 1
                elif wj < 3:
                    top[o, 80 * wj + 8 + 36 * ch + at + c1] = 1
                    for rh in range(2):
                        mid[rh * 288 + o, 144 * wj + 72 * rh + 36 * ch + at + c1] = 1
                else:
                    top[o, 240 + 4 + at + c1] = 1
                    for rh in range(2):
                        mid[rh * 288 + o, 432 + 36 * rh + at + c1] = 1
    return top, mid


def place_kernel(edge_ref, inner_ref, lat_ref, lon_ref, diag_ref, top_ref, mid_ref, out_ref):
    def put(k, rows):
        for lev in range(2):
            for rr in range(3):
                at = lev * 144 + rr * 48
                out_ref[0, lev, 3 * k + rr] = rows[at : at + 48].astype(BF16)

    first = jnp.concatenate([lat_ref[...], diag_ref[...]], axis=0)
    put(0, jnp.dot(top_ref[...], first, preferred_element_type=F32))
    for wi in range(4):
        if wi < 3:
            three = inner_ref[432 * wi : 432 * wi + 432]
            last = edge_ref[576 + 144 * wi : 720 + 144 * wi]
        else:
            three = edge_ref[0:432]
            last = edge_ref[432:576]
        stack = jnp.concatenate([three, last, lon_ref[80 * wi : 80 * wi + 80]], axis=0)
        both = 576 if wi < 3 else 288
        rows = jnp.dot(mid_ref[0:both], stack, preferred_element_type=F32)
        put(1 + 2 * wi, rows[0:288])
        if wi < 3:
            put(2 + 2 * wi, rows[288:576])


def to_grid(edge, inner, lat, lon, diag):
    top, mid = place_matrices()
    return pl.pallas_call(
        place_kernel,
        out_shape=jax.ShapeDtypeStruct((1, 2, 24, 48, D), BF16),
        name="to_grid",
        cost_estimate=pl.CostEstimate(flops=3_000_000_000, bytes_accessed=8_000_000, transcendentals=0),
    )(edge, inner, lat, lon, diag, jnp.asarray(top, BF16), jnp.asarray(mid, BF16))


def widen(own, stage):
    return jnp.stack([own, *[stage(own, d) for d in (1, 2, 3)]])


def pieces_of(block):
    group = widen(block, along_first)
    mine = [group, *[along_second(group, d) for d in (1, 2, 3)]]
    return mine + [other_core(m) for m in mine]


def body(fields, region, gain_attn, w_qkv, w_proj, gain_mlp, w_up, w_down):
    lat, lon = lax.axis_index("lat"), lax.axis_index("lon")
    mem = lax.axis_index("mem")
    pos = jnp.stack([(lon // 4) * 2 + mem // 2, lat, mem % 2]).astype(jnp.int32)

    down = w_down.T.reshape(4, 4, D).transpose(1, 0, 2).reshape(16, D)
    block = jnp.concatenate([w_qkv.T, w_proj.T, w_up.T, down], axis=0)
    line = widen(block, along_x)
    line = lax.dynamic_slice_in_dim(jnp.concatenate([line, line]), (4 - lon % 4) % 4, 4)
    qkv_pieces = pieces_of(line[:, 0:12].reshape(48, D))
    rest = jnp.concatenate(
        [
            line[:, 12:16].reshape(16, D),
            line[:, 16:32].reshape(64, D),
            line[:, 32:48].reshape(4, 4, 4, D).transpose(1, 0, 2, 3).reshape(64, D),
        ]
    )
    rest_pieces = pieces_of(rest)

    member = fields[0]
    levels, clat, clon, _ = member.shape
    row = lax.broadcasted_iota(jnp.int32, (clat, clon), 0)
    ids = (region * 2 + ((lat == 0) & (row < SH)).astype(jnp.int32)).astype(BF16)
    below = from_grid(member[:, :SH], 1, 0)
    right = from_grid(member[:, :, :SL], 0, 1)
    corner = from_grid(member[:, :SH, :SL], 1, 1)
    ids_below = from_grid(ids[:SH], 1, 0)
    ids_right = from_grid(ids[:, :SL], 0, 1)
    ids_corner = from_grid(ids[:SH, :SL], 1, 1)
    gap = jnp.zeros((levels, clat + SH, 64 - clon - SL, D), BF16)
    ext = jnp.concatenate(
        [
            jnp.concatenate([member, below], axis=1),
            jnp.concatenate([right, corner], axis=1),
            gap,
        ],
        axis=2,
    )
    ids = jnp.concatenate(
        [jnp.concatenate([ids, ids_below], axis=0), jnp.concatenate([ids_right, ids_corner], axis=0)], axis=1
    )
    ids = jnp.pad(ids, ((0, 0), (0, 64 - clon - SL)))
    ids = jnp.broadcast_to(ids[:, :, None], (clat + SH, 64, 128))
    f, x, xq, bias = prep(ext, ids, gain_attn.reshape(1, D))

    mixed_edge = attend(pos, x[:EDGE], xq, bias, qkv_pieces, 0, EDGE)
    mixed_inner = attend(pos, x[EDGE:], xq, bias, qkv_pieces, EDGE, INNER)
    f = f.reshape(-1, D)
    gain = gain_mlp.reshape(1, D)
    edge = mlp(pos, mixed_edge.reshape(-1, D), f, gain, rest_pieces, 0, EDGE * TOK, 336)
    win = edge.reshape(EDGE, TOK, D)
    lat_out = jnp.concatenate([win[0:3, 64:144].reshape(240, D), win[3, 32:112]])
    lon_out = jnp.concatenate([win[4:7, 64:144].reshape(240, D), win[3, 64:144]])
    diag_out = win[3, 96:144]
    lat_in = from_grid(lat_out, -1, 0)
    lon_in = from_grid(lon_out, 0, -1)
    diag_in = from_grid(diag_out, -1, -1)
    inner = mlp(pos, mixed_inner.reshape(-1, D), f, gain, rest_pieces, EDGE * TOK, INNER * TOK, 432)
    return to_grid(edge, inner, lat_in, lon_in, diag_in)


def solution(mesh):
    weight = P(None, AXES)
    in_specs = (
        P("mem", None, "lat", "lon", None),
        P("lat", "lon"),
        P(),
        weight,
        weight,
        P(),
        weight,
        weight,
    )
    out_specs = P("mem", None, "lat", "lon", None)
    return jax.shard_map(body, mesh=mesh, in_specs=in_specs, out_specs=out_specs, check_vma=False)
```

time: 652 us -> 175 us (0.27)
  waiting for transfers between devices: 295 us -> 4.63 us
  local copies, waits for them, and re-layouts: 201 us -> 16.8 us
  matrix products: 100 us -> 0 us
  Pallas kernels: 0 us -> 98.4 us
  starting transfers between devices: 18.8 us -> 42.7 us
  between operations: 14.2 us -> 0.42 us
    all_gather x1 -> x0, waiting for transfers between devices: 277 us -> none  [one_gather(): lines, at, gathered = (lax.all_gather(flat, axis), 0, [])]
    pallas_call x0 -> x6, Pallas kernels: none -> 98.4 us  [the longest x2 56.8 us: attend(): pl.pallas_call(functools.partial(attn_kernel, count), grid=(count,), in_s...]
    dot_general x5 -> x0, matrix products: 80.3 us -> none  [the longest x1 45.8 us: body(): pre_act = jnp.dot(normed2, gathered[2], preferred_element_type=jnp.float32)]
    reshape x10 -> x7, local copies, waits for them, and re-layouts: 56 us -> 1.61 us  [the longest x2 0.9 us: body(): down = w_down.T.reshape(4, 4, D).transpose(1, 0, 2).reshape(16, D)]
    unnamed x31 -> x36, local copies, waits for them, and re-layouts: 42.4 us -> 3.19 us
    transpose x8 -> x1, local copies, waits for them, and re-layouts: 29.1 us -> 0.01 us  [body(): down = w_down.T.reshape(4, 4, D).transpose(1, 0, 2).reshape(16, D)]
    slice x14 -> x11, local copies, waits for them, and re-layouts: 36.8 us -> 8.47 us  [the longest x1 2.49 us: body(): mixed_inner = attend(pos, x[EDGE:], xq, bias, qkv_pieces, EDGE, INNER)]
    ppermute x6 -> x32, starting transfers between devices: 18.8 us -> 42.7 us  [the longest x23 28.8 us: send(): return lax.ppermute(block, AXES, pairs)]
  transfers between devices with their start and end apart: 7 -> 32, of which waited for: 5 -> 1; matrix products, arithmetic and copies ran while one was open for 5% -> 11% of each run, Pallas kernels for 0% -> 47%
where the time goes in v1:
time: 175 us; the launch traced here: 172 us
  Pallas kernels  98.4 us (56%)
  starting transfers between devices  42.7 us (24%)
  local copies, waits for them, and re-layouts  16.8 us (10%)
  other arithmetic  8.92 us (5%)
  waiting for transfers between devices  4.63 us (3%)
    pallas_call x2, Pallas kernels, attend(): pl.pallas_call(functools.partial(attn_kernel, count), grid=(count,), in_s...  56.8 us
    ppermute x23, starting transfers between devices, send(): return lax.ppermute(block, AXES, pairs)  28.8 us
    pallas_call x2, Pallas kernels, mlp(): pl.pallas_call(mlp_kernel, grid=(rows // tile,), in_specs=[pl.BlockSpec(m...  23.9 us
    ppermute x9, starting transfers between devices, from_grid(): return lax.ppermute(block, AXES, pairs)  13.9 us
    pallas_call x1, Pallas kernels, prep(): pl.pallas_call(prep_kernel, grid=(n,), in_specs=[whole(ext), whole(ids),...  12.2 us
    pallas_call x1, Pallas kernels, to_grid(): pl.pallas_call(place_kernel, out_shape=jax.ShapeDtypeStruct((1, 2, 24, 48...  5.48 us
    ppermute x9, waiting for transfers between devices, from_grid(): return lax.ppermute(block, AXES, pairs)  4.57 us
  transfers between devices with their start and end apart: 32, of which 1 were waited for; matrix products, arithmetic and copies ran while one was open for 11% of the time, Pallas kernels for 47%

profile of v1, /device:TPU:1, one launch (start us, length us, event | category | flops | bytes accessed | tf_op | source)
XLA Modules:
  0.0 171.9 jit_solution(7266752674304698337)
XLA Ops:
  0.0 0.9 reshape.47
  0.9 0.8 bitcast_dynamic-update-slice_fusion.6
  1.7 3.4 %collective-permute-start.6 = (bf16[48,512]{1,0:T(8,128)(2,1)S(1)}, bf16[48,512]{1,0:T(8,128)(2,1)S(1)}, u32[]{:S(2)}, u32[]{:S(2)}) collective-permute-start(bf16[48,512]{1,0:T(8,128)(2,1)S(1)} %get-tuple-element.14), channel_id=1, source_target_pairs={{1,0},{2,1},{3,2},{0,3},{5,4},{6,5},{7,6},{4,7},{9,8},{10,9},{11,1... | collective-permute-start | bytes 147464 | tf_op jit(solution)/shard_map/ppermute | solution.py:40
  6.2 0.8 slice.70
  7.0 8.2 %collective-permute-start.2 = (bf16[2,3,6,512]{3,2,1,0:T(8,128)(2,1)S(1)}, bf16[2,3,6,512]{3,2,1,0:T(8,128)(2,1)S(1)}, u32[]{:S(2)}, u32[]{:S(2)}) collective-permute-start(bf16[2,3,6,512]{3,2,1,0:T(8,128)(2,1)S(1)} %slice.70), channel_id=1, source_target_pairs={{9,0},{10,1},{11,2},{12,3},{13,4},{14,5},{15,6},{8,7},{17,8},{18,9... | collective-permute-start | bytes 110600 | tf_op jit(solution)/shard_map/ppermute | solution.py:64
  15.2 0.8 copy.15
  16.2 1.3 collective-permute-start.4
  17.6 0.6 reshape.49
  18.2 1.4 collective-permute-start.11
  19.8 0.7 fusion
  20.5 1.7 collective-permute-start.10
  22.2 2.1 %collective-permute-start.9 = (bf16[48,512]{1,0:T(8,128)(2,1)}, bf16[48,512]{1,0:T(8,128)(2,1)S(1)}, u32[]{:S(2)}, u32[]{:S(2)}) collective-permute-start(bf16[48,512]{1,0:T(8,128)(2,1)} %reshape.49), channel_id=1, source_target_pairs={{64,0},{65,1},{66,2},{67,3},{68,4},{69,5},{70,6},{71,7},{72,8},{73... | collective-permute-start | bytes 147464 | tf_op jit(solution)/shard_map/ppermute | solution.py:40
  24.3 1.3 collective-permute-start.20
  25.5 1.5 collective-permute-start.19
  27.0 0.7 pad_add_fusion.pos_ref
  27.7 1.0 slice.69
  28.7 0.7 slice.68
  29.4 0.6 pad.32.clone
  30.1 2.0 %collective-permute-start.1 = (bf16[2,24,6,512]{3,2,1,0:T(8,128)(2,1)S(1)}, bf16[2,24,6,512]{3,2,1,0:T(8,128)(2,1)}, u32[]{:S(2)}, u32[]{:S(2)}) collective-permute-start(bf16[2,24,6,512]{3,2,1,0:T(8,128)(2,1)S(1)} %slice.69), channel_id=1, source_target_pairs={{1,0},{2,1},{3,2},{4,3},{5,4},{6,5},{7,6},{0,7},{9,8},{10,9},{11,1... | collective-permute-start | bytes 884744 | tf_op jit(solution)/shard_map/ppermute | solution.py:64
  32.1 0.6 collective-permute-start
  32.7 1.5 pad_maximum_fusion.3.refs_0_
  34.2 0.8 collective-permute-start.12
  35.0 1.4 collective-permute-start.13
  36.4 0.8 maximum_maximum_fusion.1
  37.4 1.1 pad_maximum_fusion.refs_0_
  38.5 6.4 %collective-permute-start.15 = (bf16[4,48,512]{2,1,0:T(8,128)(2,1)}, bf16[4,48,512]{2,1,0:T(8,128)(2,1)S(1)}, u32[]{:S(2)}, u32[]{:S(2)}) collective-permute-start(bf16[4,48,512]{2,1,0:T(8,128)(2,1)} %pad_maximum_fusion.3.refs_0_), channel_id=1, source_target_pairs={{32,0},{33,1},{34,2},{35,3},{36,4},{37,5},{38,6},{39,7},{40,8},{41... | collective-permute-start | bytes 589832 | tf_op jit(solution)/shard_map/ppermute | solution.py:40
  44.9 0.9 collective-permute-start.22
  45.9 1.6 collective-permute-start.16
  47.6 1.7 %collective-permute-start.18 = (bf16[4,48,512]{2,1,0:T(8,128)(2,1)}, bf16[4,48,512]{2,1,0:T(8,128)(2,1)}, u32[]{:S(2)}, u32[]{:S(2)}) collective-permute-start(bf16[4,48,512]{2,1,0:T(8,128)(2,1)} %collective-permute-done.14.refs_3_), channel_id=1, source_target_pairs={{32,0},{33,1},{34,2},{35,3},{36,4},{37,5},{38,6},{39,7},{40,8},{41... | collective-permute-start | bytes 589832 | tf_op jit(solution)/shard_map/ppermute | solution.py:40
  49.3 3.3 %maximum_maximum_fusion.ext_ref = bf16[2,27,64,512]{3,2,1,0:T(8,128)(2,1)} fusion(bf16[2,3,6,512]{3,2,1,0:T(8,128)(2,1)S(1)} %collective-permute-done.2, bf16[2,24,6,512]{3,2,1,0:T(8,128)(2,1)} %collective-permute-done.1, bf16[2,3,48,512]{3,2,1,0:T(8,128)(2,1)} %collective-permute-done, bf16[2,24,48,512]{3,2,1,0:T(8,128)(2,1)S(1)} %bitcast.51, ...), kind=kLoop, calls=%fused_computation | loop fusion | flops 17694720 | bytes 6525056 | tf_op jit(solution)/shard_map/concatenate | solution.py:377
  52.7 1.1 broadcast_in_dim.10.ids_ref
  53.8 12.2 %prep.1 = (bf16[16,144,512]{2,1,0:T(8,128)(2,1)}, bf16[16,144,512]{2,1,0:T(8,128)(2,1)}, bf16[16,256,512]{2,1,0:T(8,128)(2,1)}, bf16[16,144,256]{2,1,0:T(8,128)(2,1)}) custom-call(bf16[2,27,64,512]{3,2,1,0:T(8,128)(2,1)} %maximum_maximum_fusion.ext_ref, bf16[27,64,128]{2,1,0:T(8,128)(2,1)} %broadcast_in_dim.10.ids_ref, f32[1,512]{1,0:T(1,128)} %bitcast.70), custom_call_target="tpu_custom_call" | custom-call | flops 3000000000 | bytes 16000000 | tf_op jit(solution)/shard_map/prep/pallas_call | solution.py:115
  65.9 2.3 %slice.57.x_ref = bf16[7,144,512]{2,1,0:T(8,128)(2,1)} slice(bf16[16,144,512]{2,1,0:T(8,128)(2,1)} %get-tuple-element.9), slice={[0:7], [0:144], [0:512]} | slice | bytes 2064384 | tf_op jit(solution)/shard_map/slice | solution.py:392
  68.2 2.5 %slice.62.x_ref = bf16[9,144,512]{2,1,0:T(8,128)(2,1)} slice(bf16[16,144,512]{2,1,0:T(8,128)(2,1)} %get-tuple-element.9), slice={[7:16], [0:144], [0:512]} | slice | bytes 2654208 | tf_op jit(solution)/shard_map/slice | solution.py:393
  70.7 1.4 collective-permute-start.23
  72.2 1.2 collective-permute-start.25
  73.4 31.6 %attend_7.1 = bf16[9,144,512]{2,1,0:T(8,128)(2,1)} custom-call(s32[3]{0:T(128)} %pad_add_fusion.pos_ref, bf16[9,144,512]{2,1,0:T(8,128)(2,1)} %slice.62.x_ref, bf16[16,256,512]{2,1,0:T(8,128)(2,1)} %get-tuple-element.10.xq_ref, bf16[16,144,256]{2,1,0:T(8,128)(2,1)} %get-tuple-element.11.bias_ref, bf16[4,48,512]{2,1,0:T(8,128)(2,1)} %pad_maximum_fusion.3.refs_0_, ...), custom_call_target="tpu_custom_call" | custom-call | flops 8999999488 | bytes 5400000 | tf_op jit(solution)/shard_map/attend_7/pallas_call | solution.py:202
  105.7 25.3 %attend_0.1 = bf16[7,144,512]{2,1,0:T(8,128)(2,1)} custom-call(s32[3]{0:T(128)} %pad_add_fusion.pos_ref, bf16[7,144,512]{2,1,0:T(8,128)(2,1)} %slice.57.x_ref, bf16[16,256,512]{2,1,0:T(8,128)(2,1)} %get-tuple-element.10.xq_ref, bf16[16,144,256]{2,1,0:T(8,128)(2,1)} %get-tuple-element.11.bias_ref, bf16[4,48,512]{2,1,0:T(8,128)(2,1)} %pad_maximum_fusion.3.refs_0_, ...), custom_call_target="tpu_custom_call" | custom-call | flops 7000000000 | bytes 4200000 | tf_op jit(solution)/shard_map/attend_0/pallas_call | solution.py:202
  131.1 0.8 copy-done.8
  131.8 11.5 %mlp_0.1.edge_ref = bf16[1008,512]{1,0:T(8,128)(2,1)} custom-call(s32[3]{0:T(128)} %pad_add_fusion.pos_ref, bf16[1008,512]{1,0:T(8,128)(2,1)} %bitcast.76, bf16[2304,512]{1,0:T(8,128)(2,1)} %bitcast.73, f32[1,512]{1,0:T(1,128)} %bitcast.71, bf16[4,144,512]{2,1,0:T(8,128)(2,1)} %copy-done.1, bf16[4,144,512]{2,1,0:T(8,128)(2,1)} %collective-permute-done.22.refs_1_, ...), custom_call_target="tpu_custom_call" | custom-call | flops 5040000000 | bytes 8096576 | tf_op jit(solution)/shard_map/mlp_0/pallas_call | solution.py:254
  143.3 1.0 slice_bitcast_fusion
  144.3 1.1 fusion.1
  145.4 0.8 slice_bitcast_fusion.2
  146.8 1.0 collective-permute-start.30
  147.9 12.4 %mlp_1008.1.inner_ref = bf16[1296,512]{1,0:T(8,128)(2,1)} custom-call(s32[3]{0:T(128)} %pad_add_fusion.pos_ref, bf16[1296,512]{1,0:T(8,128)(2,1)} %bitcast.75, bf16[2304,512]{1,0:T(8,128)(2,1)} %bitcast.74, f32[1,512]{1,0:T(1,128)} %bitcast.72, bf16[4,144,512]{2,1,0:T(8,128)(2,1)} %copy-done.1, bf16[4,144,512]{2,1,0:T(8,128)(2,1)} %collective-permute-done.22.refs_1_, ...), custom_call_target="tpu_custom_call" | custom-call | flops 6480000000 | bytes 8981312 | tf_op jit(solution)/shard_map/mlp_1008/pallas_call | solution.py:254
  160.4 4.6 %collective-permute-done.31.diag_ref = bf16[48,512]{1,0:T(8,128)(2,1)S(1)} collective-permute-done((bf16[48,512]{1,0:T(8,128)(2,1)S(1)}, bf16[48,512]{1,0:T(8,128)(2,1)S(1)}, u32[]{:S(2)}, u32[]{:S(2)}) %collective-permute-start.31) | collective-permute-done | bytes 49184 | tf_op jit(solution)/shard_map/ppermute | solution.py:64
  165.7 0.7 copy-done.10
  166.4 5.5 %to_grid.1 = bf16[1,2,24,48,512]{4,3,2,1,0:T(8,128)(2,1)} custom-call(bf16[1008,512]{1,0:T(8,128)(2,1)} %mlp_0.1.edge_ref, bf16[1296,512]{1,0:T(8,128)(2,1)} %mlp_1008.1.inner_ref, bf16[320,512]{1,0:T(8,128)(2,1)} %copy-done.9, bf16[320,512]{1,0:T(8,128)(2,1)} %copy-done.10, bf16[48,512]{1,0:T(8,128)(2,1)} %copy-done.13, ...), custom_call_target="tpu_custom_call" | custom-call | flops 3000000000 | bytes 8000000 | tf_op jit(solution)/shard_map/to_grid/pallas_call | solution.py:329
  (96 shorter events, 4.1 us)
Async XLA Ops:
  0.0 28.7 %copy-start = (bf16[1,2,24,48,512]{4,3,2,1,0:T(8,128)(2,1)S(1)}, bf16[1,2,24,48,512]{4,3,2,1,0:T(8,128)(2,1)}, u32[]{:S(2)}) copy-start(bf16[1,2,24,48,512]{4,3,2,1,0:T(8,128)(2,1)} %param.10) | copy-start | bytes 7077892
  1.7 14.5 %collective-permute-start.6 = (bf16[48,512]{1,0:T(8,128)(2,1)S(1)}, bf16[48,512]{1,0:T(8,128)(2,1)S(1)}, u32[]{:S(2)}, u32[]{:S(2)}) collective-permute-start(bf16[48,512]{1,0:T(8,128)(2,1)S(1)} %get-tuple-element.14), channel_id=1, source_target_pairs={{1,0},{2,1},{3,2},{0,3},{5,4},{6,5},{7,6},{4,7},{9,8},{10,9},{11,1... | collective-permute-start | bytes 147464 | tf_op jit(solution)/shard_map/ppermute | solution.py:40
  5.1 12.4 %collective-permute-start.7 = (bf16[48,512]{1,0:T(8,128)(2,1)S(1)}, bf16[48,512]{1,0:T(8,128)(2,1)S(1)}, u32[]{:S(2)}, u32[]{:S(2)}) collective-permute-start(bf16[48,512]{1,0:T(8,128)(2,1)S(1)} %get-tuple-element.14), channel_id=1, source_target_pairs={{2,0},{3,1},{0,2},{1,3},{6,4},{7,5},{4,6},{5,7},{10,8},{11,9},{8,1... | collective-permute-start | bytes 147464 | tf_op jit(solution)/shard_map/ppermute | solution.py:40
  5.6 11.9 %collective-permute-start.8 = (bf16[48,512]{1,0:T(8,128)(2,1)S(1)}, bf16[48,512]{1,0:T(8,128)(2,1)S(1)}, u32[]{:S(2)}, u32[]{:S(2)}) collective-permute-start(bf16[48,512]{1,0:T(8,128)(2,1)S(1)} %get-tuple-element.14), channel_id=1, source_target_pairs={{3,0},{0,1},{1,2},{2,3},{7,4},{4,5},{5,6},{6,7},{11,8},{8,9},{9,10... | collective-permute-start | bytes 147464 | tf_op jit(solution)/shard_map/ppermute | solution.py:40
  7.0 17.3 %collective-permute-start.2 = (bf16[2,3,6,512]{3,2,1,0:T(8,128)(2,1)S(1)}, bf16[2,3,6,512]{3,2,1,0:T(8,128)(2,1)S(1)}, u32[]{:S(2)}, u32[]{:S(2)}) collective-permute-start(bf16[2,3,6,512]{3,2,1,0:T(8,128)(2,1)S(1)} %slice.70), channel_id=1, source_target_pairs={{9,0},{10,1},{11,2},{12,3},{13,4},{14,5},{15,6},{8,7},{17,8},{18,9... | collective-permute-start | bytes 110600 | tf_op jit(solution)/shard_map/ppermute | solution.py:64
  16.0 4.5 %collective-permute-start.5 = (bf16[3,6]{0,1:T(8,128)(2,1)S(1)}, bf16[3,6]{0,1:T(8,128)(2,1)S(1)}, u32[]{:S(2)}, u32[]{:S(2)}) collective-permute-start(bf16[3,6]{0,1:T(8,128)(2,1)S(1)} %slice.73), channel_id=1, source_target_pairs={{9,0},{10,1},{11,2},{12,3},{13,4},{14,5},{15,6},{8,7},{17,8},{18,9... | collective-permute-start | bytes 116 | tf_op jit(solution)/shard_map/ppermute | solution.py:64
  16.2 6.0 %collective-permute-start.4 = (bf16[24,6]{0,1:T(8,128)(2,1)S(1)}, bf16[24,6]{0,1:T(8,128)(2,1)S(1)}, u32[]{:S(2)}, u32[]{:S(2)}) collective-permute-start(bf16[24,6]{0,1:T(8,128)(2,1)S(1)} %slice.72), channel_id=1, source_target_pairs={{1,0},{2,1},{3,2},{4,3},{5,4},{6,5},{7,6},{0,7},{9,8},{10,9},{11,1... | collective-permute-start | bytes 872 | tf_op jit(solution)/shard_map/ppermute | solution.py:64
  17.4 6.8 %collective-permute-start.3 = (bf16[3,48]{0,1:T(8,128)(2,1)S(1)}, bf16[3,48]{0,1:T(8,128)(2,1)}, u32[]{:S(2)}, u32[]{:S(2)}) collective-permute-start(bf16[3,48]{0,1:T(8,128)(2,1)S(1)} %bitcast.61), channel_id=1, source_target_pairs={{8,0},{9,1},{10,2},{11,3},{12,4},{13,5},{14,6},{15,7},{16,8},{17,9... | collective-permute-start | bytes 872 | tf_op jit(solution)/shard_map/ppermute | solution.py:64
  18.2 7.3 %collective-permute-start.11 = (bf16[48,512]{1,0:T(8,128)(2,1)}, bf16[48,512]{1,0:T(8,128)(2,1)S(1)}, u32[]{:S(2)}, u32[]{:S(2)}) collective-permute-start(bf16[48,512]{1,0:T(8,128)(2,1)} %reshape.49), channel_id=1, source_target_pairs={{68,0},{69,1},{70,2},{71,3},{64,4},{65,5},{66,6},{67,7},{76,8},{77... | collective-permute-start | bytes 147464 | tf_op jit(solution)/shard_map/ppermute | solution.py:40
  20.5 9.6 %collective-permute-start.10 = (bf16[48,512]{1,0:T(8,128)(2,1)}, bf16[48,512]{1,0:T(8,128)(2,1)S(1)}, u32[]{:S(2)}, u32[]{:S(2)}) collective-permute-start(bf16[48,512]{1,0:T(8,128)(2,1)} %reshape.49), channel_id=1, source_target_pairs={{4,0},{5,1},{6,2},{7,3},{0,4},{1,5},{2,6},{3,7},{12,8},{13,9},{14,... | collective-permute-start | bytes 147464 | tf_op jit(solution)/shard_map/ppermute | solution.py:40
  22.2 4.8 %copy-start.5 = (bf16[24,6]{0,1:T(8,128)(2,1)}, bf16[24,6]{0,1:T(8,128)(2,1)S(1)}, u32[]{:S(2)}) copy-start(bf16[24,6]{0,1:T(8,128)(2,1)S(1)} %collective-permute-done.4) | copy-start | bytes 868
  22.2 10.0 %collective-permute-start.9 = (bf16[48,512]{1,0:T(8,128)(2,1)}, bf16[48,512]{1,0:T(8,128)(2,1)S(1)}, u32[]{:S(2)}, u32[]{:S(2)}) collective-permute-start(bf16[48,512]{1,0:T(8,128)(2,1)} %reshape.49), channel_id=1, source_target_pairs={{64,0},{65,1},{66,2},{67,3},{68,4},{69,5},{70,6},{71,7},{72,8},{73... | collective-permute-start | bytes 147464 | tf_op jit(solution)/shard_map/ppermute | solution.py:40
  24.2 10.0 %collective-permute-start.21 = (bf16[144,512]{1,0:T(8,128)(2,1)}, bf16[144,512]{1,0:T(8,128)(2,1)S(1)}, u32[]{:S(2)}, u32[]{:S(2)}) collective-permute-start(bf16[144,512]{1,0:T(8,128)(2,1)} %get-tuple-element.22), channel_id=1, source_target_pairs={{68,0},{69,1},{70,2},{71,3},{64,4},{65,5},{66,6},{67,7},{76,8},{77... | collective-permute-start | bytes 442376 | tf_op jit(solution)/shard_map/ppermute | solution.py:40
  24.3 10.8 %collective-permute-start.20 = (bf16[144,512]{1,0:T(8,128)(2,1)}, bf16[144,512]{1,0:T(8,128)(2,1)S(1)}, u32[]{:S(2)}, u32[]{:S(2)}) collective-permute-start(bf16[144,512]{1,0:T(8,128)(2,1)} %get-tuple-element.22), channel_id=1, source_target_pairs={{4,0},{5,1},{6,2},{7,3},{0,4},{1,5},{2,6},{3,7},{12,8},{13,9},{14,... | collective-permute-start | bytes 442376 | tf_op jit(solution)/shard_map/ppermute | solution.py:40
  25.5 1.5 copy-start.4
  25.5 10.9 %collective-permute-start.19 = (bf16[144,512]{1,0:T(8,128)(2,1)}, bf16[144,512]{1,0:T(8,128)(2,1)}, u32[]{:S(2)}, u32[]{:S(2)}) collective-permute-start(bf16[144,512]{1,0:T(8,128)(2,1)} %get-tuple-element.22), channel_id=1, source_target_pairs={{64,0},{65,1},{66,2},{67,3},{68,4},{69,5},{70,6},{71,7},{72,8},{73... | collective-permute-start | bytes 442376 | tf_op jit(solution)/shard_map/ppermute | solution.py:40
  30.1 8.4 %collective-permute-start.1 = (bf16[2,24,6,512]{3,2,1,0:T(8,128)(2,1)S(1)}, bf16[2,24,6,512]{3,2,1,0:T(8,128)(2,1)}, u32[]{:S(2)}, u32[]{:S(2)}) collective-permute-start(bf16[2,24,6,512]{3,2,1,0:T(8,128)(2,1)S(1)} %slice.69), channel_id=1, source_target_pairs={{1,0},{2,1},{3,2},{4,3},{5,4},{6,5},{7,6},{0,7},{9,8},{10,9},{11,1... | collective-permute-start | bytes 884744 | tf_op jit(solution)/shard_map/ppermute | solution.py:64
  32.1 12.8 %collective-permute-start = (bf16[2,3,48,512]{3,2,1,0:T(8,128)(2,1)}, bf16[2,3,48,512]{3,2,1,0:T(8,128)(2,1)}, u32[]{:S(2)}, u32[]{:S(2)}) collective-permute-start(bf16[2,3,48,512]{3,2,1,0:T(8,128)(2,1)} %slice.68), channel_id=1, source_target_pairs={{8,0},{9,1},{10,2},{11,3},{12,4},{13,5},{14,6},{15,7},{16,8},{17,9... | collective-permute-start | bytes 884744 | tf_op jit(solution)/shard_map/ppermute | solution.py:64
  34.2 3.1 %copy-start.2 = (bf16[144,512]{1,0:T(8,128)(2,1)}, bf16[144,512]{1,0:T(8,128)(2,1)S(1)}, u32[]{:S(2)}) copy-start(bf16[144,512]{1,0:T(8,128)(2,1)S(1)} %collective-permute-done.21) | copy-start | bytes 442372
  34.2 11.6 %collective-permute-start.12 = (bf16[4,48,512]{2,1,0:T(8,128)(2,1)}, bf16[4,48,512]{2,1,0:T(8,128)(2,1)}, u32[]{:S(2)}, u32[]{:S(2)}) collective-permute-start(bf16[4,48,512]{2,1,0:T(8,128)(2,1)} %pad_maximum_fusion.3.refs_0_), channel_id=1, source_target_pairs={{8,0},{9,1},{10,2},{11,3},{12,4},{13,5},{14,6},{15,7},{16,8},{17,9... | collective-permute-start | bytes 589832 | tf_op jit(solution)/shard_map/ppermute | solution.py:40
  35.0 2.3 %copy-start.3 = (bf16[144,512]{1,0:T(8,128)(2,1)}, bf16[144,512]{1,0:T(8,128)(2,1)S(1)}, u32[]{:S(2)}) copy-start(bf16[144,512]{1,0:T(8,128)(2,1)S(1)} %collective-permute-done.20) | copy-start | bytes 442372
  35.0 12.5 %collective-permute-start.13 = (bf16[4,48,512]{2,1,0:T(8,128)(2,1)}, bf16[4,48,512]{2,1,0:T(8,128)(2,1)}, u32[]{:S(2)}, u32[]{:S(2)}) collective-permute-start(bf16[4,48,512]{2,1,0:T(8,128)(2,1)} %pad_maximum_fusion.3.refs_0_), channel_id=1, source_target_pairs={{16,0},{17,1},{18,2},{19,3},{20,4},{21,5},{22,6},{23,7},{24,8},{25... | collective-permute-start | bytes 589832 | tf_op jit(solution)/shard_map/ppermute | solution.py:40
  36.4 11.2 %collective-permute-start.14 = (bf16[4,48,512]{2,1,0:T(8,128)(2,1)}, bf16[4,48,512]{2,1,0:T(8,128)(2,1)}, u32[]{:S(2)}, u32[]{:S(2)}) collective-permute-start(bf16[4,48,512]{2,1,0:T(8,128)(2,1)} %pad_maximum_fusion.3.refs_0_), channel_id=1, source_target_pairs={{24,0},{25,1},{26,2},{27,3},{28,4},{29,5},{30,6},{31,7},{0,8},{1,9... | collective-permute-start | bytes 589832 | tf_op jit(solution)/shard_map/ppermute | solution.py:40
  38.5 33.7 %copy-start.1 = (bf16[4,144,512]{2,1,0:T(8,128)(2,1)}, bf16[4,144,512]{2,1,0:T(8,128)(2,1)S(1)}, u32[]{:S(2)}) copy-start(bf16[4,144,512]{2,1,0:T(8,128)(2,1)S(1)} %pad_maximum_fusion.refs_0_) | copy-start | bytes 1769476
  38.5 32.2 %collective-permute-start.15 = (bf16[4,48,512]{2,1,0:T(8,128)(2,1)}, bf16[4,48,512]{2,1,0:T(8,128)(2,1)S(1)}, u32[]{:S(2)}, u32[]{:S(2)}) collective-permute-start(bf16[4,48,512]{2,1,0:T(8,128)(2,1)} %pad_maximum_fusion.3.refs_0_), channel_id=1, source_target_pairs={{32,0},{33,1},{34,2},{35,3},{36,4},{37,5},{38,6},{39,7},{40,8},{41... | collective-permute-start | bytes 589832 | tf_op jit(solution)/shard_map/ppermute | solution.py:40
  44.9 60.1 %collective-permute-start.22 = (bf16[4,144,512]{2,1,0:T(8,128)(2,1)S(1)}, bf16[4,144,512]{2,1,0:T(8,128)(2,1)}, u32[]{:S(2)}, u32[]{:S(2)}) collective-permute-start(bf16[4,144,512]{2,1,0:T(8,128)(2,1)S(1)} %pad_maximum_fusion.refs_0_), channel_id=1, source_target_pairs={{8,0},{9,1},{10,2},{11,3},{12,4},{13,5},{14,6},{15,7},{16,8},{17,9... | collective-permute-start | bytes 1769480 | tf_op jit(solution)/shard_map/ppermute | solution.py:40
  45.9 26.2 %collective-permute-start.16 = (bf16[4,48,512]{2,1,0:T(8,128)(2,1)}, bf16[4,48,512]{2,1,0:T(8,128)(2,1)S(1)}, u32[]{:S(2)}, u32[]{:S(2)}) collective-permute-start(bf16[4,48,512]{2,1,0:T(8,128)(2,1)} %collective-permute-done.12.refs_1_), channel_id=1, source_target_pairs={{32,0},{33,1},{34,2},{35,3},{36,4},{37,5},{38,6},{39,7},{40,8},{41... | collective-permute-start | bytes 589832 | tf_op jit(solution)/shard_map/ppermute | solution.py:40
  47.5 24.7 %collective-permute-start.17 = (bf16[4,48,512]{2,1,0:T(8,128)(2,1)}, bf16[4,48,512]{2,1,0:T(8,128)(2,1)}, u32[]{:S(2)}, u32[]{:S(2)}) collective-permute-start(bf16[4,48,512]{2,1,0:T(8,128)(2,1)} %collective-permute-done.13.refs_2_), channel_id=1, source_target_pairs={{32,0},{33,1},{34,2},{35,3},{36,4},{37,5},{38,6},{39,7},{40,8},{41... | collective-permute-start | bytes 589832 | tf_op jit(solution)/shard_map/ppermute | solution.py:40
  47.6 25.8 %collective-permute-start.18 = (bf16[4,48,512]{2,1,0:T(8,128)(2,1)}, bf16[4,48,512]{2,1,0:T(8,128)(2,1)}, u32[]{:S(2)}, u32[]{:S(2)}) collective-permute-start(bf16[4,48,512]{2,1,0:T(8,128)(2,1)} %collective-permute-done.14.refs_3_), channel_id=1, source_target_pairs={{32,0},{33,1},{34,2},{35,3},{36,4},{37,5},{38,6},{39,7},{40,8},{41... | collective-permute-start | bytes 589832 | tf_op jit(solution)/shard_map/ppermute | solution.py:40
  70.7 2.7 %copy-start.11 = (bf16[4,48,512]{2,1,0:T(8,128)(2,1)}, bf16[4,48,512]{2,1,0:T(8,128)(2,1)S(1)}, u32[]{:S(2)}) copy-start(bf16[4,48,512]{2,1,0:T(8,128)(2,1)S(1)} %collective-permute-done.15.refs_4_) | copy-start | bytes 589828
  70.7 34.4 %collective-permute-start.23 = (bf16[4,144,512]{2,1,0:T(8,128)(2,1)S(1)}, bf16[4,144,512]{2,1,0:T(8,128)(2,1)S(1)}, u32[]{:S(2)}, u32[]{:S(2)}) collective-permute-start(bf16[4,144,512]{2,1,0:T(8,128)(2,1)S(1)} %pad_maximum_fusion.refs_0_), channel_id=1, source_target_pairs={{16,0},{17,1},{18,2},{19,3},{20,4},{21,5},{22,6},{23,7},{24,8},{25... | collective-permute-start | bytes 1769480 | tf_op jit(solution)/shard_map/ppermute | solution.py:40
  72.1 1.3 copy-start.12
  72.1 33.5 %collective-permute-start.24 = (bf16[4,144,512]{2,1,0:T(8,128)(2,1)S(1)}, bf16[4,144,512]{2,1,0:T(8,128)(2,1)S(1)}, u32[]{:S(2)}, u32[]{:S(2)}) collective-permute-start(bf16[4,144,512]{2,1,0:T(8,128)(2,1)S(1)} %pad_maximum_fusion.refs_0_), channel_id=1, source_target_pairs={{24,0},{25,1},{26,2},{27,3},{28,4},{29,5},{30,6},{31,7},{0,8},{1,9... | collective-permute-start | bytes 1769480 | tf_op jit(solution)/shard_map/ppermute | solution.py:40
  72.2 58.8 %collective-permute-start.25 = (bf16[4,144,512]{2,1,0:T(8,128)(2,1)S(1)}, bf16[4,144,512]{2,1,0:T(8,128)(2,1)S(1)}, u32[]{:S(2)}, u32[]{:S(2)}) collective-permute-start(bf16[4,144,512]{2,1,0:T(8,128)(2,1)S(1)} %pad_maximum_fusion.refs_0_), channel_id=1, source_target_pairs={{32,0},{33,1},{34,2},{35,3},{36,4},{37,5},{38,6},{39,7},{40,8},{41... | collective-permute-start | bytes 1769480 | tf_op jit(solution)/shard_map/ppermute | solution.py:40
  105.0 26.0 %collective-permute-start.26 = (bf16[4,144,512]{2,1,0:T(8,128)(2,1)}, bf16[4,144,512]{2,1,0:T(8,128)(2,1)}, u32[]{:S(2)}, u32[]{:S(2)}) collective-permute-start(bf16[4,144,512]{2,1,0:T(8,128)(2,1)} %collective-permute-done.22.refs_1_), channel_id=1, source_target_pairs={{32,0},{33,1},{34,2},{35,3},{36,4},{37,5},{38,6},{39,7},{40,8},{41... | collective-permute-start | bytes 1769480 | tf_op jit(solution)/shard_map/ppermute | solution.py:40
  105.1 25.9 %copy-start.6 = (bf16[4,144,512]{2,1,0:T(8,128)(2,1)}, bf16[4,144,512]{2,1,0:T(8,128)(2,1)S(1)}, u32[]{:S(2)}) copy-start(bf16[4,144,512]{2,1,0:T(8,128)(2,1)S(1)} %collective-permute-done.23.refs_2_) | copy-start | bytes 1769476
  105.1 25.9 %collective-permute-start.27 = (bf16[4,144,512]{2,1,0:T(8,128)(2,1)S(1)}, bf16[4,144,512]{2,1,0:T(8,128)(2,1)}, u32[]{:S(2)}, u32[]{:S(2)}) collective-permute-start(bf16[4,144,512]{2,1,0:T(8,128)(2,1)S(1)} %collective-permute-done.23.refs_2_), channel_id=1, source_target_pairs={{32,0},{33,1},{34,2},{35,3},{36,4},{37,5},{38,6},{39,7},{40,8},{41... | collective-permute-start | bytes 1769480 | tf_op jit(solution)/shard_map/ppermute | solution.py:40
  105.6 25.4 %copy-start.7 = (bf16[4,144,512]{2,1,0:T(8,128)(2,1)}, bf16[4,144,512]{2,1,0:T(8,128)(2,1)S(1)}, u32[]{:S(2)}) copy-start(bf16[4,144,512]{2,1,0:T(8,128)(2,1)S(1)} %collective-permute-done.24.refs_3_) | copy-start | bytes 1769476
  105.6 25.4 %collective-permute-start.28 = (bf16[4,144,512]{2,1,0:T(8,128)(2,1)S(1)}, bf16[4,144,512]{2,1,0:T(8,128)(2,1)}, u32[]{:S(2)}, u32[]{:S(2)}) collective-permute-start(bf16[4,144,512]{2,1,0:T(8,128)(2,1)S(1)} %collective-permute-done.24.refs_3_), channel_id=1, source_target_pairs={{32,0},{33,1},{34,2},{35,3},{36,4},{37,5},{38,6},{39,7},{40,8},{41... | collective-permute-start | bytes 1769480 | tf_op jit(solution)/shard_map/ppermute | solution.py:40
  131.0 0.8 copy-start.8
  146.2 18.7 %collective-permute-start.29 = (bf16[320,512]{1,0:T(8,128)(2,1)S(1)}, bf16[320,512]{1,0:T(8,128)(2,1)S(1)}, u32[]{:S(2)}, u32[]{:S(2)}) collective-permute-start(bf16[320,512]{1,0:T(8,128)(2,1)S(1)} %pad_maximum_fusion.1), channel_id=1, source_target_pairs={{24,0},{25,1},{26,2},{27,3},{28,4},{29,5},{30,6},{31,7},{0,8},{1,9... | collective-permute-start | bytes 983048 | tf_op jit(solution)/shard_map/ppermute | solution.py:64
  146.8 18.1 %collective-permute-start.30 = (bf16[320,512]{1,0:T(8,128)(2,1)S(1)}, bf16[320,512]{1,0:T(8,128)(2,1)S(1)}, u32[]{:S(2)}, u32[]{:S(2)}) collective-permute-start(bf16[320,512]{1,0:T(8,128)(2,1)S(1)} %pad_maximum_fusion.2), channel_id=1, source_target_pairs={{7,0},{0,1},{1,2},{2,3},{3,4},{4,5},{5,6},{6,7},{15,8},{8,9},{9,10... | collective-permute-start | bytes 983048 | tf_op jit(solution)/shard_map/ppermute | solution.py:64
  147.8 17.1 %collective-permute-start.31 = (bf16[48,512]{1,0:T(8,128)(2,1)S(1)}, bf16[48,512]{1,0:T(8,128)(2,1)S(1)}, u32[]{:S(2)}, u32[]{:S(2)}) collective-permute-start(bf16[48,512]{1,0:T(8,128)(2,1)S(1)} %slice_bitcast_fusion.2), channel_id=1, source_target_pairs={{31,0},{24,1},{25,2},{26,3},{27,4},{28,5},{29,6},{30,7},{7,8},{0,9... | collective-permute-start | bytes 147464 | tf_op jit(solution)/shard_map/ppermute | solution.py:64
  164.9 0.6 copy-start.13
  164.9 0.7 copy-start.9
  165.7 0.7 copy-start.10

commit v2 on v1

v2 whole, which is shorter than its diff:
```python
import functools
import math

import jax
import jax.numpy as jnp
import numpy as np
from jax import lax
from jax.experimental import pallas as pl
from jax.experimental.pallas import tpu as pltpu
from jax.sharding import PartitionSpec as P

D = 512
HDIM = 32
FF = 2048
SH = 3
SL = 6
TOK = 144
EDGE = 7
INNER = 9
AXES = ("mem", "lat", "lon")
MASKED = -1e30
EXP2_SCALE = math.log2(math.e) / math.sqrt(HDIM)
BF16 = jnp.bfloat16
F32 = jnp.float32
NT = (((1,), (1,)), ((), ()))

eps = 1e-05


def place(j):
    return j & 3, ((j >> 2) & 1) * 2 + ((j >> 6) & 1), (j >> 3) & 3, (j >> 5) & 1


def flat(x, y, z, core):
    return ((y & 1) << 6) | (core << 5) | (z << 3) | ((y >> 1) << 2) | x


def send(block, source_of):
    pairs = [(flat(*source_of(*place(j))), j) for j in range(128)]
    return lax.ppermute(block, AXES, pairs)


def along_x(block, d):
    return send(block, lambda x, y, z, c: ((x + d) % 4, y, z, c))


def along_first(block, d):
    return send(block, lambda x, y, z, c: (x, (y + d * (1 - c)) % 4, (z + d * c) % 4, c))


def along_second(block, d):
    return send(block, lambda x, y, z, c: (x, (y + d * c) % 4, (z + d * (1 - c)) % 4, c))


def other_core(block):
    return send(block, lambda x, y, z, c: (x, y, z, 1 - c))


def from_grid(block, dlat, dlon):
    pairs = []
    for j in range(128):
        mem, lat, lon = j >> 5, (j >> 3) & 3, j & 7
        pairs.append((mem * 32 + ((lat + dlat) % 4) * 8 + (lon + dlon) % 8, j))
    return lax.ppermute(block, AXES, pairs)


def norm(values, gain):
    average = jnp.mean(values, axis=-1, keepdims=True)
    centred = values - average
    variance = jnp.mean(centred * centred, axis=-1, keepdims=True)
    return (centred * lax.rsqrt(variance + eps) * gain).astype(BF16)


def prep_kernel(member_ref, rows_ref, cols_ref, both_ref, ids_ref, gain_ref, f_ref, x_ref, xq_ref, bias_ref, ext, near_ref):
    step = pl.program_id(0)

    @pl.when(step == 0)
    def _():
        ext[:, 0:24, 0:48] = member_ref[...]
        for lev in range(2):
            for n in range(24):
                at = (24 * lev + n) * 8
                ext[lev, n, 48:56] = cols_ref[at : at + 8]
            for n in range(3):
                at = 3 * lev + n
                ext[lev, 24 + n, 0:48] = rows_ref[48 * at : 48 * at + 48]
                ext[lev, 24 + n, 48:56] = both_ref[8 * at : 8 * at + 8]
        ext[:, :, 56:64] = jnp.zeros((2, 27, 8, D), BF16)
        ids = ids_ref[...].astype(F32)
        for ref, at in ((rows_ref, 288), (cols_ref, 384), (both_ref, 48)):
            ids = ids + ref[at : at + 32, 0:128].astype(F32)
        near_ref[...] = jnp.concatenate([ids, jnp.zeros((96, 128), F32)], axis=0).T

    col = lax.broadcasted_iota(jnp.int32, (1, 384), 1)
    seg = col // 32
    lev = (seg >= 6).astype(jnp.int32)
    r = seg - 6 * lev
    rh = (r >= 3).astype(jnp.int32)
    lane = lax.broadcasted_iota(jnp.int32, (32, 128), 1)
    every = jnp.ones((128, 128), BF16)
    for at in range(4):
        i = 4 * step + at
        k = i - EDGE
        wi = jnp.where(i < 4, 3, jnp.where(i < EDGE, i - 4, k // 3))
        wj = jnp.where(i < 4, i, jnp.where(i < EDGE, 3, k % 3))
        base = jnp.where(wj < 2, 0, jnp.where(wj == 2, 16, 32))
        cc = col - seg * 32 - (12 * wj + SL - base)
        ch = (cc >= 6).astype(jnp.int32)
        quad = jnp.where(wj == 3, ch * 2 + rh, rh * 2 + ch)
        row = quad * 36 + lev * 18 + (r - 3 * rh) * 6 + cc - 6 * ch
        row = jnp.where((cc >= 0) & (cc < 12), row, -1)
        pick = (lax.broadcasted_iota(jnp.int32, (TOK, 384), 0) == row).astype(F32).astype(BF16)
        start = pl.multiple_of(base, 16)
        tokens = jnp.concatenate(
            [ext[n // 6, 6 * wi + SH + n % 6, pl.ds(start, 32), :] for n in range(12)], axis=0
        )
        f = jnp.dot(pick, tokens, preferred_element_type=F32)
        f_ref[at] = f.astype(BF16)
        x = norm(f, gain_ref[...])
        x_ref[at] = x
        xq_ref[at, 0:128] = x[0:128]
        for t in range(8):
            xq_ref[at, 128 + 16 * t : 144 + 16 * t] = x[128:144]
        near = near_ref[pl.ds(start, 32), :]
        marks = [jnp.where(lane == 6 * wi + SH + n, near, 0.0).astype(BF16) for n in range(6)]
        marks = jnp.dot(pick, jnp.concatenate(marks * 2, axis=0), preferred_element_type=F32)
        idk = jnp.dot(marks.astype(BF16), every, preferred_element_type=F32)
        idq = jnp.concatenate([idk[0:128]] + [idk[128:144]] * 8, axis=0).T[0:1]
        bias_ref[at] = jnp.where(jnp.concatenate([idk, idk], axis=1) == idq, 0.0, MASKED).astype(BF16)


def prep(*operands):
    n = EDGE + INNER
    whole = lambda a: pl.BlockSpec(a.shape, lambda i: (0,) * a.ndim, pipeline_mode=pl.Buffered(1))
    out = lambda *s: (jax.ShapeDtypeStruct((n, *s), BF16), pl.BlockSpec((4, *s), lambda i: (i, 0, 0)))
    shapes, specs = zip(out(TOK, D), out(TOK, D), out(256, D), out(TOK, 256))
    return pl.pallas_call(
        prep_kernel,
        grid=(n // 4,),
        in_specs=[whole(a) for a in operands],
        out_specs=specs,
        out_shape=shapes,
        scratch_shapes=[pltpu.VMEM((2, 27, 64, D), BF16), pltpu.VMEM((128, 128), F32)],
        name="prep",
        cost_estimate=pl.CostEstimate(flops=6_000_000_000, bytes_accessed=16_000_000, transcendentals=0),
    )(*operands)


def block_rows(pos_ref, side, d2, d3):
    core = pos_ref[2]
    core = core if side == 0 else 1 - core
    dy = jnp.where(core == 0, d2, d3)
    dz = jnp.where(core == 0, d3, d2)
    y = (pos_ref[0] + dy) % 4
    z = (pos_ref[1] + dz) % 4
    return (y % 2) * 16 + core * 8 + z * 2 + y // 2


def attn_kernel(pos_ref, x_ref, xq_a, xq_b, xv_a, xv_b, bias_ref, *refs):
    pieces, out_ref = refs[:2], refs[2]
    w, kall, own = refs[3:6]
    q2, v2, s2, p2, m2 = (refs[n : n + 2] for n in range(6, 16, 2))
    i = pl.program_id(0)

    @pl.when(i == 0)
    def _():
        for p in range(8):
            for d2 in range(4):
                b = block_rows(pos_ref, p // 4, d2, p % 4)
                w[pl.ds(pl.multiple_of(b * 48, 16), 48), :] = pieces[p // 4][p % 4, d2]
        keys = lax.dot_general(x_ref[...], w[D : 2 * D, :], NT, preferred_element_type=F32)
        kall[...] = keys.astype(BF16)
        own[...] = (
            lax.broadcasted_iota(jnp.int32, (256, 128), 0) // 32
            == lax.broadcasted_iota(jnp.int32, (256, 128), 1) // 16
        ).astype(F32).astype(BF16)

    ones = jnp.ones((16, TOK), BF16)
    zeros = jnp.zeros((32, 128), BF16)

    def project(dst, x, first, n):
        at = 256 * n
        out = lax.dot_general(w[first + at : first + at + 256, :], x[0], NT, preferred_element_type=F32)
        dst[at : at + 256] = out.astype(BF16)

    def scores(qt, s, krow, n):
        if n < 8:
            g = n // 2
            heads = []
            for h in (2 * (n % 2), 2 * (n % 2) + 1):
                q = qt[128 * g + 32 * h : 128 * g + 32 * h + 32, 0:128]
                heads.append(jnp.concatenate([zeros] * h + [q] + [zeros] * (3 - h), axis=0))
            kg = kall[pl.ds(krow, TOK), 128 * g : 128 * g + 128]
            s[:, 256 * n : 256 * n + 256] = jnp.dot(
                kg, jnp.concatenate(heads, axis=1), preferred_element_type=F32
            )
        else:
            for a in range(2):
                q = qt[256 * a : 256 * a + 256, 128:256] * own[...]
                s[:, 2048 + 128 * a : 2176 + 128 * a] = jnp.dot(
                    kall[pl.ds(krow, TOK), 256 * a : 256 * a + 256], q, preferred_element_type=F32
                )

    def soften(s, p, win, n):
        side = 0 if n < 8 else 128
        bias = bias_ref[win, :, side : side + 128].astype(F32)
        for at in (256 * n, 256 * n + 128):
            v = s[:, at : at + 128] + bias
            m = jnp.max(v, axis=0, keepdims=True)
            p[:, at : at + 128] = jnp.exp2((v - m) * EXP2_SCALE).astype(BF16)

    def mix(vt, p, mt, n):
        at = 64 * n
        if n < 8:
            lhs = jnp.concatenate([vt[at : at + 64, 0:TOK], ones], axis=0)
            o = jnp.dot(lhs, p[:, 256 * n : 256 * n + 256], preferred_element_type=F32)
            inv = 1.0 / o[64:65]
            mt[at : at + 32, 0:128] = o[0:32, 0:128] * inv[:, 0:128]
            mt[at + 32 : at + 64, 0:128] = o[32:64, 128:256] * inv[:, 128:256]
        else:
            lhs = jnp.concatenate([vt[:, 0:TOK], ones], axis=0)
            o = jnp.dot(lhs, p[:, 2048:2304], preferred_element_type=F32)
            inv = 1.0 / o[D : D + 1]
            for h in range(16):
                side = 128 * (h // 8)
                part = o[32 * h : 32 * h + 32, side : side + 128] * inv[:, side : side + 128]
                mt[32 * h : 32 * h + 32, 128:256] = pltpu.roll(part, (128 - 16 * (h % 8)) % 128, 1)

    def half(par, win, xq, xv):
        new, old = par, 1 - par
        krow = pl.multiple_of(jnp.clip(win - 1, 0, 15) * TOK, 16)
        soft = jnp.clip(win - 2, 0, 15)
        for n in range(9):
            if n < 2:
                project(q2[new], xq, 0, n)
            elif n < 4:
                project(v2[new], xv, 2 * D, n - 2)
            scores(q2[old], s2[old], krow, n)
            soften(s2[new], p2[new], soft, n)
            mix(v2[old], p2[old], m2[old], n)
        out_ref[old] = m2[old][...].T[0:TOK].astype(BF16)

    half(1, 2 * i - 1, xq_a, xv_a)
    half(0, 2 * i, xq_b, xv_b)


def attend(pos, x, xq, bias, pieces):
    whole = lambda a: pl.BlockSpec(a.shape, lambda i: (0,) * a.ndim, pipeline_mode=pl.Buffered(1))
    one = lambda d: pl.BlockSpec((1, 256, D), lambda i: (jnp.clip(2 * i + d, 0, 15), 0, 0))
    return pl.pallas_call(
        attn_kernel,
        grid=(10,),
        in_specs=[
            pl.BlockSpec(memory_space=pltpu.SMEM),
            whole(x),
            one(-1),
            one(0),
            one(-3),
            one(-2),
            whole(bias),
            *[whole(p) for p in pieces],
        ],
        out_specs=pl.BlockSpec((2, TOK, D), lambda i: (jnp.clip(i - 2, 0, 7), 0, 0)),
        out_shape=jax.ShapeDtypeStruct((16, TOK, D), BF16),
        scratch_shapes=[
            pltpu.VMEM((3 * D, D), BF16),
            pltpu.VMEM((16 * TOK, D), BF16),
            pltpu.VMEM((256, 128), BF16),
            *[pltpu.VMEM((D, 256), BF16)] * 4,
            *[pltpu.VMEM((TOK, 2304), F32)] * 2,
            *[pltpu.VMEM((TOK, 2304), BF16)] * 2,
            *[pltpu.VMEM((D, 256), F32)] * 2,
        ],
        name="attend",
        cost_estimate=pl.CostEstimate(flops=20_000_000_000, bytes_accessed=12_000_000, transcendentals=5_000_000),
    )(pos, x, xq, xq, xq, xq, bias, *pieces)


def mlp_kernel(pos_ref, mixed_ref, f_ref, gain_ref, *refs):
    pieces, out_ref, (wp, wu, wd, held, normed) = refs[:8], refs[8], refs[9:]

    @pl.when(pl.program_id(0) == 0)
    def _():
        for d3 in range(4):
            for d2 in range(4):
                for side in range(2):
                    b = block_rows(pos_ref, side, d2, d3)
                    piece = pieces[4 * side + d3].at[d2]
                    wp[pl.ds(pl.multiple_of(b * 16, 16), 16), :] = piece[0:16]
                    wu[pl.ds(pl.multiple_of(b * 64, 16), 64), :] = piece[16:80]
                    for c in range(4):
                        wd[c, pl.ds(pl.multiple_of(b * 16, 16), 16), :] = piece[80 + 16 * c : 96 + 16 * c]

    rows = out_ref.shape[0]
    sub = rows // 2

    def first(j):
        r = slice(j * sub, (j + 1) * sub)
        attn = lax.dot_general(mixed_ref[r], wp[...], NT, preferred_element_type=F32).astype(BF16)
        resid = (f_ref[r].astype(F32) + attn.astype(F32)).astype(BF16)
        held[r] = resid
        normed[r] = norm(resid.astype(F32), gain_ref[...])

    def second(j):
        r = slice(j * sub, (j + 1) * sub)
        total = None
        for c in range(4):
            pre = lax.dot_general(normed[r], wu[512 * c : 512 * c + 512, :], NT, preferred_element_type=F32)
            hidden = (0.5 * pre * (1.0 + lax.erf(pre * math.sqrt(0.5)))).astype(BF16)
            part = lax.dot_general(hidden, wd[c], NT, preferred_element_type=F32)
            total = part if total is None else total + part
        out_ref[r] = (held[r].astype(F32) + total).astype(BF16)

    first(0)
    first(1)
    second(0)
    second(1)


def mlp(pos, mixed, f, gain, pieces, first, rows):
    run = pl.BlockSpec((pl.Element(rows), pl.Element(D)), lambda i: (first, 0), pipeline_mode=pl.Buffered(1))
    whole = lambda a: pl.BlockSpec(a.shape, lambda i: (0,) * a.ndim, pipeline_mode=pl.Buffered(1))
    return pl.pallas_call(
        mlp_kernel,
        grid=(1,),
        in_specs=[
            pl.BlockSpec(memory_space=pltpu.SMEM),
            run,
            run,
            whole(gain),
            *[whole(p) for p in pieces],
        ],
        out_specs=pl.BlockSpec((rows, D), lambda i: (0, 0)),
        out_shape=jax.ShapeDtypeStruct((rows, D), BF16),
        scratch_shapes=[
            pltpu.VMEM((D, D), BF16),
            pltpu.VMEM((FF, D), BF16),
            pltpu.VMEM((4, D, D), BF16),
            pltpu.VMEM((rows, D), BF16),
            pltpu.VMEM((rows, D), BF16),
        ],
        name=f"mlp_{first}",
        compiler_params=pltpu.CompilerParams(vmem_limit_bytes=26 * 2**20),
        cost_estimate=pl.CostEstimate(
            flops=rows * 5_000_000, bytes_accessed=rows * 3072 + 5_000_000, transcendentals=rows * 2048
        ),
    )(pos, mixed, f, gain, *pieces)


def place_matrices():
    top = np.zeros((288, 368), np.float32)
    mid = np.zeros((576, 656), np.float32)
    for lev in range(2):
        for rr in range(3):
            for c in range(48):
                o = lev * 144 + rr * 48 + c
                at = lev * 18 + rr * 6
                wj, cc = (c - 6) // 12, (c - 6) % 12
                ch, c1 = cc // 6, cc % 6
                if c < 6:
                    top[o, 320 + 12 + at + c] = 1
                    for rh in range(2):
                        mid[rh * 288 + o, 576 + 8 + 36 * rh + at + c] = 1
                elif wj < 3:
                    top[o, 80 * wj + 8 + 36 * ch + at + c1] = 1
                    for rh in range(2):
                        mid[rh * 288 + o, 144 * wj + 72 * rh + 36 * ch + at + c1] = 1
                else:
                    top[o, 240 + 4 + at + c1] = 1
                    for rh in range(2):
                        mid[rh * 288 + o, 432 + 36 * rh + at + c1] = 1
    return top, mid


def place_kernel(edge_ref, inner_ref, lat_ref, lon_ref, diag_ref, top_ref, mid_ref, out_ref):
    def put(k, rows):
        for lev in range(2):
            for rr in range(3):
                at = lev * 144 + rr * 48
                out_ref[0, lev, 3 * k + rr] = rows[at : at + 48].astype(BF16)

    first = jnp.concatenate([lat_ref[...], diag_ref[...]], axis=0)
    put(0, jnp.dot(top_ref[...], first, preferred_element_type=F32))
    for wi in range(4):
        if wi < 3:
            three = inner_ref[432 * wi : 432 * wi + 432]
            last = edge_ref[576 + 144 * wi : 720 + 144 * wi]
        else:
            three = edge_ref[0:432]
            last = edge_ref[432:576]
        stack = jnp.concatenate([three, last, lon_ref[80 * wi : 80 * wi + 80]], axis=0)
        both = 576 if wi < 3 else 288
        rows = jnp.dot(mid_ref[0:both], stack, preferred_element_type=F32)
        put(1 + 2 * wi, rows[0:288])
        if wi < 3:
            put(2 + 2 * wi, rows[288:576])


def to_grid(edge, inner, lat, lon, diag):
    top, mid = place_matrices()
    return pl.pallas_call(
        place_kernel,
        out_shape=jax.ShapeDtypeStruct((1, 2, 24, 48, D), BF16),
        name="to_grid",
        compiler_params=pltpu.CompilerParams(vmem_limit_bytes=20 * 2**20),
        cost_estimate=pl.CostEstimate(flops=3_000_000_000, bytes_accessed=8_000_000, transcendentals=0),
    )(edge, inner, lat, lon, diag, jnp.asarray(top, BF16), jnp.asarray(mid, BF16))


def widen(own, stage):
    return jnp.stack([own, *[stage(own, d) for d in (1, 2, 3)]])


def after(value, *others):
    return lax.optimization_barrier((value, *others))[0]


def body(fields, region, gain_attn, w_qkv, w_proj, gain_mlp, w_up, w_down):
    lat, lon = lax.axis_index("lat"), lax.axis_index("lon")
    mem = lax.axis_index("mem")
    pos = jnp.stack([(lon // 4) * 2 + mem // 2, lat, mem % 2]).astype(jnp.int32)

    down = w_down.T.reshape(4, 4, D).transpose(1, 0, 2).reshape(16, D)
    block = jnp.concatenate([w_qkv.T, w_proj.T, w_up.T, down], axis=0)
    line = widen(block, along_x)
    line = lax.dynamic_slice_in_dim(jnp.concatenate([line, line]), (4 - lon % 4) % 4, 4)
    stage = jnp.concatenate(
        [
            line[:, 0:12].reshape(48, D),
            line[:, 12:16].reshape(16, D),
            line[:, 16:32].reshape(64, D),
            line[:, 32:48].reshape(4, 4, 4, D).transpose(1, 0, 2, 3).reshape(64, D),
        ]
    )

    member = fields[0]
    levels, clat, clon, _ = member.shape
    row = lax.broadcasted_iota(jnp.int32, (clat, clon), 0)
    ids = (region * 2 + ((lat == 0) & (row < SH)).astype(jnp.int32)).astype(BF16)

    def payload(part, marks, top, left):
        marks = jnp.pad(marks, ((top, 32 - top - marks.shape[0]), (left, D - left - marks.shape[1])))
        return jnp.concatenate([part.reshape(-1, D), marks])

    rows = from_grid(payload(member[:, :SH], ids[:SH], clat, 0), 1, 0)
    cols = from_grid(payload(member[:, :, :8], ids[:, :8], 0, clon), 0, 1)
    both = from_grid(payload(member[:, :SH, :8], ids[:SH, :8], clat, clon), 1, 1)
    ids = jnp.pad(ids, ((0, 32 - clat), (0, 128 - clon)))

    firsts = [along_first(stage, d) for d in (1, 2, 3)]
    f, x, xq, bias = prep(member, rows, cols, both, ids, gain_attn.reshape(1, D))
    firsts = lax.optimization_barrier((*firsts, f))[:3]
    group = jnp.stack([p[0:48] for p in (stage, *firsts)])
    rest = jnp.stack([p[48:192] for p in (stage, *firsts)])
    qkv_mine = widen(group, along_second)
    qkv_pieces = [qkv_mine, other_core(qkv_mine)]
    rest = after(rest, qkv_mine)
    rest_mine = [rest, *[along_second(rest, d) for d in (1, 2, 3)]]
    mixed = attend(pos, x.reshape(-1, D), xq, bias, qkv_pieces).reshape(-1, D)
    late = lax.optimization_barrier((*rest_mine, mixed))[:4]
    rest_pieces = [*late, *[other_core(p) for p in late]]
    f = f.reshape(-1, D)
    gain = gain_mlp.reshape(1, D)
    edge = mlp(pos, mixed, f, gain, rest_pieces, 0, EDGE * TOK)
    win = edge.reshape(EDGE, TOK, D)
    lat_out = jnp.concatenate([win[0:3, 64:144].reshape(240, D), win[3, 32:112]])
    lon_out = jnp.concatenate([win[4:7, 64:144].reshape(240, D), win[3, 64:144]])
    diag_out = win[3, 96:144]
    lat_in = from_grid(lat_out, -1, 0)
    lon_in = from_grid(lon_out, 0, -1)
    diag_in = from_grid(diag_out, -1, -1)
    inner = mlp(pos, mixed, f, gain, rest_pieces, EDGE * TOK, INNER * TOK)
    return to_grid(edge, inner, lat_in, lon_in, diag_in)


def solution(mesh):
    weight = P(None, AXES)
    in_specs = (
        P("mem", None, "lat", "lon", None),
        P("lat", "lon"),
        P(),
        weight,
        weight,
        P(),
        weight,
        weight,
    )
    out_specs = P("mem", None, "lat", "lon", None)
    return jax.shard_map(body, mesh=mesh, in_specs=in_specs, out_specs=out_specs, check_vma=False)
```

time: 175 us -> 115 us (0.66); the launches traced: 172 us -> 114 us
  Pallas kernels: 98.4 us -> 51.6 us
  waiting for transfers between devices: 4.63 us -> 19.2 us
  starting transfers between devices: 42.7 us -> 31.1 us
  local copies, waits for them, and re-layouts: 16.8 us -> 9.59 us
  other arithmetic: 8.92 us -> 2.6 us
    pallas_call x5 -> x4, Pallas kernels: 92.9 us -> 48.2 us  [the longest x1 25 us: attend(): pl.pallas_call(attn_kernel, grid=(10,), in_specs=[pl.BlockSpec(memory_spa...]
    ppermute x23 -> x17, starting transfers between devices: 28.8 us -> 19.6 us  [send(): return lax.ppermute(block, AXES, pairs)]
    ppermute x23 -> x17, waiting for transfers between devices: 0.06 us -> 9.23 us  [send(): return lax.ppermute(block, AXES, pairs)]
    ppermute x9 -> x6, waiting for transfers between devices: 4.57 us -> 9.95 us  [from_grid(): return lax.ppermute(block, AXES, pairs)]
    slice x8 -> x6, local copies, waits for them, and re-layouts: 7.34 us -> 2.82 us  [the longest x1 1.02 us: body(): cols = from_grid(payload(member[:, :, :8], ids[:, :8], 0, clon), 0, 1)]
    concatenate x2 -> x4, other arithmetic: 4.14 us -> 0.2 us  [the longest x3 0.18 us: payload(): return jnp.concatenate([part.reshape(-1, D), marks])]
    another operation x3 -> x2, other arithmetic: 3.3 us -> 0.14 us  [widen(): return jnp.stack([own, *[stage(own, d) for d in (1, 2, 3)]])]
    ppermute x9 -> x6, starting transfers between devices: 13.9 us -> 11.6 us  [from_grid(): return lax.ppermute(block, AXES, pairs)]
  transfers between devices with their start and end apart: 32 -> 23, of which waited for: 1 -> 8; matrix products, arithmetic and copies ran while one was open for 11% -> 5% of each run, Pallas kernels for 47% -> 36%
where the time goes in v2:
time: 115 us; the launch traced here: 114 us
  Pallas kernels  51.6 us (45%)
  starting transfers between devices  31.1 us (27%)
  waiting for transfers between devices  19.2 us (17%)
  local copies, waits for them, and re-layouts  9.59 us (8%)
  other arithmetic  2.6 us (2%)
    pallas_call x1, Pallas kernels, attend(): pl.pallas_call(attn_kernel, grid=(10,), in_specs=[pl.BlockSpec(memory_spa...  25 us
    ppermute x17, starting transfers between devices, send(): return lax.ppermute(block, AXES, pairs)  19.6 us
    pallas_call x2, Pallas kernels, mlp(): pl.pallas_call(mlp_kernel, grid=(1,), in_specs=[pl.BlockSpec(memory_space...  15 us
    ppermute x6, starting transfers between devices, from_grid(): return lax.ppermute(block, AXES, pairs)  11.6 us
    ppermute x6, waiting for transfers between devices, from_grid(): return lax.ppermute(block, AXES, pairs)  9.95 us
    ppermute x17, waiting for transfers between devices, send(): return lax.ppermute(block, AXES, pairs)  9.23 us
    pallas_call x1, Pallas kernels, prep(): pl.pallas_call(prep_kernel, grid=(n // 4,), in_specs=[whole(a) for a in o...  8.26 us
    unnamed x28, local copies, waits for them, and re-layouts  5.15 us
  transfers between devices with their start and end apart: 23, of which 8 were waited for; matrix products, arithmetic and copies ran while one was open for 5% of the time, Pallas kernels for 36%

profile of v2, /device:TPU:1, one launch (start us, length us, event | category | flops | bytes accessed | tf_op | source)
XLA Modules:
  0.0 114.5 jit_solution(2952231280195238677)
XLA Ops:
  0.0 0.7 reshape.59
  0.8 0.8 bitcast_dynamic-update-slice_fusion.6
  1.5 3.4 %collective-permute-start.3 = (bf16[48,512]{1,0:T(8,128)(2,1)S(1)}, bf16[48,512]{1,0:T(8,128)(2,1)S(1)}, u32[]{:S(2)}, u32[]{:S(2)}) collective-permute-start(bf16[48,512]{1,0:T(8,128)(2,1)S(1)} %get-tuple-element.30), channel_id=1, source_target_pairs={{1,0},{2,1},{3,2},{0,3},{5,4},{6,5},{7,6},{4,7},{9,8},{10,9},{11,1... | collective-permute-start | bytes 147464 | tf_op jit(solution)/shard_map/ppermute | solution.py:40
  4.9 0.5 collective-permute-start.4
  5.4 0.6 collective-permute-start.5
  6.0 0.8 add_convert_fusion
  6.8 1.0 slice.86
  7.8 3.8 %collective-permute-start = (bf16[320,512]{1,0:T(8,128)(2,1)S(1)}, bf16[320,512]{1,0:T(8,128)(2,1)S(1)}, u32[]{:S(2)}, u32[]{:S(2)}) collective-permute-start(bf16[320,512]{1,0:T(8,128)(2,1)S(1)} %fusion.3), channel_id=1, source_target_pairs={{8,0},{9,1},{10,2},{11,3},{12,4},{13,5},{14,6},{15,7},{16,8},{17,9... | collective-permute-start | bytes 983048 | tf_op jit(solution)/shard_map/ppermute | solution.py:64
  11.7 1.0 slice.88
  12.8 4.7 %collective-permute-start.1 = (bf16[416,512]{1,0:T(8,128)(2,1)S(1)}, bf16[416,512]{1,0:T(8,128)(2,1)S(1)}, u32[]{:S(2)}, u32[]{:S(2)}) collective-permute-start(bf16[416,512]{1,0:T(8,128)(2,1)S(1)} %fusion.2), channel_id=1, source_target_pairs={{1,0},{2,1},{3,2},{4,3},{5,4},{6,5},{7,6},{0,7},{9,8},{10,9},{11,1... | collective-permute-start | bytes 1277960 | tf_op jit(solution)/shard_map/ppermute | solution.py:64
  17.5 0.8 slice.90
  18.4 0.6 pad.19.ids_ref
  19.3 0.2 collective-permute-start.6
  19.5 2.9 %collective-permute-start.7 = (bf16[192,512]{1,0:T(8,128)(2,1)S(1)}, bf16[192,512]{1,0:T(8,128)(2,1)S(1)}, u32[]{:S(2)}, u32[]{:S(2)}) collective-permute-start(bf16[192,512]{1,0:T(8,128)(2,1)S(1)} %pad_maximum_fusion.4), channel_id=1, source_target_pairs={{4,0},{5,1},{6,2},{7,3},{0,4},{1,5},{2,6},{3,7},{12,8},{13,9},{14,... | collective-permute-start | bytes 589832 | tf_op jit(solution)/shard_map/ppermute | solution.py:40
  22.4 4.2 %collective-permute-done.2.both_ref = bf16[80,512]{1,0:T(8,128)(2,1)S(1)} collective-permute-done((bf16[80,512]{1,0:T(8,128)(2,1)S(1)}, bf16[80,512]{1,0:T(8,128)(2,1)S(1)}, u32[]{:S(2)}, u32[]{:S(2)}) %collective-permute-start.2) | collective-permute-done | bytes 81952 | tf_op jit(solution)/shard_map/ppermute | solution.py:64
  26.7 0.6 copy-done.10
  27.3 0.1 copy-done.9
  27.4 0.1 copy-done.8
  27.6 8.3 %prep.1 = (bf16[16,144,512]{2,1,0:T(8,128)(2,1)}, bf16[16,144,512]{2,1,0:T(8,128)(2,1)}, bf16[16,256,512]{2,1,0:T(8,128)(2,1)}, bf16[16,144,256]{2,1,0:T(8,128)(2,1)}) custom-call(bf16[2,24,48,512]{3,2,1,0:T(8,128)(2,1)} %bitcast.81, bf16[320,512]{1,0:T(8,128)(2,1)} %copy-done.9, bf16[416,512]{1,0:T(8,128)(2,1)} %copy-done.8, bf16[80,512]{1,0:T(8,128)(2,1)} %copy-done.10, ...), custom_call_target="tpu_custom_call" | custom-call | flops 6000000000 | bytes 16000000 | tf_op jit(solution)/shard_map/prep/pallas_call | solution.py:137
  35.9 0.5 collective-permute-start.11
  36.4 1.5 %collective-permute-start.10 = (bf16[4,48,512]{2,1,0:T(8,128)(2,1)S(1)}, bf16[4,48,512]{2,1,0:T(8,128)(2,1)S(1)}, u32[]{:S(2)}, u32[]{:S(2)}) collective-permute-start(bf16[4,48,512]{2,1,0:T(8,128)(2,1)S(1)} %get-tuple-element.38), channel_id=1, source_target_pairs={{16,0},{17,1},{18,2},{19,3},{20,4},{21,5},{22,6},{23,7},{24,8},{25... | collective-permute-start | bytes 589832 | tf_op jit(solution)/shard_map/ppermute | solution.py:40
  38.0 1.0 collective-permute-start.9
  38.9 5.2 %collective-permute-done.11 = bf16[4,48,512]{2,1,0:T(8,128)(2,1)S(1)} collective-permute-done((bf16[4,48,512]{2,1,0:T(8,128)(2,1)S(1)}, bf16[4,48,512]{2,1,0:T(8,128)(2,1)S(1)}, u32[]{:S(2)}, u32[]{:S(2)}) %collective-permute-start.11) | collective-permute-done | bytes 196640 | tf_op jit(solution)/shard_map/ppermute | solution.py:40
  44.1 0.6 collective-permute-done.9
  44.8 0.1 pad_maximum_fusion.refs_0_
  44.9 4.6 %collective-permute-start.12 = (bf16[4,4,48,512]{3,2,1,0:T(8,128)(2,1)S(1)}, bf16[4,4,48,512]{3,2,1,0:T(8,128)(2,1)S(1)}, u32[]{:S(2)}, u32[]{:S(2)}) collective-permute-start(bf16[4,4,48,512]{3,2,1,0:T(8,128)(2,1)S(1)} %pad_maximum_fusion.refs_0_), channel_id=1, source_target_pairs={{32,0},{33,1},{34,2},{35,3},{36,4},{37,5},{38,6},{39,7},{40,8},{41... | collective-permute-start | bytes 2359304 | tf_op jit(solution)/shard_map/ppermute | solution.py:40
  49.4 0.6 pad_add_fusion.pos_ref
  50.2 2.3 %collective-permute-start.13 = (bf16[4,144,512]{2,1,0:T(8,128)(2,1)S(1)}, bf16[4,144,512]{2,1,0:T(8,128)(2,1)S(1)}, u32[]{:S(2)}, u32[]{:S(2)}) collective-permute-start(bf16[4,144,512]{2,1,0:T(8,128)(2,1)S(1)} %pad_maximum_fusion.1.refs_0_), channel_id=1, source_target_pairs={{8,0},{9,1},{10,2},{11,3},{12,4},{13,5},{14,6},{15,7},{16,8},{17,9... | collective-permute-start | bytes 1769480 | tf_op jit(solution)/shard_map/ppermute | solution.py:40
  52.5 0.7 collective-permute-start.15
  53.1 0.9 copy-done.7
  54.0 25.0 %attend.1 = bf16[16,144,512]{2,1,0:T(8,128)(2,1)} custom-call(s32[3]{0:T(128)} %pad_add_fusion.pos_ref, bf16[2304,512]{1,0:T(8,128)(2,1)} %bitcast.93, bf16[16,256,512]{2,1,0:T(8,128)(2,1)} %get-tuple-element.18.xq_a.xq_b.xv_a.xv_b, bf16[16,256,512]{2,1,0:T(8,128)(2,1)} %get-tuple-element.18.xq_a.xq_b.xv_a.xv_b, ...), custom_call_target="tpu_custom_call" | custom-call | flops 20000000000 | bytes 12000000 | tf_op jit(solution)/shard_map/attend/pallas_call | solution.py:250
  79.1 0.7 collective-permute-start.16
  79.8 0.3 collective-permute-start.17
  80.1 0.2 collective-permute-start.18
  80.3 0.3 collective-permute-start.19
  80.6 0.8 collective-permute-done.16.refs_4_
  81.4 0.8 collective-permute-done.17.refs_5_
  82.3 0.8 collective-permute-done.18.refs_6_
  83.1 0.8 collective-permute-done.19.refs_7_
  84.0 1.7 %copy-done.2 = bf16[16,144,512]{2,1,0:T(8,128)(2,1)S(1)} copy-done((bf16[16,144,512]{2,1,0:T(8,128)(2,1)S(1)}, bf16[16,144,512]{2,1,0:T(8,128)(2,1)}, u32[]{:S(2)}) %copy-start.2) | copy-done | bytes 2359320
  85.6 1.7 %copy-done.3 = bf16[16,144,512]{2,1,0:T(8,128)(2,1)S(1)} copy-done((bf16[16,144,512]{2,1,0:T(8,128)(2,1)S(1)}, bf16[16,144,512]{2,1,0:T(8,128)(2,1)}, u32[]{:S(2)}) %copy-start.3) | copy-done | bytes 2359320
  87.3 6.7 %mlp_0.1.edge_ref = bf16[1008,512]{1,0:T(8,128)(2,1)S(1)} custom-call(s32[3]{0:T(128)S(1)} %copy-done, bf16[2304,512]{1,0:T(8,128)(2,1)S(1)} %bitcast.69, bf16[2304,512]{1,0:T(8,128)(2,1)S(1)} %bitcast.67, f32[1,512]{1,0:T(1,128)S(1)} %bitcast.65, bf16[4,144,512]{2,1,0:T(8,128)(2,1)S(1)} %pad_maximum_fusion.1.refs_0_, ...), custom_call_target="tpu_custom_call" | custom-call | flops 5040000000 | bytes 8096576 | tf_op jit(solution)/shard_map/mlp_0/pallas_call | solution.py:323
  94.1 2.3 %collective-permute-start.20 = (bf16[320,512]{1,0:T(8,128)(2,1)S(1)}, bf16[320,512]{1,0:T(8,128)(2,1)S(1)}, u32[]{:S(2)}, u32[]{:S(2)}) collective-permute-start(bf16[320,512]{1,0:T(8,128)(2,1)S(1)} %pad_maximum_fusion.2), channel_id=1, source_target_pairs={{24,0},{25,1},{26,2},{27,3},{28,4},{29,5},{30,6},{31,7},{0,8},{1,9... | collective-permute-start | bytes 983048 | tf_op jit(solution)/shard_map/ppermute | solution.py:64
  96.5 0.5 collective-permute-start.21
  96.9 0.2 collective-permute-start.22
  97.2 8.2 %mlp_1008.1.inner_ref = bf16[1296,512]{1,0:T(8,128)(2,1)S(1)} custom-call(s32[3]{0:T(128)S(1)} %copy-done, bf16[2304,512]{1,0:T(8,128)(2,1)S(1)} %bitcast.70, bf16[2304,512]{1,0:T(8,128)(2,1)S(1)} %bitcast.68, f32[1,512]{1,0:T(1,128)S(1)} %bitcast.66, bf16[4,144,512]{2,1,0:T(8,128)(2,1)S(1)} %pad_maximum_fusion.1.refs_0_, ...), custom_call_target="tpu_custom_call" | custom-call | flops 6480000000 | bytes 8981312 | tf_op jit(solution)/shard_map/mlp_1008/pallas_call | solution.py:323
  105.4 5.7 %collective-permute-done.22.diag_ref = bf16[48,512]{1,0:T(8,128)(2,1)S(1)} collective-permute-done((bf16[48,512]{1,0:T(8,128)(2,1)S(1)}, bf16[48,512]{1,0:T(8,128)(2,1)S(1)}, u32[]{:S(2)}, u32[]{:S(2)}) %collective-permute-start.22) | collective-permute-done | bytes 49184 | tf_op jit(solution)/shard_map/ppermute | solution.py:64
  111.1 3.3 %to_grid.1 = bf16[1,2,24,48,512]{4,3,2,1,0:T(8,128)(2,1)} custom-call(bf16[1008,512]{1,0:T(8,128)(2,1)S(1)} %mlp_0.1.edge_ref, bf16[1296,512]{1,0:T(8,128)(2,1)S(1)} %mlp_1008.1.inner_ref, bf16[320,512]{1,0:T(8,128)(2,1)S(1)} %collective-permute-done.20.lat_ref, bf16[320,512]{1,0:T(8,128)(2,1)S(1)} %collective-permute-done.21.lon_ref, ...), custom_call_target="tpu_custom_call" | custom-call | flops 3000000000 | bytes 8000000 | tf_op jit(solution)/shard_map/to_grid/pallas_call | solution.py:401
  (71 shorter events, 0.8 us)
Async XLA Ops:
  1.5 17.4 %collective-permute-start.3 = (bf16[48,512]{1,0:T(8,128)(2,1)S(1)}, bf16[48,512]{1,0:T(8,128)(2,1)S(1)}, u32[]{:S(2)}, u32[]{:S(2)}) collective-permute-start(bf16[48,512]{1,0:T(8,128)(2,1)S(1)} %get-tuple-element.30), channel_id=1, source_target_pairs={{1,0},{2,1},{3,2},{0,3},{5,4},{6,5},{7,6},{4,7},{9,8},{10,9},{11,1... | collective-permute-start | bytes 147464 | tf_op jit(solution)/shard_map/ppermute | solution.py:40
  4.9 14.1 %collective-permute-start.4 = (bf16[48,512]{1,0:T(8,128)(2,1)S(1)}, bf16[48,512]{1,0:T(8,128)(2,1)S(1)}, u32[]{:S(2)}, u32[]{:S(2)}) collective-permute-start(bf16[48,512]{1,0:T(8,128)(2,1)S(1)} %get-tuple-element.30), channel_id=1, source_target_pairs={{2,0},{3,1},{0,2},{1,3},{6,4},{7,5},{4,6},{5,7},{10,8},{11,9},{8,1... | collective-permute-start | bytes 147464 | tf_op jit(solution)/shard_map/ppermute | solution.py:40
  5.4 13.6 %collective-permute-start.5 = (bf16[48,512]{1,0:T(8,128)(2,1)S(1)}, bf16[48,512]{1,0:T(8,128)(2,1)S(1)}, u32[]{:S(2)}, u32[]{:S(2)}) collective-permute-start(bf16[48,512]{1,0:T(8,128)(2,1)S(1)} %get-tuple-element.30), channel_id=1, source_target_pairs={{3,0},{0,1},{1,2},{2,3},{7,4},{4,5},{5,6},{6,7},{11,8},{8,9},{9,10... | collective-permute-start | bytes 147464 | tf_op jit(solution)/shard_map/ppermute | solution.py:40
  7.8 18.8 %collective-permute-start = (bf16[320,512]{1,0:T(8,128)(2,1)S(1)}, bf16[320,512]{1,0:T(8,128)(2,1)S(1)}, u32[]{:S(2)}, u32[]{:S(2)}) collective-permute-start(bf16[320,512]{1,0:T(8,128)(2,1)S(1)} %fusion.3), channel_id=1, source_target_pairs={{8,0},{9,1},{10,2},{11,3},{12,4},{13,5},{14,6},{15,7},{16,8},{17,9... | collective-permute-start | bytes 983048 | tf_op jit(solution)/shard_map/ppermute | solution.py:64
  12.8 13.9 %collective-permute-start.1 = (bf16[416,512]{1,0:T(8,128)(2,1)S(1)}, bf16[416,512]{1,0:T(8,128)(2,1)S(1)}, u32[]{:S(2)}, u32[]{:S(2)}) collective-permute-start(bf16[416,512]{1,0:T(8,128)(2,1)S(1)} %fusion.2), channel_id=1, source_target_pairs={{1,0},{2,1},{3,2},{4,3},{5,4},{6,5},{7,6},{0,7},{9,8},{10,9},{11,1... | collective-permute-start | bytes 1277960 | tf_op jit(solution)/shard_map/ppermute | solution.py:64
  19.0 7.7 %collective-permute-start.2 = (bf16[80,512]{1,0:T(8,128)(2,1)S(1)}, bf16[80,512]{1,0:T(8,128)(2,1)S(1)}, u32[]{:S(2)}, u32[]{:S(2)}) collective-permute-start(bf16[80,512]{1,0:T(8,128)(2,1)S(1)} %fusion.5), channel_id=1, source_target_pairs={{9,0},{10,1},{11,2},{12,3},{13,4},{14,5},{15,6},{8,7},{17,8},{18,9... | collective-permute-start | bytes 245768 | tf_op jit(solution)/shard_map/ppermute | solution.py:64
  19.3 16.5 %collective-permute-start.6 = (bf16[192,512]{1,0:T(8,128)(2,1)S(1)}, bf16[192,512]{1,0:T(8,128)(2,1)S(1)}, u32[]{:S(2)}, u32[]{:S(2)}) collective-permute-start(bf16[192,512]{1,0:T(8,128)(2,1)S(1)} %pad_maximum_fusion.4), channel_id=1, source_target_pairs={{64,0},{65,1},{66,2},{67,3},{68,4},{69,5},{70,6},{71,7},{72,8},{73... | collective-permute-start | bytes 589832 | tf_op jit(solution)/shard_map/ppermute | solution.py:40
  19.5 16.3 %collective-permute-start.7 = (bf16[192,512]{1,0:T(8,128)(2,1)S(1)}, bf16[192,512]{1,0:T(8,128)(2,1)S(1)}, u32[]{:S(2)}, u32[]{:S(2)}) collective-permute-start(bf16[192,512]{1,0:T(8,128)(2,1)S(1)} %pad_maximum_fusion.4), channel_id=1, source_target_pairs={{4,0},{5,1},{6,2},{7,3},{0,4},{1,5},{2,6},{3,7},{12,8},{13,9},{14,... | collective-permute-start | bytes 589832 | tf_op jit(solution)/shard_map/ppermute | solution.py:40
  26.7 0.6 copy-start.10
  26.7 9.2 %collective-permute-start.8 = (bf16[192,512]{1,0:T(8,128)(2,1)S(1)}, bf16[192,512]{1,0:T(8,128)(2,1)S(1)}, u32[]{:S(2)}, u32[]{:S(2)}) collective-permute-start(bf16[192,512]{1,0:T(8,128)(2,1)S(1)} %pad_maximum_fusion.4), channel_id=1, source_target_pairs={{68,0},{69,1},{70,2},{71,3},{64,4},{65,5},{66,6},{67,7},{76,8},{77... | collective-permute-start | bytes 589832 | tf_op jit(solution)/shard_map/ppermute | solution.py:40
  26.7 0.8 copy-start.9
  26.7 0.9 copy-start.8
  35.9 8.2 %collective-permute-start.11 = (bf16[4,48,512]{2,1,0:T(8,128)(2,1)S(1)}, bf16[4,48,512]{2,1,0:T(8,128)(2,1)S(1)}, u32[]{:S(2)}, u32[]{:S(2)}) collective-permute-start(bf16[4,48,512]{2,1,0:T(8,128)(2,1)S(1)} %get-tuple-element.38), channel_id=1, source_target_pairs={{24,0},{25,1},{26,2},{27,3},{28,4},{29,5},{30,6},{31,7},{0,8},{1,9... | collective-permute-start | bytes 589832 | tf_op jit(solution)/shard_map/ppermute | solution.py:40
  36.4 7.7 %collective-permute-start.10 = (bf16[4,48,512]{2,1,0:T(8,128)(2,1)S(1)}, bf16[4,48,512]{2,1,0:T(8,128)(2,1)S(1)}, u32[]{:S(2)}, u32[]{:S(2)}) collective-permute-start(bf16[4,48,512]{2,1,0:T(8,128)(2,1)S(1)} %get-tuple-element.38), channel_id=1, source_target_pairs={{16,0},{17,1},{18,2},{19,3},{20,4},{21,5},{22,6},{23,7},{24,8},{25... | collective-permute-start | bytes 589832 | tf_op jit(solution)/shard_map/ppermute | solution.py:40
  38.0 6.8 %collective-permute-start.9 = (bf16[4,48,512]{2,1,0:T(8,128)(2,1)S(1)}, bf16[4,48,512]{2,1,0:T(8,128)(2,1)S(1)}, u32[]{:S(2)}, u32[]{:S(2)}) collective-permute-start(bf16[4,48,512]{2,1,0:T(8,128)(2,1)S(1)} %get-tuple-element.38), channel_id=1, source_target_pairs={{8,0},{9,1},{10,2},{11,3},{12,4},{13,5},{14,6},{15,7},{16,8},{17,9... | collective-permute-start | bytes 589832 | tf_op jit(solution)/shard_map/ppermute | solution.py:40
  44.9 9.2 %copy-start.6 = (bf16[4,4,48,512]{3,2,1,0:T(8,128)(2,1)}, bf16[4,4,48,512]{3,2,1,0:T(8,128)(2,1)S(1)}, u32[]{:S(2)}) copy-start(bf16[4,4,48,512]{3,2,1,0:T(8,128)(2,1)S(1)} %pad_maximum_fusion.refs_0_) | copy-start | bytes 2359300
  44.9 8.3 %collective-permute-start.12 = (bf16[4,4,48,512]{3,2,1,0:T(8,128)(2,1)S(1)}, bf16[4,4,48,512]{3,2,1,0:T(8,128)(2,1)S(1)}, u32[]{:S(2)}, u32[]{:S(2)}) collective-permute-start(bf16[4,4,48,512]{3,2,1,0:T(8,128)(2,1)S(1)} %pad_maximum_fusion.refs_0_), channel_id=1, source_target_pairs={{32,0},{33,1},{34,2},{35,3},{36,4},{37,5},{38,6},{39,7},{40,8},{41... | collective-permute-start | bytes 2359304 | tf_op jit(solution)/shard_map/ppermute | solution.py:40
  50.2 28.9 %collective-permute-start.13 = (bf16[4,144,512]{2,1,0:T(8,128)(2,1)S(1)}, bf16[4,144,512]{2,1,0:T(8,128)(2,1)S(1)}, u32[]{:S(2)}, u32[]{:S(2)}) collective-permute-start(bf16[4,144,512]{2,1,0:T(8,128)(2,1)S(1)} %pad_maximum_fusion.1.refs_0_), channel_id=1, source_target_pairs={{8,0},{9,1},{10,2},{11,3},{12,4},{13,5},{14,6},{15,7},{16,8},{17,9... | collective-permute-start | bytes 1769480 | tf_op jit(solution)/shard_map/ppermute | solution.py:40
  52.5 26.6 %collective-permute-start.14 = (bf16[4,144,512]{2,1,0:T(8,128)(2,1)S(1)}, bf16[4,144,512]{2,1,0:T(8,128)(2,1)S(1)}, u32[]{:S(2)}, u32[]{:S(2)}) collective-permute-start(bf16[4,144,512]{2,1,0:T(8,128)(2,1)S(1)} %pad_maximum_fusion.1.refs_0_), channel_id=1, source_target_pairs={{16,0},{17,1},{18,2},{19,3},{20,4},{21,5},{22,6},{23,7},{24,8},{25... | collective-permute-start | bytes 1769480 | tf_op jit(solution)/shard_map/ppermute | solution.py:40
  52.5 26.6 %collective-permute-start.15 = (bf16[4,144,512]{2,1,0:T(8,128)(2,1)S(1)}, bf16[4,144,512]{2,1,0:T(8,128)(2,1)S(1)}, u32[]{:S(2)}, u32[]{:S(2)}) collective-permute-start(bf16[4,144,512]{2,1,0:T(8,128)(2,1)S(1)} %pad_maximum_fusion.1.refs_0_), channel_id=1, source_target_pairs={{24,0},{25,1},{26,2},{27,3},{28,4},{29,5},{30,6},{31,7},{0,8},{1,9... | collective-permute-start | bytes 1769480 | tf_op jit(solution)/shard_map/ppermute | solution.py:40
  53.1 0.9 copy-start.7
  54.0 29.9 %copy-start = (s32[3]{0:T(128)S(1)}, s32[3]{0:T(128)}, u32[]{:S(2)}) copy-start(s32[3]{0:T(128)} %pad_add_fusion.pos_ref) | copy-start | bytes 40
  54.0 29.9 %copy-start.1 = (f32[512]{0:T(512)S(1)}, f32[512]{0:T(512)}, u32[]{:S(2)}) copy-start(f32[512]{0:T(512)} %param.15) | copy-start | bytes 6148
  79.1 2.3 %collective-permute-start.16 = (bf16[4,144,512]{2,1,0:T(8,128)(2,1)S(1)}, bf16[4,144,512]{2,1,0:T(8,128)(2,1)S(1)}, u32[]{:S(2)}, u32[]{:S(2)}) collective-permute-start(bf16[4,144,512]{2,1,0:T(8,128)(2,1)S(1)} %pad_maximum_fusion.1.refs_0_), channel_id=1, source_target_pairs={{32,0},{33,1},{34,2},{35,3},{36,4},{37,5},{38,6},{39,7},{40,8},{41... | collective-permute-start | bytes 1769480 | tf_op jit(solution)/shard_map/ppermute | solution.py:40
  79.8 2.5 %collective-permute-start.17 = (bf16[4,144,512]{2,1,0:T(8,128)(2,1)S(1)}, bf16[4,144,512]{2,1,0:T(8,128)(2,1)S(1)}, u32[]{:S(2)}, u32[]{:S(2)}) collective-permute-start(bf16[4,144,512]{2,1,0:T(8,128)(2,1)S(1)} %collective-permute-done.13.refs_1_), channel_id=1, source_target_pairs={{32,0},{33,1},{34,2},{35,3},{36,4},{37,5},{38,6},{39,7},{40,8},{41... | collective-permute-start | bytes 1769480 | tf_op jit(solution)/shard_map/ppermute | solution.py:40
  80.1 3.0 %collective-permute-start.18 = (bf16[4,144,512]{2,1,0:T(8,128)(2,1)S(1)}, bf16[4,144,512]{2,1,0:T(8,128)(2,1)S(1)}, u32[]{:S(2)}, u32[]{:S(2)}) collective-permute-start(bf16[4,144,512]{2,1,0:T(8,128)(2,1)S(1)} %collective-permute-done.14.refs_2_), channel_id=1, source_target_pairs={{32,0},{33,1},{34,2},{35,3},{36,4},{37,5},{38,6},{39,7},{40,8},{41... | collective-permute-start | bytes 1769480 | tf_op jit(solution)/shard_map/ppermute | solution.py:40
  80.3 3.6 %collective-permute-start.19 = (bf16[4,144,512]{2,1,0:T(8,128)(2,1)S(1)}, bf16[4,144,512]{2,1,0:T(8,128)(2,1)S(1)}, u32[]{:S(2)}, u32[]{:S(2)}) collective-permute-start(bf16[4,144,512]{2,1,0:T(8,128)(2,1)S(1)} %collective-permute-done.15.refs_3_), channel_id=1, source_target_pairs={{32,0},{33,1},{34,2},{35,3},{36,4},{37,5},{38,6},{39,7},{40,8},{41... | collective-permute-start | bytes 1769480 | tf_op jit(solution)/shard_map/ppermute | solution.py:40
  84.0 1.7 %copy-start.2 = (bf16[16,144,512]{2,1,0:T(8,128)(2,1)S(1)}, bf16[16,144,512]{2,1,0:T(8,128)(2,1)}, u32[]{:S(2)}) copy-start(bf16[16,144,512]{2,1,0:T(8,128)(2,1)} %get-tuple-element.20) | copy-start | bytes 7077892
  85.6 1.7 %copy-start.3 = (bf16[16,144,512]{2,1,0:T(8,128)(2,1)S(1)}, bf16[16,144,512]{2,1,0:T(8,128)(2,1)}, u32[]{:S(2)}) copy-start(bf16[16,144,512]{2,1,0:T(8,128)(2,1)} %attend.1) | copy-start | bytes 7077892
  94.1 17.0 %collective-permute-start.20 = (bf16[320,512]{1,0:T(8,128)(2,1)S(1)}, bf16[320,512]{1,0:T(8,128)(2,1)S(1)}, u32[]{:S(2)}, u32[]{:S(2)}) collective-permute-start(bf16[320,512]{1,0:T(8,128)(2,1)S(1)} %pad_maximum_fusion.2), channel_id=1, source_target_pairs={{24,0},{25,1},{26,2},{27,3},{28,4},{29,5},{30,6},{31,7},{0,8},{1,9... | collective-permute-start | bytes 983048 | tf_op jit(solution)/shard_map/ppermute | solution.py:64
  96.5 14.7 %copy-start.4 = (bf16[576,656]{1,0:T(8,128)(2,1)S(1)}, bf16[576,656]{1,0:T(8,128)(2,1)}, u32[]{:S(2)}) copy-start(bf16[576,656]{1,0:T(8,128)(2,1)} %constant.70.clone.mid_ref) | copy-start | bytes 2267140
  96.5 14.6 %copy-start.5 = (bf16[288,368]{1,0:T(8,128)(2,1)S(1)}, bf16[288,368]{1,0:T(8,128)(2,1)}, u32[]{:S(2)}) copy-start(bf16[288,368]{1,0:T(8,128)(2,1)} %constant.69.clone.top_ref) | copy-start | bytes 635908
  96.5 14.6 %collective-permute-start.21 = (bf16[320,512]{1,0:T(8,128)(2,1)S(1)}, bf16[320,512]{1,0:T(8,128)(2,1)S(1)}, u32[]{:S(2)}, u32[]{:S(2)}) collective-permute-start(bf16[320,512]{1,0:T(8,128)(2,1)S(1)} %pad_maximum_fusion.3), channel_id=1, source_target_pairs={{7,0},{0,1},{1,2},{2,3},{3,4},{4,5},{5,6},{6,7},{15,8},{8,9},{9,10... | collective-permute-start | bytes 983048 | tf_op jit(solution)/shard_map/ppermute | solution.py:64
  96.9 14.2 %collective-permute-start.22 = (bf16[48,512]{1,0:T(8,128)(2,1)S(1)}, bf16[48,512]{1,0:T(8,128)(2,1)S(1)}, u32[]{:S(2)}, u32[]{:S(2)}) collective-permute-start(bf16[48,512]{1,0:T(8,128)(2,1)S(1)} %slice_bitcast_fusion.5), channel_id=1, source_target_pairs={{31,0},{24,1},{25,2},{26,3},{27,4},{28,5},{29,6},{30,7},{7,8},{0,9... | collective-permute-start | bytes 147464 | tf_op jit(solution)/shard_map/ppermute | solution.py:64

commit v3 on v2

--- a/solution.py
+++ b/solution.py
@@ -1,4 +1,3 @@
-import functools
 import math
 
 import jax
@@ -8,6 +7,7 @@
 from jax.experimental import pallas as pl
 from jax.experimental.pallas import tpu as pltpu
 from jax.sharding import PartitionSpec as P
+
 
 D = 512
 HDIM = 32
@@ -156,6 +156,15 @@
     return (y % 2) * 16 + core * 8 + z * 2 + y // 2
 
 
+def rest_rows(pos_ref, side, d2, d3):
+    mine = pos_ref[2]
+    dy = jnp.where(mine == 0, d2, d3)
+    dz = jnp.where(mine == 0, d3, d2)
+    y = (pos_ref[0] + dy) % 4
+    z = (pos_ref[1] + dz) % 4
+    return (y % 2) * 16 + (mine if side == 0 else 1 - mine) * 8 + z * 2 + y // 2
+
+
 def attn_kernel(pos_ref, x_ref, xq_a, xq_b, xv_a, xv_b, bias_ref, *refs):
     pieces, out_ref = refs[:2], refs[2]
     w, kall, own = refs[3:6]
@@ -242,6 +251,10 @@
 
     half(1, 2 * i - 1, xq_a, xv_a)
     half(0, 2 * i, xq_b, xv_b)
+
+
+def far(array):
+    return pltpu.with_memory_space_constraint(array, pltpu.HBM)
 
 
 def attend(pos, x, xq, bias, pieces):
@@ -272,20 +285,21 @@
             *[pltpu.VMEM((D, 256), F32)] * 2,
         ],
         name="attend",
+        compiler_params=pltpu.CompilerParams(vmem_limit_bytes=36 * 2**20),
         cost_estimate=pl.CostEstimate(flops=20_000_000_000, bytes_accessed=12_000_000, transcendentals=5_000_000),
-    )(pos, x, xq, xq, xq, xq, bias, *pieces)
+    )(pos, far(x), *[far(xq)] * 4, far(bias), *pieces)
 
 
 def mlp_kernel(pos_ref, mixed_ref, f_ref, gain_ref, *refs):
-    pieces, out_ref, (wp, wu, wd, held, normed) = refs[:8], refs[8], refs[9:]
+    pieces, out_ref, sent, (wp, wu, wd, held, normed) = refs[:4], refs[4], refs[5:-5], refs[-5:]
 
     @pl.when(pl.program_id(0) == 0)
     def _():
         for d3 in range(4):
             for d2 in range(4):
                 for side in range(2):
-                    b = block_rows(pos_ref, side, d2, d3)
-                    piece = pieces[4 * side + d3].at[d2]
+                    b = rest_rows(pos_ref, side, d2, d3)
+                    piece = pieces[d3].at[d2, side]
                     wp[pl.ds(pl.multiple_of(b * 16, 16), 16), :] = piece[0:16]
                     wu[pl.ds(pl.multiple_of(b * 64, 16), 64), :] = piece[16:80]
                     for c in range(4):
@@ -315,9 +329,18 @@
     first(1)
     second(0)
     second(1)
-
-
-def mlp(pos, mixed, f, gain, pieces, first, rows):
+    if sent:
+        lat_ref, lon_ref, diag_ref = sent
+        corner = 3 * TOK
+        for n in range(3):
+            lat_ref[80 * n : 80 * n + 80] = out_ref[TOK * n + 64 : TOK * n + 144]
+            lon_ref[80 * n : 80 * n + 80] = out_ref[TOK * n + 4 * TOK + 64 : TOK * n + 5 * TOK]
+        lat_ref[240:320] = out_ref[corner + 32 : corner + 112]
+        lon_ref[240:320] = out_ref[corner + 64 : corner + 144]
+        diag_ref[...] = out_ref[corner + 96 : corner + 144]
+
+
+def mlp(pos, mixed, f, gain, pieces, first, rows, sent=()):
     run = pl.BlockSpec((pl.Element(rows), pl.Element(D)), lambda i: (first, 0), pipeline_mode=pl.Buffered(1))
     whole = lambda a: pl.BlockSpec(a.shape, lambda i: (0,) * a.ndim, pipeline_mode=pl.Buffered(1))
     return pl.pallas_call(
@@ -330,8 +353,8 @@
             whole(gain),
             *[whole(p) for p in pieces],
         ],
-        out_specs=pl.BlockSpec((rows, D), lambda i: (0, 0)),
-        out_shape=jax.ShapeDtypeStruct((rows, D), BF16),
+        out_specs=[pl.BlockSpec((n, D), lambda i: (0, 0)) for n in (rows, *sent)],
+        out_shape=[jax.ShapeDtypeStruct((n, D), BF16) for n in (rows, *sent)],
         scratch_shapes=[
             pltpu.VMEM((D, D), BF16),
             pltpu.VMEM((FF, D), BF16),
@@ -339,7 +362,6 @@
             pltpu.VMEM((rows, D), BF16),
             pltpu.VMEM((rows, D), BF16),
         ],
-        name=f"mlp_{first}",
         compiler_params=pltpu.CompilerParams(vmem_limit_bytes=26 * 2**20),
         cost_estimate=pl.CostEstimate(
             flops=rows * 5_000_000, bytes_accessed=rows * 3072 + 5_000_000, transcendentals=rows * 2048
@@ -411,10 +433,6 @@
     return jnp.stack([own, *[stage(own, d) for d in (1, 2, 3)]])
 
 
-def after(value, *others):
-    return lax.optimization_barrier((value, *others))[0]
-
-
 def body(fields, region, gain_attn, w_qkv, w_proj, gain_mlp, w_up, w_down):
     lat, lon = lax.axis_index("lat"), lax.axis_index("lon")
     mem = lax.axis_index("mem")
@@ -434,7 +452,7 @@
     )
 
     member = fields[0]
-    levels, clat, clon, _ = member.shape
+    _, clat, clon, _ = member.shape
     row = lax.broadcasted_iota(jnp.int32, (clat, clon), 0)
     ids = (region * 2 + ((lat == 0) & (row < SH)).astype(jnp.int32)).astype(BF16)
 
@@ -447,29 +465,25 @@
     both = from_grid(payload(member[:, :SH, :8], ids[:SH, :8], clat, clon), 1, 1)
     ids = jnp.pad(ids, ((0, 32 - clat), (0, 128 - clon)))
 
+    stage = jnp.concatenate([stage, other_core(stage[48:192])])
     firsts = [along_first(stage, d) for d in (1, 2, 3)]
     f, x, xq, bias = prep(member, rows, cols, both, ids, gain_attn.reshape(1, D))
     firsts = lax.optimization_barrier((*firsts, f))[:3]
     group = jnp.stack([p[0:48] for p in (stage, *firsts)])
-    rest = jnp.stack([p[48:192] for p in (stage, *firsts)])
-    qkv_mine = widen(group, along_second)
+    rest = jnp.stack([p[48:336].reshape(2, 144, D) for p in (stage, *firsts)])
+    qkv_sent = [along_second(group, d) for d in (1, 2, 3)]
+    qkv_mine = jnp.stack([group, *qkv_sent])
     qkv_pieces = [qkv_mine, other_core(qkv_mine)]
-    rest = after(rest, qkv_mine)
     rest_mine = [rest, *[along_second(rest, d) for d in (1, 2, 3)]]
     mixed = attend(pos, x.reshape(-1, D), xq, bias, qkv_pieces).reshape(-1, D)
-    late = lax.optimization_barrier((*rest_mine, mixed))[:4]
-    rest_pieces = [*late, *[other_core(p) for p in late]]
+    rest_pieces = lax.optimization_barrier((*rest_mine, mixed))[:4]
     f = f.reshape(-1, D)
     gain = gain_mlp.reshape(1, D)
-    edge = mlp(pos, mixed, f, gain, rest_pieces, 0, EDGE * TOK)
-    win = edge.reshape(EDGE, TOK, D)
-    lat_out = jnp.concatenate([win[0:3, 64:144].reshape(240, D), win[3, 32:112]])
-    lon_out = jnp.concatenate([win[4:7, 64:144].reshape(240, D), win[3, 64:144]])
-    diag_out = win[3, 96:144]
+    edge, lat_out, lon_out, diag_out = mlp(pos, mixed, f, gain, rest_pieces, 0, EDGE * TOK, (320, 320, 48))
     lat_in = from_grid(lat_out, -1, 0)
     lon_in = from_grid(lon_out, 0, -1)
     diag_in = from_grid(diag_out, -1, -1)
-    inner = mlp(pos, mixed, f, gain, rest_pieces, EDGE * TOK, INNER * TOK)
+    (inner,) = mlp(pos, mixed, f, gain, rest_pieces, EDGE * TOK, INNER * TOK)
     return to_grid(edge, inner, lat_in, lon_in, diag_in)
 
 

time: 115 us -> 106 us (0.922)
  local copies, waits for them, and re-layouts: 9.59 us -> 6.18 us
  waiting for transfers between devices: 19.2 us -> 16 us
  Pallas kernels: 51.6 us -> 50.1 us
    ppermute x6, starting transfers between devices: 11.6 us -> 7.25 us  [from_grid(): return lax.ppermute(block, AXES, pairs)]
    unnamed x28 -> x24, local copies, waits for them, and re-layouts: 5.15 us -> 0.87 us
    ppermute x6, waiting for transfers between devices: 9.95 us -> 5.94 us  [from_grid(): return lax.ppermute(block, AXES, pairs)]
    ppermute x17 -> x14, starting transfers between devices: 19.6 us -> 23 us  [send(): return lax.ppermute(block, AXES, pairs)]
    pallas_call x1, Pallas kernels: 25 us -> 23.8 us  [attend(): pl.pallas_call(attn_kernel, grid=(10,), in_specs=[pl.BlockSpec(memory_spa...]
    ppermute x17 -> x14, waiting for transfers between devices: 9.23 us -> 10.1 us  [send(): return lax.ppermute(block, AXES, pairs)]
  transfers between devices with their start and end apart: 23 -> 20, of which waited for: 8 -> 10; matrix products, arithmetic and copies ran while one was open for 5% -> 5% of each run, Pallas kernels for 36% -> 38%
where the time goes in v3:
time: 106 us; the launch traced here: 105 us
  Pallas kernels  50.1 us (47%)
  starting transfers between devices  30.2 us (28%)
  waiting for transfers between devices  16 us (15%)
  local copies, waits for them, and re-layouts  6.18 us (6%)
  other arithmetic  2.12 us (2%)
    pallas_call x1, Pallas kernels, attend(): pl.pallas_call(attn_kernel, grid=(10,), in_specs=[pl.BlockSpec(memory_spa...  23.8 us
    ppermute x14, starting transfers between devices, send(): return lax.ppermute(block, AXES, pairs)  23 us
    pallas_call x2, Pallas kernels, mlp(): pl.pallas_call(mlp_kernel, grid=(1,), in_specs=[pl.BlockSpec(memory_space...  14.7 us
    ppermute x14, waiting for transfers between devices, send(): return lax.ppermute(block, AXES, pairs)  10.1 us
    pallas_call x1, Pallas kernels, prep(): pl.pallas_call(prep_kernel, grid=(n // 4,), in_specs=[whole(a) for a in o...  8.23 us
    ppermute x6, starting transfers between devices, from_grid(): return lax.ppermute(block, AXES, pairs)  7.25 us
    ppermute x6, waiting for transfers between devices, from_grid(): return lax.ppermute(block, AXES, pairs)  5.94 us
    pallas_call x1, Pallas kernels, to_grid(): pl.pallas_call(place_kernel, out_shape=jax.ShapeDtypeStruct((1, 2, 24, 48...  3.32 us
  transfers between devices with their start and end apart: 20, of which 10 were waited for; matrix products, arithmetic and copies ran while one was open for 5% of the time, Pallas kernels for 38%

profile of v3, /device:TPU:1, one launch (start us, length us, event | category | flops | bytes accessed | tf_op | source)
XLA Modules:
  0.0 105.0 jit_solution(17286028025440949409)
XLA Ops:
  0.0 0.7 reshape.50
  0.8 0.8 bitcast_dynamic-update-slice_fusion.6
  1.5 2.1 %collective-permute-start.5 = (bf16[48,512]{1,0:T(8,128)(2,1)S(1)}, bf16[48,512]{1,0:T(8,128)(2,1)S(1)}, u32[]{:S(2)}, u32[]{:S(2)}) collective-permute-start(bf16[48,512]{1,0:T(8,128)(2,1)S(1)} %get-tuple-element.36), channel_id=1, source_target_pairs={{3,0},{0,1},{1,2},{2,3},{7,4},{4,5},{5,6},{6,7},{11,8},{8,9},{9,10... | collective-permute-start | bytes 147464 | tf_op jit(solution)/shard_map/ppermute | solution.py:40
  3.6 2.5 %collective-permute-start.4 = (bf16[48,512]{1,0:T(8,128)(2,1)S(1)}, bf16[48,512]{1,0:T(8,128)(2,1)S(1)}, u32[]{:S(2)}, u32[]{:S(2)}) collective-permute-start(bf16[48,512]{1,0:T(8,128)(2,1)S(1)} %get-tuple-element.36), channel_id=1, source_target_pairs={{2,0},{3,1},{0,2},{1,3},{6,4},{7,5},{4,6},{5,7},{10,8},{11,9},{8,1... | collective-permute-start | bytes 147464 | tf_op jit(solution)/shard_map/ppermute | solution.py:40
  6.1 1.2 %collective-permute-start.3 = (bf16[48,512]{1,0:T(8,128)(2,1)S(1)}, bf16[48,512]{1,0:T(8,128)(2,1)S(1)}, u32[]{:S(2)}, u32[]{:S(2)}) collective-permute-start(bf16[48,512]{1,0:T(8,128)(2,1)S(1)} %get-tuple-element.36), channel_id=1, source_target_pairs={{1,0},{2,1},{3,2},{0,3},{5,4},{6,5},{7,6},{4,7},{9,8},{10,9},{11,1... | collective-permute-start | bytes 147464 | tf_op jit(solution)/shard_map/ppermute | solution.py:40
  7.2 0.8 add_convert_fusion
  8.0 0.8 slice.72
  8.8 0.1 fusion.5
  8.9 6.1 %collective-permute-start.2 = (bf16[80,512]{1,0:T(8,128)(2,1)S(1)}, bf16[80,512]{1,0:T(8,128)(2,1)S(1)}, u32[]{:S(2)}, u32[]{:S(2)}) collective-permute-start(bf16[80,512]{1,0:T(8,128)(2,1)S(1)} %fusion.5), channel_id=1, source_target_pairs={{9,0},{10,1},{11,2},{12,3},{13,4},{14,5},{15,6},{8,7},{17,8},{18,9... | collective-permute-start | bytes 245768 | tf_op jit(solution)/shard_map/ppermute | solution.py:64
  15.0 1.0 slice.68
  16.0 0.2 collective-permute-start
  16.2 1.0 slice.70
  17.3 0.1 fusion.2
  17.3 0.6 pad.19.ids_ref
  17.9 0.5 collective-permute-start.1
  18.8 2.4 %collective-permute-start.6 = (bf16[144,512]{1,0:T(8,128)(2,1)S(1)}, bf16[144,512]{1,0:T(8,128)(2,1)S(1)}, u32[]{:S(2)}, u32[]{:S(2)}) collective-permute-start(bf16[144,512]{1,0:T(8,128)(2,1)S(1)} %pad_maximum_fusion.4), channel_id=1, source_target_pairs={{32,0},{33,1},{34,2},{35,3},{36,4},{37,5},{38,6},{39,7},{40,8},{41... | collective-permute-start | bytes 442376 | tf_op jit(solution)/shard_map/ppermute | solution.py:40
  21.3 1.0 collective-permute-done.6
  22.2 1.4 %collective-permute-start.9 = (bf16[336,512]{1,0:T(8,128)(2,1)S(1)}, bf16[336,512]{1,0:T(8,128)(2,1)S(1)}, u32[]{:S(2)}, u32[]{:S(2)}) collective-permute-start(bf16[336,512]{1,0:T(8,128)(2,1)S(1)} %constant_dynamic-update-slice_fusion), channel_id=1, source_target_pairs={{68,0},{69,1},{70,2},{71,3},{64,4},{65,5},{66,6},{67,7},{76,8},{77... | collective-permute-start | bytes 1032200 | tf_op jit(solution)/shard_map/ppermute | solution.py:40
  23.6 2.5 %collective-permute-start.7 = (bf16[336,512]{1,0:T(8,128)(2,1)S(1)}, bf16[336,512]{1,0:T(8,128)(2,1)S(1)}, u32[]{:S(2)}, u32[]{:S(2)}) collective-permute-start(bf16[336,512]{1,0:T(8,128)(2,1)S(1)} %constant_dynamic-update-slice_fusion), channel_id=1, source_target_pairs={{64,0},{65,1},{66,2},{67,3},{68,4},{69,5},{70,6},{71,7},{72,8},{73... | collective-permute-start | bytes 1032200 | tf_op jit(solution)/shard_map/ppermute | solution.py:40
  26.1 1.4 %collective-permute-done.1.cols_ref = bf16[416,512]{1,0:T(8,128)(2,1)S(1)} collective-permute-done((bf16[416,512]{1,0:T(8,128)(2,1)S(1)}, bf16[416,512]{1,0:T(8,128)(2,1)S(1)}, u32[]{:S(2)}, u32[]{:S(2)}) %collective-permute-start.1) | collective-permute-done | bytes 426016 | tf_op jit(solution)/shard_map/ppermute | solution.py:64
  27.5 0.8 copy-done.5
  28.3 8.2 %prep.1 = (bf16[16,144,512]{2,1,0:T(8,128)(2,1)}, bf16[16,144,512]{2,1,0:T(8,128)(2,1)}, bf16[16,256,512]{2,1,0:T(8,128)(2,1)}, bf16[16,144,256]{2,1,0:T(8,128)(2,1)}) custom-call(bf16[2,24,48,512]{3,2,1,0:T(8,128)(2,1)} %bitcast.68, bf16[320,512]{1,0:T(8,128)(2,1)} %collective-permute-done.rows_ref, bf16[416,512]{1,0:T(8,128)(2,1)} %copy-done.5, ...), custom_call_target="tpu_custom_call" | custom-call | flops 6000000000 | bytes 16000000 | tf_op jit(solution)/shard_map/prep/pallas_call | solution.py:137
  36.7 0.6 collective-permute-start.11
  37.2 2.3 %collective-permute-start.10 = (bf16[4,48,512]{2,1,0:T(8,128)(2,1)S(1)}, bf16[4,48,512]{2,1,0:T(8,128)(2,1)S(1)}, u32[]{:S(2)}, u32[]{:S(2)}) collective-permute-start(bf16[4,48,512]{2,1,0:T(8,128)(2,1)S(1)} %get-tuple-element.40), channel_id=1, source_target_pairs={{8,0},{9,1},{10,2},{11,3},{12,4},{13,5},{14,6},{15,7},{16,8},{17,9... | collective-permute-start | bytes 589832 | tf_op jit(solution)/shard_map/ppermute | solution.py:40
  39.5 3.2 %collective-permute-done.11 = bf16[4,48,512]{2,1,0:T(8,128)(2,1)S(1)} collective-permute-done((bf16[4,48,512]{2,1,0:T(8,128)(2,1)S(1)}, bf16[4,48,512]{2,1,0:T(8,128)(2,1)S(1)}, u32[]{:S(2)}, u32[]{:S(2)}) %collective-permute-start.11) | collective-permute-done | bytes 196640 | tf_op jit(solution)/shard_map/ppermute | solution.py:40
  42.8 0.5 collective-permute-done.10
  43.3 2.3 %collective-permute-done.12 = bf16[4,48,512]{2,1,0:T(8,128)(2,1)S(1)} collective-permute-done((bf16[4,48,512]{2,1,0:T(8,128)(2,1)S(1)}, bf16[4,48,512]{2,1,0:T(8,128)(2,1)S(1)}, u32[]{:S(2)}, u32[]{:S(2)}) %collective-permute-start.12) | collective-permute-done | bytes 196640 | tf_op jit(solution)/shard_map/ppermute | solution.py:40
  45.6 0.1 pad_maximum_fusion.1.refs_0_
  45.7 5.1 %collective-permute-start.13 = (bf16[4,4,48,512]{3,2,1,0:T(8,128)(2,1)S(1)}, bf16[4,4,48,512]{3,2,1,0:T(8,128)(2,1)S(1)}, u32[]{:S(2)}, u32[]{:S(2)}) collective-permute-start(bf16[4,4,48,512]{3,2,1,0:T(8,128)(2,1)S(1)} %pad_maximum_fusion.1.refs_0_), channel_id=1, source_target_pairs={{32,0},{33,1},{34,2},{35,3},{36,4},{37,5},{38,6},{39,7},{40,8},{41... | collective-permute-start | bytes 2359304 | tf_op jit(solution)/shard_map/ppermute | solution.py:40
  50.8 0.1 pad_add_fusion.pos_ref
  50.9 0.9 slice-done
  51.8 0.1 pad_maximum_fusion.refs_0_
  52.0 0.5 collective-permute-start.16
  52.4 1.6 %collective-permute-start.15 = (bf16[4,2,144,512]{3,2,1,0:T(8,128)(2,1)S(1)}, bf16[4,2,144,512]{3,2,1,0:T(8,128)(2,1)S(1)}, u32[]{:S(2)}, u32[]{:S(2)}) collective-permute-start(bf16[4,2,144,512]{3,2,1,0:T(8,128)(2,1)S(1)} %pad_maximum_fusion.refs_0_), channel_id=1, source_target_pairs={{16,0},{17,1},{18,2},{19,3},{20,4},{21,5},{22,6},{23,7},{24,8},{25... | collective-permute-start | bytes 3538952 | tf_op jit(solution)/shard_map/ppermute | solution.py:40
  54.0 0.9 collective-permute-start.14
  54.9 23.8 %attend.1 = bf16[16,144,512]{2,1,0:T(8,128)(2,1)S(1)} custom-call(s32[3]{0:T(128)S(1)} %pad_add_fusion.pos_ref, bf16[2304,512]{1,0:T(8,128)(2,1)} %bitcast.80, bf16[16,256,512]{2,1,0:T(8,128)(2,1)} %get-tuple-element.21.xq_a.xq_b.xv_a.xv_b, bf16[16,256,512]{2,1,0:T(8,128)(2,1)} %get-tuple-element.21.xq_a.xq_b.xv_a.xv_b, ...), custom_call_target="tpu_custom_call" | custom-call | flops 20000000000 | bytes 12000000 | tf_op jit(solution)/shard_map/attend/pallas_call | solution.py:263
  78.8 2.5 %collective-permute-done.16.refs_3_ = bf16[4,2,144,512]{3,2,1,0:T(8,128)(2,1)S(1)} collective-permute-done((bf16[4,2,144,512]{3,2,1,0:T(8,128)(2,1)S(1)}, bf16[4,2,144,512]{3,2,1,0:T(8,128)(2,1)S(1)}, u32[]{:S(2)}, u32[]{:S(2)}) %collective-permute-start.16) | collective-permute-done | bytes 1179680 | tf_op jit(solution)/shard_map/ppermute | solution.py:40
  81.2 0.6 collective-permute-done.14.refs_1_
  81.9 6.6 %shard_map.100 = (bf16[1008,512]{1,0:T(8,128)(2,1)S(1)}, bf16[320,512]{1,0:T(8,128)(2,1)S(1)}, bf16[320,512]{1,0:T(8,128)(2,1)S(1)}, bf16[48,512]{1,0:T(8,128)(2,1)S(1)}) custom-call(s32[3]{0:T(128)S(1)} %pad_add_fusion.pos_ref, bf16[2304,512]{1,0:T(8,128)(2,1)S(1)} %bitcast.53, bf16[2304,512]{1,0:T(8,128)(2,1)S(1)} %bitcast.51, f32[1,512]{1,0:T(1,128)S(1)} %bitcast.49, ...), custom_call_target="tpu_custom_call" | custom-call | flops 5040000000 | bytes 8096576 | tf_op jit(solution)/shard_map/pallas_call | solution.py:346
  88.5 0.1 collective-permute-start.19
  88.5 0.1 collective-permute-start.17
  88.6 0.0 copy-start.2
  88.7 0.3 collective-permute-start.18
  89.0 8.1 %shard_map.101.inner_ref = bf16[1296,512]{1,0:T(8,128)(2,1)S(1)} custom-call(s32[3]{0:T(128)S(1)} %pad_add_fusion.pos_ref, bf16[2304,512]{1,0:T(8,128)(2,1)S(1)} %bitcast.54, bf16[2304,512]{1,0:T(8,128)(2,1)S(1)} %bitcast.52, f32[1,512]{1,0:T(1,128)S(1)} %bitcast.50, bf16[4,2,144,512]{3,2,1,0:T(8,128)(2,1)S(1)} %pad_maximum_fusion.refs_0_, ...), custom_call_target="tpu_custom_call" | custom-call | flops 6480000000 | bytes 8981312 | tf_op jit(solution)/shard_map/pallas_call | solution.py:346
  97.1 0.2 collective-permute-done.19.diag_ref
  97.3 1.1 %collective-permute-done.17.lat_ref = bf16[320,512]{1,0:T(8,128)(2,1)S(1)} collective-permute-done((bf16[320,512]{1,0:T(8,128)(2,1)S(1)}, bf16[320,512]{1,0:T(8,128)(2,1)S(1)}, u32[]{:S(2)}, u32[]{:S(2)}) %collective-permute-start.17) | collective-permute-done | bytes 327712 | tf_op jit(solution)/shard_map/ppermute | solution.py:64
  98.4 3.2 %collective-permute-done.18.lon_ref = bf16[320,512]{1,0:T(8,128)(2,1)S(1)} collective-permute-done((bf16[320,512]{1,0:T(8,128)(2,1)S(1)}, bf16[320,512]{1,0:T(8,128)(2,1)S(1)}, u32[]{:S(2)}, u32[]{:S(2)}) %collective-permute-start.18) | collective-permute-done | bytes 327712 | tf_op jit(solution)/shard_map/ppermute | solution.py:64
  101.7 3.3 %to_grid.1 = bf16[1,2,24,48,512]{4,3,2,1,0:T(8,128)(2,1)} custom-call(bf16[1008,512]{1,0:T(8,128)(2,1)S(1)} %get-tuple-element.31.edge_ref, bf16[1296,512]{1,0:T(8,128)(2,1)S(1)} %shard_map.101.inner_ref, bf16[320,512]{1,0:T(8,128)(2,1)S(1)} %collective-permute-done.17.lat_ref, bf16[320,512]{1,0:T(8,128)(2,1)S(1)} %collective-permute-done.18.lon_ref, ...), custom_call_target="tpu_custom_call" | custom-call | flops 3000000000 | bytes 8000000 | tf_op jit(solution)/shard_map/to_grid/pallas_call | solution.py:423
  (59 shorter events, 0.5 us)
Async XLA Ops:
  1.5 16.9 %collective-permute-start.5 = (bf16[48,512]{1,0:T(8,128)(2,1)S(1)}, bf16[48,512]{1,0:T(8,128)(2,1)S(1)}, u32[]{:S(2)}, u32[]{:S(2)}) collective-permute-start(bf16[48,512]{1,0:T(8,128)(2,1)S(1)} %get-tuple-element.36), channel_id=1, source_target_pairs={{3,0},{0,1},{1,2},{2,3},{7,4},{4,5},{5,6},{6,7},{11,8},{8,9},{9,10... | collective-permute-start | bytes 147464 | tf_op jit(solution)/shard_map/ppermute | solution.py:40
  3.6 14.8 %collective-permute-start.4 = (bf16[48,512]{1,0:T(8,128)(2,1)S(1)}, bf16[48,512]{1,0:T(8,128)(2,1)S(1)}, u32[]{:S(2)}, u32[]{:S(2)}) collective-permute-start(bf16[48,512]{1,0:T(8,128)(2,1)S(1)} %get-tuple-element.36), channel_id=1, source_target_pairs={{2,0},{3,1},{0,2},{1,3},{6,4},{7,5},{4,6},{5,7},{10,8},{11,9},{8,1... | collective-permute-start | bytes 147464 | tf_op jit(solution)/shard_map/ppermute | solution.py:40
  6.1 11.9 %collective-permute-start.3 = (bf16[48,512]{1,0:T(8,128)(2,1)S(1)}, bf16[48,512]{1,0:T(8,128)(2,1)S(1)}, u32[]{:S(2)}, u32[]{:S(2)}) collective-permute-start(bf16[48,512]{1,0:T(8,128)(2,1)S(1)} %get-tuple-element.36), channel_id=1, source_target_pairs={{1,0},{2,1},{3,2},{0,3},{5,4},{6,5},{7,6},{4,7},{9,8},{10,9},{11,1... | collective-permute-start | bytes 147464 | tf_op jit(solution)/shard_map/ppermute | solution.py:40
  8.9 14.7 %collective-permute-start.2 = (bf16[80,512]{1,0:T(8,128)(2,1)S(1)}, bf16[80,512]{1,0:T(8,128)(2,1)S(1)}, u32[]{:S(2)}, u32[]{:S(2)}) collective-permute-start(bf16[80,512]{1,0:T(8,128)(2,1)S(1)} %fusion.5), channel_id=1, source_target_pairs={{9,0},{10,1},{11,2},{12,3},{13,4},{14,5},{15,6},{8,7},{17,8},{18,9... | collective-permute-start | bytes 245768 | tf_op jit(solution)/shard_map/ppermute | solution.py:64
  16.0 10.1 %collective-permute-start = (bf16[320,512]{1,0:T(8,128)(2,1)S(1)}, bf16[320,512]{1,0:T(8,128)(2,1)}, u32[]{:S(2)}, u32[]{:S(2)}) collective-permute-start(bf16[320,512]{1,0:T(8,128)(2,1)S(1)} %fusion.3), channel_id=1, source_target_pairs={{8,0},{9,1},{10,2},{11,3},{12,4},{13,5},{14,6},{15,7},{16,8},{17,9... | collective-permute-start | bytes 983048 | tf_op jit(solution)/shard_map/ppermute | solution.py:64
  17.9 9.6 %collective-permute-start.1 = (bf16[416,512]{1,0:T(8,128)(2,1)S(1)}, bf16[416,512]{1,0:T(8,128)(2,1)S(1)}, u32[]{:S(2)}, u32[]{:S(2)}) collective-permute-start(bf16[416,512]{1,0:T(8,128)(2,1)S(1)} %fusion.2), channel_id=1, source_target_pairs={{1,0},{2,1},{3,2},{4,3},{5,4},{6,5},{7,6},{0,7},{9,8},{10,9},{11,1... | collective-permute-start | bytes 1277960 | tf_op jit(solution)/shard_map/ppermute | solution.py:64
  18.8 3.4 %collective-permute-start.6 = (bf16[144,512]{1,0:T(8,128)(2,1)S(1)}, bf16[144,512]{1,0:T(8,128)(2,1)S(1)}, u32[]{:S(2)}, u32[]{:S(2)}) collective-permute-start(bf16[144,512]{1,0:T(8,128)(2,1)S(1)} %pad_maximum_fusion.4), channel_id=1, source_target_pairs={{32,0},{33,1},{34,2},{35,3},{36,4},{37,5},{38,6},{39,7},{40,8},{41... | collective-permute-start | bytes 442376 | tf_op jit(solution)/shard_map/ppermute | solution.py:40
  22.2 14.3 %collective-permute-start.9 = (bf16[336,512]{1,0:T(8,128)(2,1)S(1)}, bf16[336,512]{1,0:T(8,128)(2,1)S(1)}, u32[]{:S(2)}, u32[]{:S(2)}) collective-permute-start(bf16[336,512]{1,0:T(8,128)(2,1)S(1)} %constant_dynamic-update-slice_fusion), channel_id=1, source_target_pairs={{68,0},{69,1},{70,2},{71,3},{64,4},{65,5},{66,6},{67,7},{76,8},{77... | collective-permute-start | bytes 1032200 | tf_op jit(solution)/shard_map/ppermute | solution.py:40
  23.6 12.9 %collective-permute-start.8 = (bf16[336,512]{1,0:T(8,128)(2,1)S(1)}, bf16[336,512]{1,0:T(8,128)(2,1)S(1)}, u32[]{:S(2)}, u32[]{:S(2)}) collective-permute-start(bf16[336,512]{1,0:T(8,128)(2,1)S(1)} %constant_dynamic-update-slice_fusion), channel_id=1, source_target_pairs={{4,0},{5,1},{6,2},{7,3},{0,4},{1,5},{2,6},{3,7},{12,8},{13,9},{14,... | collective-permute-start | bytes 1032200 | tf_op jit(solution)/shard_map/ppermute | solution.py:40
  23.6 3.9 %copy-start.6 = (bf16[80,512]{1,0:T(8,128)(2,1)}, bf16[80,512]{1,0:T(8,128)(2,1)S(1)}, u32[]{:S(2)}) copy-start(bf16[80,512]{1,0:T(8,128)(2,1)S(1)} %collective-permute-done.2.both_ref) | copy-start | bytes 245764
  23.6 12.9 %collective-permute-start.7 = (bf16[336,512]{1,0:T(8,128)(2,1)S(1)}, bf16[336,512]{1,0:T(8,128)(2,1)S(1)}, u32[]{:S(2)}, u32[]{:S(2)}) collective-permute-start(bf16[336,512]{1,0:T(8,128)(2,1)S(1)} %constant_dynamic-update-slice_fusion), channel_id=1, source_target_pairs={{64,0},{65,1},{66,2},{67,3},{68,4},{69,5},{70,6},{71,7},{72,8},{73... | collective-permute-start | bytes 1032200 | tf_op jit(solution)/shard_map/ppermute | solution.py:40
  27.5 0.8 copy-start.5
  36.6 14.3 %copy-start.4 = (bf16[336,512]{1,0:T(8,128)(2,1)}, bf16[336,512]{1,0:T(8,128)(2,1)S(1)}, u32[]{:S(2)}) copy-start(bf16[336,512]{1,0:T(8,128)(2,1)S(1)} %collective-permute-done.7) | copy-start | bytes 1032196
  36.7 6.1 %collective-permute-start.11 = (bf16[4,48,512]{2,1,0:T(8,128)(2,1)S(1)}, bf16[4,48,512]{2,1,0:T(8,128)(2,1)S(1)}, u32[]{:S(2)}, u32[]{:S(2)}) collective-permute-start(bf16[4,48,512]{2,1,0:T(8,128)(2,1)S(1)} %get-tuple-element.40), channel_id=1, source_target_pairs={{16,0},{17,1},{18,2},{19,3},{20,4},{21,5},{22,6},{23,7},{24,8},{25... | collective-permute-start | bytes 589832 | tf_op jit(solution)/shard_map/ppermute | solution.py:40
  37.2 6.0 %collective-permute-start.10 = (bf16[4,48,512]{2,1,0:T(8,128)(2,1)S(1)}, bf16[4,48,512]{2,1,0:T(8,128)(2,1)S(1)}, u32[]{:S(2)}, u32[]{:S(2)}) collective-permute-start(bf16[4,48,512]{2,1,0:T(8,128)(2,1)S(1)} %get-tuple-element.40), channel_id=1, source_target_pairs={{8,0},{9,1},{10,2},{11,3},{12,4},{13,5},{14,6},{15,7},{16,8},{17,9... | collective-permute-start | bytes 589832 | tf_op jit(solution)/shard_map/ppermute | solution.py:40
  39.5 6.0 %collective-permute-start.12 = (bf16[4,48,512]{2,1,0:T(8,128)(2,1)S(1)}, bf16[4,48,512]{2,1,0:T(8,128)(2,1)S(1)}, u32[]{:S(2)}, u32[]{:S(2)}) collective-permute-start(bf16[4,48,512]{2,1,0:T(8,128)(2,1)S(1)} %get-tuple-element.40), channel_id=1, source_target_pairs={{24,0},{25,1},{26,2},{27,3},{28,4},{29,5},{30,6},{31,7},{0,8},{1,9... | collective-permute-start | bytes 589832 | tf_op jit(solution)/shard_map/ppermute | solution.py:40
  45.7 9.3 %collective-permute-start.13 = (bf16[4,4,48,512]{3,2,1,0:T(8,128)(2,1)S(1)}, bf16[4,4,48,512]{3,2,1,0:T(8,128)(2,1)S(1)}, u32[]{:S(2)}, u32[]{:S(2)}) collective-permute-start(bf16[4,4,48,512]{3,2,1,0:T(8,128)(2,1)S(1)} %pad_maximum_fusion.1.refs_0_), channel_id=1, source_target_pairs={{32,0},{33,1},{34,2},{35,3},{36,4},{37,5},{38,6},{39,7},{40,8},{41... | collective-permute-start | bytes 2359304 | tf_op jit(solution)/shard_map/ppermute | solution.py:40
  50.9 1.0 slice-start
  52.0 29.3 %collective-permute-start.16 = (bf16[4,2,144,512]{3,2,1,0:T(8,128)(2,1)S(1)}, bf16[4,2,144,512]{3,2,1,0:T(8,128)(2,1)S(1)}, u32[]{:S(2)}, u32[]{:S(2)}) collective-permute-start(bf16[4,2,144,512]{3,2,1,0:T(8,128)(2,1)S(1)} %pad_maximum_fusion.refs_0_), channel_id=1, source_target_pairs={{24,0},{25,1},{26,2},{27,3},{28,4},{29,5},{30,6},{31,7},{0,8},{1,9... | collective-permute-start | bytes 3538952 | tf_op jit(solution)/shard_map/ppermute | solution.py:40
  52.4 28.8 %collective-permute-start.15 = (bf16[4,2,144,512]{3,2,1,0:T(8,128)(2,1)S(1)}, bf16[4,2,144,512]{3,2,1,0:T(8,128)(2,1)S(1)}, u32[]{:S(2)}, u32[]{:S(2)}) collective-permute-start(bf16[4,2,144,512]{3,2,1,0:T(8,128)(2,1)S(1)} %pad_maximum_fusion.refs_0_), channel_id=1, source_target_pairs={{16,0},{17,1},{18,2},{19,3},{20,4},{21,5},{22,6},{23,7},{24,8},{25... | collective-permute-start | bytes 3538952 | tf_op jit(solution)/shard_map/ppermute | solution.py:40
  54.0 27.9 %collective-permute-start.14 = (bf16[4,2,144,512]{3,2,1,0:T(8,128)(2,1)S(1)}, bf16[4,2,144,512]{3,2,1,0:T(8,128)(2,1)S(1)}, u32[]{:S(2)}, u32[]{:S(2)}) collective-permute-start(bf16[4,2,144,512]{3,2,1,0:T(8,128)(2,1)S(1)} %pad_maximum_fusion.refs_0_), channel_id=1, source_target_pairs={{8,0},{9,1},{10,2},{11,3},{12,4},{13,5},{14,6},{15,7},{16,8},{17,9... | collective-permute-start | bytes 3538952 | tf_op jit(solution)/shard_map/ppermute | solution.py:40
  54.9 26.9 %copy-start = (f32[512]{0:T(512)S(1)}, f32[512]{0:T(512)}, u32[]{:S(2)}) copy-start(f32[512]{0:T(512)} %param.15) | copy-start | bytes 6148
  54.9 26.9 %copy-start.1 = (bf16[16,144,512]{2,1,0:T(8,128)(2,1)S(1)}, bf16[16,144,512]{2,1,0:T(8,128)(2,1)}, u32[]{:S(2)}) copy-start(bf16[16,144,512]{2,1,0:T(8,128)(2,1)} %get-tuple-element.23) | copy-start | bytes 7077892
  88.5 8.8 %collective-permute-start.19 = (bf16[48,512]{1,0:T(8,128)(2,1)S(1)}, bf16[48,512]{1,0:T(8,128)(2,1)S(1)}, u32[]{:S(2)}, u32[]{:S(2)}) collective-permute-start(bf16[48,512]{1,0:T(8,128)(2,1)S(1)} %get-tuple-element.34), channel_id=1, source_target_pairs={{31,0},{24,1},{25,2},{26,3},{27,4},{28,5},{29,6},{30,7},{7,8},{0,9... | collective-permute-start | bytes 147464 | tf_op jit(solution)/shard_map/ppermute | solution.py:64
  88.5 9.9 %collective-permute-start.17 = (bf16[320,512]{1,0:T(8,128)(2,1)S(1)}, bf16[320,512]{1,0:T(8,128)(2,1)S(1)}, u32[]{:S(2)}, u32[]{:S(2)}) collective-permute-start(bf16[320,512]{1,0:T(8,128)(2,1)S(1)} %get-tuple-element.32), channel_id=1, source_target_pairs={{24,0},{25,1},{26,2},{27,3},{28,4},{29,5},{30,6},{31,7},{0,8},{1,9... | collective-permute-start | bytes 983048 | tf_op jit(solution)/shard_map/ppermute | solution.py:64
  88.6 13.0 %copy-start.2 = (bf16[576,656]{1,0:T(8,128)(2,1)S(1)}, bf16[576,656]{1,0:T(8,128)(2,1)}, u32[]{:S(2)}) copy-start(bf16[576,656]{1,0:T(8,128)(2,1)} %constant.70.clone.mid_ref) | copy-start | bytes 2267140
  88.6 13.0 %copy-start.3 = (bf16[288,368]{1,0:T(8,128)(2,1)S(1)}, bf16[288,368]{1,0:T(8,128)(2,1)}, u32[]{:S(2)}) copy-start(bf16[288,368]{1,0:T(8,128)(2,1)} %constant.69.clone.top_ref) | copy-start | bytes 635908
  88.7 13.0 %collective-permute-start.18 = (bf16[320,512]{1,0:T(8,128)(2,1)S(1)}, bf16[320,512]{1,0:T(8,128)(2,1)S(1)}, u32[]{:S(2)}, u32[]{:S(2)}) collective-permute-start(bf16[320,512]{1,0:T(8,128)(2,1)S(1)} %get-tuple-element.33), channel_id=1, source_target_pairs={{7,0},{0,1},{1,2},{2,3},{3,4},{4,5},{5,6},{6,7},{15,8},{8,9},{9,10... | collective-permute-start | bytes 983048 | tf_op jit(solution)/shard_map/ppermute | solution.py:64

commit v4 on v3

--- a/solution.py
+++ b/solution.py
@@ -71,7 +71,7 @@
     return (centred * lax.rsqrt(variance + eps) * gain).astype(BF16)
 
 
-def prep_kernel(member_ref, rows_ref, cols_ref, both_ref, ids_ref, gain_ref, f_ref, x_ref, xq_ref, bias_ref, ext, near_ref):
+def prep_kernel(member_ref, rows_ref, cols_ref, both_ref, ids_ref, gain_ref, f_ref, x_ref, bias_ref, ext, near_ref):
     step = pl.program_id(0)
 
     @pl.when(step == 0)
@@ -118,9 +118,6 @@
         f_ref[at] = f.astype(BF16)
         x = norm(f, gain_ref[...])
         x_ref[at] = x
-        xq_ref[at, 0:128] = x[0:128]
-        for t in range(8):
-            xq_ref[at, 128 + 16 * t : 144 + 16 * t] = x[128:144]
         near = near_ref[pl.ds(start, 32), :]
         marks = [jnp.where(lane == 6 * wi + SH + n, near, 0.0).astype(BF16) for n in range(6)]
         marks = jnp.dot(pick, jnp.concatenate(marks * 2, axis=0), preferred_element_type=F32)
@@ -133,7 +130,7 @@
     n = EDGE + INNER
     whole = lambda a: pl.BlockSpec(a.shape, lambda i: (0,) * a.ndim, pipeline_mode=pl.Buffered(1))
     out = lambda *s: (jax.ShapeDtypeStruct((n, *s), BF16), pl.BlockSpec((4, *s), lambda i: (i, 0, 0)))
-    shapes, specs = zip(out(TOK, D), out(TOK, D), out(256, D), out(TOK, 256))
+    shapes, specs = zip(out(TOK, D), out(TOK, D), out(TOK, 256))
     return pl.pallas_call(
         prep_kernel,
         grid=(n // 4,),
@@ -165,10 +162,10 @@
     return (y % 2) * 16 + (mine if side == 0 else 1 - mine) * 8 + z * 2 + y // 2
 
 
-def attn_kernel(pos_ref, x_ref, xq_a, xq_b, xv_a, xv_b, bias_ref, *refs):
+def attn_kernel(pos_ref, x_ref, bias_ref, *refs):
     pieces, out_ref = refs[:2], refs[2]
     w, kall, own = refs[3:6]
-    q2, v2, s2, p2, m2 = (refs[n : n + 2] for n in range(6, 16, 2))
+    q2, v2, s2, p2, m2, x2 = (refs[n : n + 2] for n in range(6, 18, 2))
     i = pl.program_id(0)
 
     @pl.when(i == 0)
@@ -189,8 +186,8 @@
 
     def project(dst, x, first, n):
         at = 256 * n
-        out = lax.dot_general(w[first + at : first + at + 256, :], x[0], NT, preferred_element_type=F32)
-        dst[at : at + 256] = out.astype(BF16)
+        out = lax.dot_general(w[first + at : first + at + 256, :], x, NT, preferred_element_type=F32)
+        dst[at : at + 256, 0 : x.shape[0]] = out.astype(BF16)
 
     def scores(qt, s, krow, n):
         if n < 8:
@@ -235,41 +232,43 @@
                 part = o[32 * h : 32 * h + 32, side : side + 128] * inv[:, side : side + 128]
                 mt[32 * h : 32 * h + 32, 128:256] = pltpu.roll(part, (128 - 16 * (h % 8)) % 128, 1)
 
-    def half(par, win, xq, xv):
+    def half(par, win):
         new, old = par, 1 - par
+        qrow = pl.multiple_of(jnp.clip(win, 0, 15) * TOK, 16)
+        vrow = pl.multiple_of(jnp.clip(win - 2, 0, 15) * TOK, 16)
+        xq = x2[new]
+        xq[0:128] = x_ref[pl.ds(qrow, 128), :]
+        few = x_ref[pl.ds(qrow + 128, 16), :]
+        for t in range(8):
+            xq[128 + 16 * t : 144 + 16 * t] = few
         krow = pl.multiple_of(jnp.clip(win - 1, 0, 15) * TOK, 16)
         soft = jnp.clip(win - 2, 0, 15)
         for n in range(9):
             if n < 2:
-                project(q2[new], xq, 0, n)
+                project(q2[new], xq[...], 0, n)
             elif n < 4:
-                project(v2[new], xv, 2 * D, n - 2)
+                project(v2[new], x_ref[pl.ds(vrow, TOK), :], 2 * D, n - 2)
             scores(q2[old], s2[old], krow, n)
             soften(s2[new], p2[new], soft, n)
             mix(v2[old], p2[old], m2[old], n)
         out_ref[old] = m2[old][...].T[0:TOK].astype(BF16)
 
-    half(1, 2 * i - 1, xq_a, xv_a)
-    half(0, 2 * i, xq_b, xv_b)
+    half(1, 2 * i - 1)
+    half(0, 2 * i)
 
 
 def far(array):
     return pltpu.with_memory_space_constraint(array, pltpu.HBM)
 
 
-def attend(pos, x, xq, bias, pieces):
+def attend(pos, x, bias, pieces):
     whole = lambda a: pl.BlockSpec(a.shape, lambda i: (0,) * a.ndim, pipeline_mode=pl.Buffered(1))
-    one = lambda d: pl.BlockSpec((1, 256, D), lambda i: (jnp.clip(2 * i + d, 0, 15), 0, 0))
     return pl.pallas_call(
         attn_kernel,
         grid=(10,),
         in_specs=[
             pl.BlockSpec(memory_space=pltpu.SMEM),
             whole(x),
-            one(-1),
-            one(0),
-            one(-3),
-            one(-2),
             whole(bias),
             *[whole(p) for p in pieces],
         ],
@@ -283,11 +282,12 @@
             *[pltpu.VMEM((TOK, 2304), F32)] * 2,
             *[pltpu.VMEM((TOK, 2304), BF16)] * 2,
             *[pltpu.VMEM((D, 256), F32)] * 2,
+            *[pltpu.VMEM((256, D), BF16)] * 2,
         ],
         name="attend",
         compiler_params=pltpu.CompilerParams(vmem_limit_bytes=36 * 2**20),
         cost_estimate=pl.CostEstimate(flops=20_000_000_000, bytes_accessed=12_000_000, transcendentals=5_000_000),
-    )(pos, far(x), *[far(xq)] * 4, far(bias), *pieces)
+    )(pos, far(x), far(bias), *pieces)
 
 
 def mlp_kernel(pos_ref, mixed_ref, f_ref, gain_ref, *refs):
@@ -467,7 +467,7 @@
 
     stage = jnp.concatenate([stage, other_core(stage[48:192])])
     firsts = [along_first(stage, d) for d in (1, 2, 3)]
-    f, x, xq, bias = prep(member, rows, cols, both, ids, gain_attn.reshape(1, D))
+    f, x, bias = prep(member, rows, cols, both, ids, gain_attn.reshape(1, D))
     firsts = lax.optimization_barrier((*firsts, f))[:3]
     group = jnp.stack([p[0:48] for p in (stage, *firsts)])
     rest = jnp.stack([p[48:336].reshape(2, 144, D) for p in (stage, *firsts)])
@@ -475,7 +475,7 @@
     qkv_mine = jnp.stack([group, *qkv_sent])
     qkv_pieces = [qkv_mine, other_core(qkv_mine)]
     rest_mine = [rest, *[along_second(rest, d) for d in (1, 2, 3)]]
-    mixed = attend(pos, x.reshape(-1, D), xq, bias, qkv_pieces).reshape(-1, D)
+    mixed = attend(pos, x.reshape(-1, D), bias, qkv_pieces).reshape(-1, D)
     rest_pieces = lax.optimization_barrier((*rest_mine, mixed))[:4]
     f = f.reshape(-1, D)
     gain = gain_mlp.reshape(1, D)

time: 106 us -> 105 us (level)
  Pallas kernels: 50.1 us -> 47.7 us
  waiting for transfers between devices: 16 us -> 18.1 us
    ppermute x14, waiting for transfers between devices: 10.1 us -> 12.1 us  [send(): return lax.ppermute(block, AXES, pairs)]
    pallas_call x1, Pallas kernels: 23.8 us -> 21.8 us  [attend(): pl.pallas_call(attn_kernel, grid=(10,), in_specs=[pl.BlockSpec(memory_spa...]
  transfers between devices with their start and end apart: 20 -> 20, of which waited for: 10 -> 10; matrix products, arithmetic and copies ran while one was open for 5% -> 5% of each run, Pallas kernels for 38% -> 36%
where the time goes in v4:
time: 105 us
  Pallas kernels  47.7 us (45%)
  starting transfers between devices  30.2 us (29%)
  waiting for transfers between devices  18.1 us (17%)
  local copies, waits for them, and re-layouts  6.15 us (6%)
  other arithmetic  2.12 us (2%)
    ppermute x14, starting transfers between devices, send(): return lax.ppermute(block, AXES, pairs)  23 us
    pallas_call x1, Pallas kernels, attend(): pl.pallas_call(attn_kernel, grid=(10,), in_specs=[pl.BlockSpec(memory_spa...  21.8 us
    pallas_call x2, Pallas kernels, mlp(): pl.pallas_call(mlp_kernel, grid=(1,), in_specs=[pl.BlockSpec(memory_space...  14.7 us
    ppermute x14, waiting for transfers between devices, send(): return lax.ppermute(block, AXES, pairs)  12.1 us
    pallas_call x1, Pallas kernels, prep(): pl.pallas_call(prep_kernel, grid=(n // 4,), in_specs=[whole(a) for a in o...  7.9 us
    ppermute x6, starting transfers between devices, from_grid(): return lax.ppermute(block, AXES, pairs)  7.25 us
    ppermute x6, waiting for transfers between devices, from_grid(): return lax.ppermute(block, AXES, pairs)  5.95 us
    pallas_call x1, Pallas kernels, to_grid(): pl.pallas_call(place_kernel, out_shape=jax.ShapeDtypeStruct((1, 2, 24, 48...  3.33 us
  transfers between devices with their start and end apart: 20, of which 10 were waited for; matrix products, arithmetic and copies ran while one was open for 5% of the time, Pallas kernels for 36%

profile of v4, /device:TPU:1, one launch (start us, length us, event | category | flops | bytes accessed | tf_op | source)
XLA Modules:
  0.0 104.6 jit_solution(13621547386013249885)
XLA Ops:
  0.0 0.7 reshape.50
  0.8 0.8 bitcast_dynamic-update-slice_fusion.6
  1.5 2.1 %collective-permute-start.5 = (bf16[48,512]{1,0:T(8,128)(2,1)S(1)}, bf16[48,512]{1,0:T(8,128)(2,1)S(1)}, u32[]{:S(2)}, u32[]{:S(2)}) collective-permute-start(bf16[48,512]{1,0:T(8,128)(2,1)S(1)} %get-tuple-element.34), channel_id=1, source_target_pairs={{3,0},{0,1},{1,2},{2,3},{7,4},{4,5},{5,6},{6,7},{11,8},{8,9},{9,10... | collective-permute-start | bytes 147464 | tf_op jit(solution)/shard_map/ppermute | solution.py:40
  3.6 2.5 %collective-permute-start.4 = (bf16[48,512]{1,0:T(8,128)(2,1)S(1)}, bf16[48,512]{1,0:T(8,128)(2,1)S(1)}, u32[]{:S(2)}, u32[]{:S(2)}) collective-permute-start(bf16[48,512]{1,0:T(8,128)(2,1)S(1)} %get-tuple-element.34), channel_id=1, source_target_pairs={{2,0},{3,1},{0,2},{1,3},{6,4},{7,5},{4,6},{5,7},{10,8},{11,9},{8,1... | collective-permute-start | bytes 147464 | tf_op jit(solution)/shard_map/ppermute | solution.py:40
  6.1 1.2 %collective-permute-start.3 = (bf16[48,512]{1,0:T(8,128)(2,1)S(1)}, bf16[48,512]{1,0:T(8,128)(2,1)S(1)}, u32[]{:S(2)}, u32[]{:S(2)}) collective-permute-start(bf16[48,512]{1,0:T(8,128)(2,1)S(1)} %get-tuple-element.34), channel_id=1, source_target_pairs={{1,0},{2,1},{3,2},{0,3},{5,4},{6,5},{7,6},{4,7},{9,8},{10,9},{11,1... | collective-permute-start | bytes 147464 | tf_op jit(solution)/shard_map/ppermute | solution.py:40
  7.2 0.8 add_convert_fusion
  8.0 0.8 slice.72
  8.8 0.1 fusion.5
  8.9 6.1 %collective-permute-start.2 = (bf16[80,512]{1,0:T(8,128)(2,1)S(1)}, bf16[80,512]{1,0:T(8,128)(2,1)S(1)}, u32[]{:S(2)}, u32[]{:S(2)}) collective-permute-start(bf16[80,512]{1,0:T(8,128)(2,1)S(1)} %fusion.5), channel_id=1, source_target_pairs={{9,0},{10,1},{11,2},{12,3},{13,4},{14,5},{15,6},{8,7},{17,8},{18,9... | collective-permute-start | bytes 245768 | tf_op jit(solution)/shard_map/ppermute | solution.py:64
  15.0 1.0 slice.68
  16.0 0.2 collective-permute-start
  16.2 1.0 slice.70
  17.3 0.1 fusion.2
  17.3 0.6 pad.19.ids_ref
  17.9 0.5 collective-permute-start.1
  18.8 2.4 %collective-permute-start.6 = (bf16[144,512]{1,0:T(8,128)(2,1)S(1)}, bf16[144,512]{1,0:T(8,128)(2,1)S(1)}, u32[]{:S(2)}, u32[]{:S(2)}) collective-permute-start(bf16[144,512]{1,0:T(8,128)(2,1)S(1)} %pad_maximum_fusion.4), channel_id=1, source_target_pairs={{32,0},{33,1},{34,2},{35,3},{36,4},{37,5},{38,6},{39,7},{40,8},{41... | collective-permute-start | bytes 442376 | tf_op jit(solution)/shard_map/ppermute | solution.py:40
  21.3 1.0 collective-permute-done.6
  22.2 1.4 %collective-permute-start.9 = (bf16[336,512]{1,0:T(8,128)(2,1)S(1)}, bf16[336,512]{1,0:T(8,128)(2,1)S(1)}, u32[]{:S(2)}, u32[]{:S(2)}) collective-permute-start(bf16[336,512]{1,0:T(8,128)(2,1)S(1)} %constant_dynamic-update-slice_fusion), channel_id=1, source_target_pairs={{68,0},{69,1},{70,2},{71,3},{64,4},{65,5},{66,6},{67,7},{76,8},{77... | collective-permute-start | bytes 1032200 | tf_op jit(solution)/shard_map/ppermute | solution.py:40
  23.6 0.0 collective-permute-start.8
  23.6 2.5 %collective-permute-start.7 = (bf16[336,512]{1,0:T(8,128)(2,1)S(1)}, bf16[336,512]{1,0:T(8,128)(2,1)S(1)}, u32[]{:S(2)}, u32[]{:S(2)}) collective-permute-start(bf16[336,512]{1,0:T(8,128)(2,1)S(1)} %constant_dynamic-update-slice_fusion), channel_id=1, source_target_pairs={{64,0},{65,1},{66,2},{67,3},{68,4},{69,5},{70,6},{71,7},{72,8},{73... | collective-permute-start | bytes 1032200 | tf_op jit(solution)/shard_map/ppermute | solution.py:40
  26.1 1.4 %collective-permute-done.1.cols_ref = bf16[416,512]{1,0:T(8,128)(2,1)S(1)} collective-permute-done((bf16[416,512]{1,0:T(8,128)(2,1)S(1)}, bf16[416,512]{1,0:T(8,128)(2,1)S(1)}, u32[]{:S(2)}, u32[]{:S(2)}) %collective-permute-start.1) | collective-permute-done | bytes 426016 | tf_op jit(solution)/shard_map/ppermute | solution.py:64
  27.5 0.8 copy-done.5
  28.3 7.9 %prep.1 = (bf16[16,144,512]{2,1,0:T(8,128)(2,1)}, bf16[16,144,512]{2,1,0:T(8,128)(2,1)}, bf16[16,144,256]{2,1,0:T(8,128)(2,1)}) custom-call(bf16[2,24,48,512]{3,2,1,0:T(8,128)(2,1)} %bitcast.68, bf16[320,512]{1,0:T(8,128)(2,1)} %collective-permute-done.rows_ref, bf16[416,512]{1,0:T(8,128)(2,1)} %copy-done.5, bf16[80,512]{1,0:T(8,128)(2,1)} %copy-done.6, ...), custom_call_target="tpu_custom_call" | custom-call | flops 6000000000 | bytes 16000000 | tf_op jit(solution)/shard_map/prep/pallas_call | solution.py:134
  36.3 0.5 collective-permute-start.11
  36.8 2.4 %collective-permute-start.10 = (bf16[4,48,512]{2,1,0:T(8,128)(2,1)S(1)}, bf16[4,48,512]{2,1,0:T(8,128)(2,1)S(1)}, u32[]{:S(2)}, u32[]{:S(2)}) collective-permute-start(bf16[4,48,512]{2,1,0:T(8,128)(2,1)S(1)} %get-tuple-element.38), channel_id=1, source_target_pairs={{8,0},{9,1},{10,2},{11,3},{12,4},{13,5},{14,6},{15,7},{16,8},{17,9... | collective-permute-start | bytes 589832 | tf_op jit(solution)/shard_map/ppermute | solution.py:40
  39.2 3.2 %collective-permute-done.11 = bf16[4,48,512]{2,1,0:T(8,128)(2,1)S(1)} collective-permute-done((bf16[4,48,512]{2,1,0:T(8,128)(2,1)S(1)}, bf16[4,48,512]{2,1,0:T(8,128)(2,1)S(1)}, u32[]{:S(2)}, u32[]{:S(2)}) %collective-permute-start.11) | collective-permute-done | bytes 196640 | tf_op jit(solution)/shard_map/ppermute | solution.py:40
  42.4 0.5 collective-permute-done.10
  42.9 2.3 %collective-permute-done.12 = bf16[4,48,512]{2,1,0:T(8,128)(2,1)S(1)} collective-permute-done((bf16[4,48,512]{2,1,0:T(8,128)(2,1)S(1)}, bf16[4,48,512]{2,1,0:T(8,128)(2,1)S(1)}, u32[]{:S(2)}, u32[]{:S(2)}) %collective-permute-start.12) | collective-permute-done | bytes 196640 | tf_op jit(solution)/shard_map/ppermute | solution.py:40
  45.2 0.1 pad_maximum_fusion.1.refs_0_
  45.3 5.1 %collective-permute-start.13 = (bf16[4,4,48,512]{3,2,1,0:T(8,128)(2,1)S(1)}, bf16[4,4,48,512]{3,2,1,0:T(8,128)(2,1)S(1)}, u32[]{:S(2)}, u32[]{:S(2)}) collective-permute-start(bf16[4,4,48,512]{3,2,1,0:T(8,128)(2,1)S(1)} %pad_maximum_fusion.1.refs_0_), channel_id=1, source_target_pairs={{32,0},{33,1},{34,2},{35,3},{36,4},{37,5},{38,6},{39,7},{40,8},{41... | collective-permute-start | bytes 2359304 | tf_op jit(solution)/shard_map/ppermute | solution.py:40
  50.4 0.1 pad_add_fusion.pos_ref
  50.6 0.9 slice-done
  51.5 0.1 pad_maximum_fusion.refs_0_
  51.6 0.5 collective-permute-start.16
  52.1 1.6 %collective-permute-start.15 = (bf16[4,2,144,512]{3,2,1,0:T(8,128)(2,1)S(1)}, bf16[4,2,144,512]{3,2,1,0:T(8,128)(2,1)S(1)}, u32[]{:S(2)}, u32[]{:S(2)}) collective-permute-start(bf16[4,2,144,512]{3,2,1,0:T(8,128)(2,1)S(1)} %pad_maximum_fusion.refs_0_), channel_id=1, source_target_pairs={{16,0},{17,1},{18,2},{19,3},{20,4},{21,5},{22,6},{23,7},{24,8},{25... | collective-permute-start | bytes 3538952 | tf_op jit(solution)/shard_map/ppermute | solution.py:40
  53.6 0.9 collective-permute-start.14
  54.6 21.8 %attend.1 = bf16[16,144,512]{2,1,0:T(8,128)(2,1)S(1)} custom-call(s32[3]{0:T(128)S(1)} %pad_add_fusion.pos_ref, bf16[2304,512]{1,0:T(8,128)(2,1)} %bitcast.80, bf16[16,144,256]{2,1,0:T(8,128)(2,1)} %get-tuple-element.20.bias_ref, bf16[4,4,48,512]{3,2,1,0:T(8,128)(2,1)S(1)} %pad_maximum_fusion.1.refs_0_, ...), custom_call_target="tpu_custom_call" | custom-call | flops 20000000000 | bytes 12000000 | tf_op jit(solution)/shard_map/attend/pallas_call | solution.py:266
  76.4 4.5 %collective-permute-done.16.refs_3_ = bf16[4,2,144,512]{3,2,1,0:T(8,128)(2,1)S(1)} collective-permute-done((bf16[4,2,144,512]{3,2,1,0:T(8,128)(2,1)S(1)}, bf16[4,2,144,512]{3,2,1,0:T(8,128)(2,1)S(1)}, u32[]{:S(2)}, u32[]{:S(2)}) %collective-permute-start.16) | collective-permute-done | bytes 1179680 | tf_op jit(solution)/shard_map/ppermute | solution.py:40
  80.9 0.6 collective-permute-done.14.refs_1_
  81.5 6.6 %shard_map.100 = (bf16[1008,512]{1,0:T(8,128)(2,1)S(1)}, bf16[320,512]{1,0:T(8,128)(2,1)S(1)}, bf16[320,512]{1,0:T(8,128)(2,1)S(1)}, bf16[48,512]{1,0:T(8,128)(2,1)S(1)}) custom-call(s32[3]{0:T(128)S(1)} %pad_add_fusion.pos_ref, bf16[2304,512]{1,0:T(8,128)(2,1)S(1)} %bitcast.53, bf16[2304,512]{1,0:T(8,128)(2,1)S(1)} %bitcast.51, f32[1,512]{1,0:T(1,128)S(1)} %bitcast.49, ...), custom_call_target="tpu_custom_call" | custom-call | flops 5040000000 | bytes 8096576 | tf_op jit(solution)/shard_map/pallas_call | solution.py:346
  88.1 0.1 collective-permute-start.19
  88.2 0.1 collective-permute-start.17
  88.3 0.3 collective-permute-start.18
  88.6 8.1 %shard_map.101.inner_ref = bf16[1296,512]{1,0:T(8,128)(2,1)S(1)} custom-call(s32[3]{0:T(128)S(1)} %pad_add_fusion.pos_ref, bf16[2304,512]{1,0:T(8,128)(2,1)S(1)} %bitcast.54, bf16[2304,512]{1,0:T(8,128)(2,1)S(1)} %bitcast.52, f32[1,512]{1,0:T(1,128)S(1)} %bitcast.50, bf16[4,2,144,512]{3,2,1,0:T(8,128)(2,1)S(1)} %pad_maximum_fusion.refs_0_, ...), custom_call_target="tpu_custom_call" | custom-call | flops 6480000000 | bytes 8981312 | tf_op jit(solution)/shard_map/pallas_call | solution.py:346
  96.7 0.2 collective-permute-done.19.diag_ref
  96.9 1.1 %collective-permute-done.17.lat_ref = bf16[320,512]{1,0:T(8,128)(2,1)S(1)} collective-permute-done((bf16[320,512]{1,0:T(8,128)(2,1)S(1)}, bf16[320,512]{1,0:T(8,128)(2,1)S(1)}, u32[]{:S(2)}, u32[]{:S(2)}) %collective-permute-start.17) | collective-permute-done | bytes 327712 | tf_op jit(solution)/shard_map/ppermute | solution.py:64
  98.1 3.2 %collective-permute-done.18.lon_ref = bf16[320,512]{1,0:T(8,128)(2,1)S(1)} collective-permute-done((bf16[320,512]{1,0:T(8,128)(2,1)S(1)}, bf16[320,512]{1,0:T(8,128)(2,1)S(1)}, u32[]{:S(2)}, u32[]{:S(2)}) %collective-permute-start.18) | collective-permute-done | bytes 327712 | tf_op jit(solution)/shard_map/ppermute | solution.py:64
  101.3 3.3 %to_grid.1 = bf16[1,2,24,48,512]{4,3,2,1,0:T(8,128)(2,1)} custom-call(bf16[1008,512]{1,0:T(8,128)(2,1)S(1)} %get-tuple-element.29.edge_ref, bf16[1296,512]{1,0:T(8,128)(2,1)S(1)} %shard_map.101.inner_ref, bf16[320,512]{1,0:T(8,128)(2,1)S(1)} %collective-permute-done.17.lat_ref, bf16[320,512]{1,0:T(8,128)(2,1)S(1)} %collective-permute-done.18.lon_ref, ...), custom_call_target="tpu_custom_call" | custom-call | flops 3000000000 | bytes 8000000 | tf_op jit(solution)/shard_map/to_grid/pallas_call | solution.py:423
  (59 shorter events, 0.5 us)
Async XLA Ops:
  1.5 16.9 %collective-permute-start.5 = (bf16[48,512]{1,0:T(8,128)(2,1)S(1)}, bf16[48,512]{1,0:T(8,128)(2,1)S(1)}, u32[]{:S(2)}, u32[]{:S(2)}) collective-permute-start(bf16[48,512]{1,0:T(8,128)(2,1)S(1)} %get-tuple-element.34), channel_id=1, source_target_pairs={{3,0},{0,1},{1,2},{2,3},{7,4},{4,5},{5,6},{6,7},{11,8},{8,9},{9,10... | collective-permute-start | bytes 147464 | tf_op jit(solution)/shard_map/ppermute | solution.py:40
  3.6 14.8 %collective-permute-start.4 = (bf16[48,512]{1,0:T(8,128)(2,1)S(1)}, bf16[48,512]{1,0:T(8,128)(2,1)S(1)}, u32[]{:S(2)}, u32[]{:S(2)}) collective-permute-start(bf16[48,512]{1,0:T(8,128)(2,1)S(1)} %get-tuple-element.34), channel_id=1, source_target_pairs={{2,0},{3,1},{0,2},{1,3},{6,4},{7,5},{4,6},{5,7},{10,8},{11,9},{8,1... | collective-permute-start | bytes 147464 | tf_op jit(solution)/shard_map/ppermute | solution.py:40
  6.1 11.9 %collective-permute-start.3 = (bf16[48,512]{1,0:T(8,128)(2,1)S(1)}, bf16[48,512]{1,0:T(8,128)(2,1)S(1)}, u32[]{:S(2)}, u32[]{:S(2)}) collective-permute-start(bf16[48,512]{1,0:T(8,128)(2,1)S(1)} %get-tuple-element.34), channel_id=1, source_target_pairs={{1,0},{2,1},{3,2},{0,3},{5,4},{6,5},{7,6},{4,7},{9,8},{10,9},{11,1... | collective-permute-start | bytes 147464 | tf_op jit(solution)/shard_map/ppermute | solution.py:40
  8.9 14.7 %collective-permute-start.2 = (bf16[80,512]{1,0:T(8,128)(2,1)S(1)}, bf16[80,512]{1,0:T(8,128)(2,1)S(1)}, u32[]{:S(2)}, u32[]{:S(2)}) collective-permute-start(bf16[80,512]{1,0:T(8,128)(2,1)S(1)} %fusion.5), channel_id=1, source_target_pairs={{9,0},{10,1},{11,2},{12,3},{13,4},{14,5},{15,6},{8,7},{17,8},{18,9... | collective-permute-start | bytes 245768 | tf_op jit(solution)/shard_map/ppermute | solution.py:64
  16.0 10.1 %collective-permute-start = (bf16[320,512]{1,0:T(8,128)(2,1)S(1)}, bf16[320,512]{1,0:T(8,128)(2,1)}, u32[]{:S(2)}, u32[]{:S(2)}) collective-permute-start(bf16[320,512]{1,0:T(8,128)(2,1)S(1)} %fusion.3), channel_id=1, source_target_pairs={{8,0},{9,1},{10,2},{11,3},{12,4},{13,5},{14,6},{15,7},{16,8},{17,9... | collective-permute-start | bytes 983048 | tf_op jit(solution)/shard_map/ppermute | solution.py:64
  17.9 9.6 %collective-permute-start.1 = (bf16[416,512]{1,0:T(8,128)(2,1)S(1)}, bf16[416,512]{1,0:T(8,128)(2,1)S(1)}, u32[]{:S(2)}, u32[]{:S(2)}) collective-permute-start(bf16[416,512]{1,0:T(8,128)(2,1)S(1)} %fusion.2), channel_id=1, source_target_pairs={{1,0},{2,1},{3,2},{4,3},{5,4},{6,5},{7,6},{0,7},{9,8},{10,9},{11,1... | collective-permute-start | bytes 1277960 | tf_op jit(solution)/shard_map/ppermute | solution.py:64
  18.8 3.4 %collective-permute-start.6 = (bf16[144,512]{1,0:T(8,128)(2,1)S(1)}, bf16[144,512]{1,0:T(8,128)(2,1)S(1)}, u32[]{:S(2)}, u32[]{:S(2)}) collective-permute-start(bf16[144,512]{1,0:T(8,128)(2,1)S(1)} %pad_maximum_fusion.4), channel_id=1, source_target_pairs={{32,0},{33,1},{34,2},{35,3},{36,4},{37,5},{38,6},{39,7},{40,8},{41... | collective-permute-start | bytes 442376 | tf_op jit(solution)/shard_map/ppermute | solution.py:40
  22.2 14.0 %collective-permute-start.9 = (bf16[336,512]{1,0:T(8,128)(2,1)S(1)}, bf16[336,512]{1,0:T(8,128)(2,1)S(1)}, u32[]{:S(2)}, u32[]{:S(2)}) collective-permute-start(bf16[336,512]{1,0:T(8,128)(2,1)S(1)} %constant_dynamic-update-slice_fusion), channel_id=1, source_target_pairs={{68,0},{69,1},{70,2},{71,3},{64,4},{65,5},{66,6},{67,7},{76,8},{77... | collective-permute-start | bytes 1032200 | tf_op jit(solution)/shard_map/ppermute | solution.py:40
  23.6 12.5 %collective-permute-start.8 = (bf16[336,512]{1,0:T(8,128)(2,1)S(1)}, bf16[336,512]{1,0:T(8,128)(2,1)S(1)}, u32[]{:S(2)}, u32[]{:S(2)}) collective-permute-start(bf16[336,512]{1,0:T(8,128)(2,1)S(1)} %constant_dynamic-update-slice_fusion), channel_id=1, source_target_pairs={{4,0},{5,1},{6,2},{7,3},{0,4},{1,5},{2,6},{3,7},{12,8},{13,9},{14,... | collective-permute-start | bytes 1032200 | tf_op jit(solution)/shard_map/ppermute | solution.py:40
  23.6 3.9 %copy-start.6 = (bf16[80,512]{1,0:T(8,128)(2,1)}, bf16[80,512]{1,0:T(8,128)(2,1)S(1)}, u32[]{:S(2)}) copy-start(bf16[80,512]{1,0:T(8,128)(2,1)S(1)} %collective-permute-done.2.both_ref) | copy-start | bytes 245764
  23.6 12.5 %collective-permute-start.7 = (bf16[336,512]{1,0:T(8,128)(2,1)S(1)}, bf16[336,512]{1,0:T(8,128)(2,1)S(1)}, u32[]{:S(2)}, u32[]{:S(2)}) collective-permute-start(bf16[336,512]{1,0:T(8,128)(2,1)S(1)} %constant_dynamic-update-slice_fusion), channel_id=1, source_target_pairs={{64,0},{65,1},{66,2},{67,3},{68,4},{69,5},{70,6},{71,7},{72,8},{73... | collective-permute-start | bytes 1032200 | tf_op jit(solution)/shard_map/ppermute | solution.py:40
  27.5 0.8 copy-start.5
  36.2 14.3 %copy-start.4 = (bf16[336,512]{1,0:T(8,128)(2,1)}, bf16[336,512]{1,0:T(8,128)(2,1)S(1)}, u32[]{:S(2)}) copy-start(bf16[336,512]{1,0:T(8,128)(2,1)S(1)} %collective-permute-done.7) | copy-start | bytes 1032196
  36.3 6.1 %collective-permute-start.11 = (bf16[4,48,512]{2,1,0:T(8,128)(2,1)S(1)}, bf16[4,48,512]{2,1,0:T(8,128)(2,1)S(1)}, u32[]{:S(2)}, u32[]{:S(2)}) collective-permute-start(bf16[4,48,512]{2,1,0:T(8,128)(2,1)S(1)} %get-tuple-element.38), channel_id=1, source_target_pairs={{16,0},{17,1},{18,2},{19,3},{20,4},{21,5},{22,6},{23,7},{24,8},{25... | collective-permute-start | bytes 589832 | tf_op jit(solution)/shard_map/ppermute | solution.py:40
  36.8 6.0 %collective-permute-start.10 = (bf16[4,48,512]{2,1,0:T(8,128)(2,1)S(1)}, bf16[4,48,512]{2,1,0:T(8,128)(2,1)S(1)}, u32[]{:S(2)}, u32[]{:S(2)}) collective-permute-start(bf16[4,48,512]{2,1,0:T(8,128)(2,1)S(1)} %get-tuple-element.38), channel_id=1, source_target_pairs={{8,0},{9,1},{10,2},{11,3},{12,4},{13,5},{14,6},{15,7},{16,8},{17,9... | collective-permute-start | bytes 589832 | tf_op jit(solution)/shard_map/ppermute | solution.py:40
  39.2 6.0 %collective-permute-start.12 = (bf16[4,48,512]{2,1,0:T(8,128)(2,1)S(1)}, bf16[4,48,512]{2,1,0:T(8,128)(2,1)S(1)}, u32[]{:S(2)}, u32[]{:S(2)}) collective-permute-start(bf16[4,48,512]{2,1,0:T(8,128)(2,1)S(1)} %get-tuple-element.38), channel_id=1, source_target_pairs={{24,0},{25,1},{26,2},{27,3},{28,4},{29,5},{30,6},{31,7},{0,8},{1,9... | collective-permute-start | bytes 589832 | tf_op jit(solution)/shard_map/ppermute | solution.py:40
  45.3 9.2 %collective-permute-start.13 = (bf16[4,4,48,512]{3,2,1,0:T(8,128)(2,1)S(1)}, bf16[4,4,48,512]{3,2,1,0:T(8,128)(2,1)S(1)}, u32[]{:S(2)}, u32[]{:S(2)}) collective-permute-start(bf16[4,4,48,512]{3,2,1,0:T(8,128)(2,1)S(1)} %pad_maximum_fusion.1.refs_0_), channel_id=1, source_target_pairs={{32,0},{33,1},{34,2},{35,3},{36,4},{37,5},{38,6},{39,7},{40,8},{41... | collective-permute-start | bytes 2359304 | tf_op jit(solution)/shard_map/ppermute | solution.py:40
  50.5 1.0 slice-start
  51.6 29.3 %collective-permute-start.16 = (bf16[4,2,144,512]{3,2,1,0:T(8,128)(2,1)S(1)}, bf16[4,2,144,512]{3,2,1,0:T(8,128)(2,1)S(1)}, u32[]{:S(2)}, u32[]{:S(2)}) collective-permute-start(bf16[4,2,144,512]{3,2,1,0:T(8,128)(2,1)S(1)} %pad_maximum_fusion.refs_0_), channel_id=1, source_target_pairs={{24,0},{25,1},{26,2},{27,3},{28,4},{29,5},{30,6},{31,7},{0,8},{1,9... | collective-permute-start | bytes 3538952 | tf_op jit(solution)/shard_map/ppermute | solution.py:40
  52.1 28.8 %collective-permute-start.15 = (bf16[4,2,144,512]{3,2,1,0:T(8,128)(2,1)S(1)}, bf16[4,2,144,512]{3,2,1,0:T(8,128)(2,1)S(1)}, u32[]{:S(2)}, u32[]{:S(2)}) collective-permute-start(bf16[4,2,144,512]{3,2,1,0:T(8,128)(2,1)S(1)} %pad_maximum_fusion.refs_0_), channel_id=1, source_target_pairs={{16,0},{17,1},{18,2},{19,3},{20,4},{21,5},{22,6},{23,7},{24,8},{25... | collective-permute-start | bytes 3538952 | tf_op jit(solution)/shard_map/ppermute | solution.py:40
  53.6 27.9 %collective-permute-start.14 = (bf16[4,2,144,512]{3,2,1,0:T(8,128)(2,1)S(1)}, bf16[4,2,144,512]{3,2,1,0:T(8,128)(2,1)S(1)}, u32[]{:S(2)}, u32[]{:S(2)}) collective-permute-start(bf16[4,2,144,512]{3,2,1,0:T(8,128)(2,1)S(1)} %pad_maximum_fusion.refs_0_), channel_id=1, source_target_pairs={{8,0},{9,1},{10,2},{11,3},{12,4},{13,5},{14,6},{15,7},{16,8},{17,9... | collective-permute-start | bytes 3538952 | tf_op jit(solution)/shard_map/ppermute | solution.py:40
  54.6 26.9 %copy-start = (f32[512]{0:T(512)S(1)}, f32[512]{0:T(512)}, u32[]{:S(2)}) copy-start(f32[512]{0:T(512)} %param.15) | copy-start | bytes 6148
  54.6 26.9 %copy-start.1 = (bf16[16,144,512]{2,1,0:T(8,128)(2,1)S(1)}, bf16[16,144,512]{2,1,0:T(8,128)(2,1)}, u32[]{:S(2)}) copy-start(bf16[16,144,512]{2,1,0:T(8,128)(2,1)} %get-tuple-element.21) | copy-start | bytes 7077892
  88.1 8.8 %collective-permute-start.19 = (bf16[48,512]{1,0:T(8,128)(2,1)S(1)}, bf16[48,512]{1,0:T(8,128)(2,1)S(1)}, u32[]{:S(2)}, u32[]{:S(2)}) collective-permute-start(bf16[48,512]{1,0:T(8,128)(2,1)S(1)} %get-tuple-element.32), channel_id=1, source_target_pairs={{31,0},{24,1},{25,2},{26,3},{27,4},{28,5},{29,6},{30,7},{7,8},{0,9... | collective-permute-start | bytes 147464 | tf_op jit(solution)/shard_map/ppermute | solution.py:64
  88.2 9.9 %collective-permute-start.17 = (bf16[320,512]{1,0:T(8,128)(2,1)S(1)}, bf16[320,512]{1,0:T(8,128)(2,1)S(1)}, u32[]{:S(2)}, u32[]{:S(2)}) collective-permute-start(bf16[320,512]{1,0:T(8,128)(2,1)S(1)} %get-tuple-element.30), channel_id=1, source_target_pairs={{24,0},{25,1},{26,2},{27,3},{28,4},{29,5},{30,6},{31,7},{0,8},{1,9... | collective-permute-start | bytes 983048 | tf_op jit(solution)/shard_map/ppermute | solution.py:64
  88.3 13.0 %copy-start.2 = (bf16[576,656]{1,0:T(8,128)(2,1)S(1)}, bf16[576,656]{1,0:T(8,128)(2,1)}, u32[]{:S(2)}) copy-start(bf16[576,656]{1,0:T(8,128)(2,1)} %constant.70.clone.mid_ref) | copy-start | bytes 2267140
  88.3 13.0 %copy-start.3 = (bf16[288,368]{1,0:T(8,128)(2,1)S(1)}, bf16[288,368]{1,0:T(8,128)(2,1)}, u32[]{:S(2)}) copy-start(bf16[288,368]{1,0:T(8,128)(2,1)} %constant.69.clone.top_ref) | copy-start | bytes 635908
  88.3 13.0 %collective-permute-start.18 = (bf16[320,512]{1,0:T(8,128)(2,1)S(1)}, bf16[320,512]{1,0:T(8,128)(2,1)S(1)}, u32[]{:S(2)}, u32[]{:S(2)}) collective-permute-start(bf16[320,512]{1,0:T(8,128)(2,1)S(1)} %get-tuple-element.31), channel_id=1, source_target_pairs={{7,0},{0,1},{1,2},{2,3},{3,4},{4,5},{5,6},{6,7},{15,8},{8,9},{9,10... | collective-permute-start | bytes 983048 | tf_op jit(solution)/shard_map/ppermute | solution.py:64

commit v5 on v4

--- a/solution.py
+++ b/solution.py
@@ -318,11 +318,14 @@
     def second(j):
         r = slice(j * sub, (j + 1) * sub)
         total = None
-        for c in range(4):
-            pre = lax.dot_general(normed[r], wu[512 * c : 512 * c + 512, :], NT, preferred_element_type=F32)
+        for c in range(2):
+            pre = lax.dot_general(normed[r], wu[1024 * c : 1024 * c + 1024, :], NT, preferred_element_type=F32)
             hidden = (0.5 * pre * (1.0 + lax.erf(pre * math.sqrt(0.5)))).astype(BF16)
-            part = lax.dot_general(hidden, wd[c], NT, preferred_element_type=F32)
-            total = part if total is None else total + part
+            for k in range(2):
+                part = lax.dot_general(
+                    hidden[:, 512 * k : 512 * k + 512], wd[2 * c + k], NT, preferred_element_type=F32
+                )
+                total = part if total is None else total + part
         out_ref[r] = (held[r].astype(F32) + total).astype(BF16)
 
     first(0)

time: 105 us -> 105 us (level)
  no operation moved by 1% of the time
where the time goes in v5:
time: 105 us
  Pallas kernels  47.7 us (45%)
  starting transfers between devices  30.2 us (29%)
  waiting for transfers between devices  18.1 us (17%)
  local copies, waits for them, and re-layouts  6.15 us (6%)
  other arithmetic  2.12 us (2%)
    ppermute x14, starting transfers between devices, send(): return lax.ppermute(block, AXES, pairs)  23 us
    pallas_call x1, Pallas kernels, attend(): pl.pallas_call(attn_kernel, grid=(10,), in_specs=[pl.BlockSpec(memory_spa...  21.8 us
    pallas_call x2, Pallas kernels, mlp(): pl.pallas_call(mlp_kernel, grid=(1,), in_specs=[pl.BlockSpec(memory_space...  14.6 us
    ppermute x14, waiting for transfers between devices, send(): return lax.ppermute(block, AXES, pairs)  12.1 us
    pallas_call x1, Pallas kernels, prep(): pl.pallas_call(prep_kernel, grid=(n // 4,), in_specs=[whole(a) for a in o...  7.9 us
    ppermute x6, starting transfers between devices, from_grid(): return lax.ppermute(block, AXES, pairs)  7.25 us
    ppermute x6, waiting for transfers between devices, from_grid(): return lax.ppermute(block, AXES, pairs)  6.01 us
    pallas_call x1, Pallas kernels, to_grid(): pl.pallas_call(place_kernel, out_shape=jax.ShapeDtypeStruct((1, 2, 24, 48...  3.33 us
  transfers between devices with their start and end apart: 20, of which 10 were waited for; matrix products, arithmetic and copies ran while one was open for 5% of the time, Pallas kernels for 36%

profile of v5, /device:TPU:1, one launch (start us, length us, event | category | flops | bytes accessed | tf_op | source)
XLA Modules:
  0.0 104.6 jit_solution(12727611629870235943)
XLA Ops:
  0.0 0.7 reshape.50
  0.8 0.8 bitcast_dynamic-update-slice_fusion.6
  1.5 2.1 %collective-permute-start.5 = (bf16[48,512]{1,0:T(8,128)(2,1)S(1)}, bf16[48,512]{1,0:T(8,128)(2,1)S(1)}, u32[]{:S(2)}, u32[]{:S(2)}) collective-permute-start(bf16[48,512]{1,0:T(8,128)(2,1)S(1)} %get-tuple-element.34), channel_id=1, source_target_pairs={{3,0},{0,1},{1,2},{2,3},{7,4},{4,5},{5,6},{6,7},{11,8},{8,9},{9,10... | collective-permute-start | bytes 147464 | tf_op jit(solution)/shard_map/ppermute | solution.py:40
  3.6 2.5 %collective-permute-start.4 = (bf16[48,512]{1,0:T(8,128)(2,1)S(1)}, bf16[48,512]{1,0:T(8,128)(2,1)S(1)}, u32[]{:S(2)}, u32[]{:S(2)}) collective-permute-start(bf16[48,512]{1,0:T(8,128)(2,1)S(1)} %get-tuple-element.34), channel_id=1, source_target_pairs={{2,0},{3,1},{0,2},{1,3},{6,4},{7,5},{4,6},{5,7},{10,8},{11,9},{8,1... | collective-permute-start | bytes 147464 | tf_op jit(solution)/shard_map/ppermute | solution.py:40
  6.1 1.2 %collective-permute-start.3 = (bf16[48,512]{1,0:T(8,128)(2,1)S(1)}, bf16[48,512]{1,0:T(8,128)(2,1)S(1)}, u32[]{:S(2)}, u32[]{:S(2)}) collective-permute-start(bf16[48,512]{1,0:T(8,128)(2,1)S(1)} %get-tuple-element.34), channel_id=1, source_target_pairs={{1,0},{2,1},{3,2},{0,3},{5,4},{6,5},{7,6},{4,7},{9,8},{10,9},{11,1... | collective-permute-start | bytes 147464 | tf_op jit(solution)/shard_map/ppermute | solution.py:40
  7.2 0.8 add_convert_fusion
  8.0 0.8 slice.72
  8.8 0.1 fusion.5
  8.9 6.1 %collective-permute-start.2 = (bf16[80,512]{1,0:T(8,128)(2,1)S(1)}, bf16[80,512]{1,0:T(8,128)(2,1)S(1)}, u32[]{:S(2)}, u32[]{:S(2)}) collective-permute-start(bf16[80,512]{1,0:T(8,128)(2,1)S(1)} %fusion.5), channel_id=1, source_target_pairs={{9,0},{10,1},{11,2},{12,3},{13,4},{14,5},{15,6},{8,7},{17,8},{18,9... | collective-permute-start | bytes 245768 | tf_op jit(solution)/shard_map/ppermute | solution.py:64
  15.0 1.0 slice.68
  16.0 0.2 collective-permute-start
  16.2 1.0 slice.70
  17.3 0.1 fusion.2
  17.3 0.6 pad.19.ids_ref
  17.9 0.5 collective-permute-start.1
  18.8 2.4 %collective-permute-start.6 = (bf16[144,512]{1,0:T(8,128)(2,1)S(1)}, bf16[144,512]{1,0:T(8,128)(2,1)S(1)}, u32[]{:S(2)}, u32[]{:S(2)}) collective-permute-start(bf16[144,512]{1,0:T(8,128)(2,1)S(1)} %pad_maximum_fusion.4), channel_id=1, source_target_pairs={{32,0},{33,1},{34,2},{35,3},{36,4},{37,5},{38,6},{39,7},{40,8},{41... | collective-permute-start | bytes 442376 | tf_op jit(solution)/shard_map/ppermute | solution.py:40
  21.3 1.0 collective-permute-done.6
  22.2 1.4 %collective-permute-start.9 = (bf16[336,512]{1,0:T(8,128)(2,1)S(1)}, bf16[336,512]{1,0:T(8,128)(2,1)S(1)}, u32[]{:S(2)}, u32[]{:S(2)}) collective-permute-start(bf16[336,512]{1,0:T(8,128)(2,1)S(1)} %constant_dynamic-update-slice_fusion), channel_id=1, source_target_pairs={{68,0},{69,1},{70,2},{71,3},{64,4},{65,5},{66,6},{67,7},{76,8},{77... | collective-permute-start | bytes 1032200 | tf_op jit(solution)/shard_map/ppermute | solution.py:40
  23.6 0.0 collective-permute-start.8
  23.6 2.5 %collective-permute-start.7 = (bf16[336,512]{1,0:T(8,128)(2,1)S(1)}, bf16[336,512]{1,0:T(8,128)(2,1)S(1)}, u32[]{:S(2)}, u32[]{:S(2)}) collective-permute-start(bf16[336,512]{1,0:T(8,128)(2,1)S(1)} %constant_dynamic-update-slice_fusion), channel_id=1, source_target_pairs={{64,0},{65,1},{66,2},{67,3},{68,4},{69,5},{70,6},{71,7},{72,8},{73... | collective-permute-start | bytes 1032200 | tf_op jit(solution)/shard_map/ppermute | solution.py:40
  26.1 1.4 %collective-permute-done.1.cols_ref = bf16[416,512]{1,0:T(8,128)(2,1)S(1)} collective-permute-done((bf16[416,512]{1,0:T(8,128)(2,1)S(1)}, bf16[416,512]{1,0:T(8,128)(2,1)S(1)}, u32[]{:S(2)}, u32[]{:S(2)}) %collective-permute-start.1) | collective-permute-done | bytes 426016 | tf_op jit(solution)/shard_map/ppermute | solution.py:64
  27.5 0.8 copy-done.5
  28.3 7.9 %prep.1 = (bf16[16,144,512]{2,1,0:T(8,128)(2,1)}, bf16[16,144,512]{2,1,0:T(8,128)(2,1)}, bf16[16,144,256]{2,1,0:T(8,128)(2,1)}) custom-call(bf16[2,24,48,512]{3,2,1,0:T(8,128)(2,1)} %bitcast.68, bf16[320,512]{1,0:T(8,128)(2,1)} %collective-permute-done.rows_ref, bf16[416,512]{1,0:T(8,128)(2,1)} %copy-done.5, bf16[80,512]{1,0:T(8,128)(2,1)} %copy-done.6, ...), custom_call_target="tpu_custom_call" | custom-call | flops 6000000000 | bytes 16000000 | tf_op jit(solution)/shard_map/prep/pallas_call | solution.py:134
  36.3 0.5 collective-permute-start.11
  36.8 2.4 %collective-permute-start.10 = (bf16[4,48,512]{2,1,0:T(8,128)(2,1)S(1)}, bf16[4,48,512]{2,1,0:T(8,128)(2,1)S(1)}, u32[]{:S(2)}, u32[]{:S(2)}) collective-permute-start(bf16[4,48,512]{2,1,0:T(8,128)(2,1)S(1)} %get-tuple-element.38), channel_id=1, source_target_pairs={{8,0},{9,1},{10,2},{11,3},{12,4},{13,5},{14,6},{15,7},{16,8},{17,9... | collective-permute-start | bytes 589832 | tf_op jit(solution)/shard_map/ppermute | solution.py:40
  39.2 3.2 %collective-permute-done.11 = bf16[4,48,512]{2,1,0:T(8,128)(2,1)S(1)} collective-permute-done((bf16[4,48,512]{2,1,0:T(8,128)(2,1)S(1)}, bf16[4,48,512]{2,1,0:T(8,128)(2,1)S(1)}, u32[]{:S(2)}, u32[]{:S(2)}) %collective-permute-start.11) | collective-permute-done | bytes 196640 | tf_op jit(solution)/shard_map/ppermute | solution.py:40
  42.4 0.5 collective-permute-done.10
  42.9 2.3 %collective-permute-done.12 = bf16[4,48,512]{2,1,0:T(8,128)(2,1)S(1)} collective-permute-done((bf16[4,48,512]{2,1,0:T(8,128)(2,1)S(1)}, bf16[4,48,512]{2,1,0:T(8,128)(2,1)S(1)}, u32[]{:S(2)}, u32[]{:S(2)}) %collective-permute-start.12) | collective-permute-done | bytes 196640 | tf_op jit(solution)/shard_map/ppermute | solution.py:40
  45.2 0.1 pad_maximum_fusion.1.refs_0_
  45.3 5.1 %collective-permute-start.13 = (bf16[4,4,48,512]{3,2,1,0:T(8,128)(2,1)S(1)}, bf16[4,4,48,512]{3,2,1,0:T(8,128)(2,1)S(1)}, u32[]{:S(2)}, u32[]{:S(2)}) collective-permute-start(bf16[4,4,48,512]{3,2,1,0:T(8,128)(2,1)S(1)} %pad_maximum_fusion.1.refs_0_), channel_id=1, source_target_pairs={{32,0},{33,1},{34,2},{35,3},{36,4},{37,5},{38,6},{39,7},{40,8},{41... | collective-permute-start | bytes 2359304 | tf_op jit(solution)/shard_map/ppermute | solution.py:40
  50.4 0.1 pad_add_fusion.pos_ref
  50.6 0.9 slice-done
  51.5 0.1 pad_maximum_fusion.refs_0_
  51.6 0.5 collective-permute-start.16
  52.1 1.6 %collective-permute-start.15 = (bf16[4,2,144,512]{3,2,1,0:T(8,128)(2,1)S(1)}, bf16[4,2,144,512]{3,2,1,0:T(8,128)(2,1)S(1)}, u32[]{:S(2)}, u32[]{:S(2)}) collective-permute-start(bf16[4,2,144,512]{3,2,1,0:T(8,128)(2,1)S(1)} %pad_maximum_fusion.refs_0_), channel_id=1, source_target_pairs={{16,0},{17,1},{18,2},{19,3},{20,4},{21,5},{22,6},{23,7},{24,8},{25... | collective-permute-start | bytes 3538952 | tf_op jit(solution)/shard_map/ppermute | solution.py:40
  53.6 0.9 collective-permute-start.14
  54.6 21.8 %attend.1 = bf16[16,144,512]{2,1,0:T(8,128)(2,1)S(1)} custom-call(s32[3]{0:T(128)S(1)} %pad_add_fusion.pos_ref, bf16[2304,512]{1,0:T(8,128)(2,1)} %bitcast.80, bf16[16,144,256]{2,1,0:T(8,128)(2,1)} %get-tuple-element.20.bias_ref, bf16[4,4,48,512]{3,2,1,0:T(8,128)(2,1)S(1)} %pad_maximum_fusion.1.refs_0_, ...), custom_call_target="tpu_custom_call" | custom-call | flops 20000000000 | bytes 12000000 | tf_op jit(solution)/shard_map/attend/pallas_call | solution.py:266
  76.4 4.5 %collective-permute-done.16.refs_3_ = bf16[4,2,144,512]{3,2,1,0:T(8,128)(2,1)S(1)} collective-permute-done((bf16[4,2,144,512]{3,2,1,0:T(8,128)(2,1)S(1)}, bf16[4,2,144,512]{3,2,1,0:T(8,128)(2,1)S(1)}, u32[]{:S(2)}, u32[]{:S(2)}) %collective-permute-start.16) | collective-permute-done | bytes 1179680 | tf_op jit(solution)/shard_map/ppermute | solution.py:40
  80.9 0.6 collective-permute-done.14.refs_1_
  81.5 6.6 %shard_map.100 = (bf16[1008,512]{1,0:T(8,128)(2,1)S(1)}, bf16[320,512]{1,0:T(8,128)(2,1)S(1)}, bf16[320,512]{1,0:T(8,128)(2,1)S(1)}, bf16[48,512]{1,0:T(8,128)(2,1)S(1)}) custom-call(s32[3]{0:T(128)S(1)} %pad_add_fusion.pos_ref, bf16[2304,512]{1,0:T(8,128)(2,1)S(1)} %bitcast.53, bf16[2304,512]{1,0:T(8,128)(2,1)S(1)} %bitcast.51, f32[1,512]{1,0:T(1,128)S(1)} %bitcast.49, ...), custom_call_target="tpu_custom_call" | custom-call | flops 5040000000 | bytes 8096576 | tf_op jit(solution)/shard_map/pallas_call | solution.py:349
  88.1 0.1 collective-permute-start.19
  88.2 0.1 collective-permute-start.17
  88.3 0.3 collective-permute-start.18
  88.6 8.1 %shard_map.101.inner_ref = bf16[1296,512]{1,0:T(8,128)(2,1)S(1)} custom-call(s32[3]{0:T(128)S(1)} %pad_add_fusion.pos_ref, bf16[2304,512]{1,0:T(8,128)(2,1)S(1)} %bitcast.54, bf16[2304,512]{1,0:T(8,128)(2,1)S(1)} %bitcast.52, f32[1,512]{1,0:T(1,128)S(1)} %bitcast.50, bf16[4,2,144,512]{3,2,1,0:T(8,128)(2,1)S(1)} %pad_maximum_fusion.refs_0_, ...), custom_call_target="tpu_custom_call" | custom-call | flops 6480000000 | bytes 8981312 | tf_op jit(solution)/shard_map/pallas_call | solution.py:349
  96.6 0.3 collective-permute-done.19.diag_ref
  96.9 1.1 %collective-permute-done.17.lat_ref = bf16[320,512]{1,0:T(8,128)(2,1)S(1)} collective-permute-done((bf16[320,512]{1,0:T(8,128)(2,1)S(1)}, bf16[320,512]{1,0:T(8,128)(2,1)S(1)}, u32[]{:S(2)}, u32[]{:S(2)}) %collective-permute-start.17) | collective-permute-done | bytes 327712 | tf_op jit(solution)/shard_map/ppermute | solution.py:64
  98.0 3.2 %collective-permute-done.18.lon_ref = bf16[320,512]{1,0:T(8,128)(2,1)S(1)} collective-permute-done((bf16[320,512]{1,0:T(8,128)(2,1)S(1)}, bf16[320,512]{1,0:T(8,128)(2,1)S(1)}, u32[]{:S(2)}, u32[]{:S(2)}) %collective-permute-start.18) | collective-permute-done | bytes 327712 | tf_op jit(solution)/shard_map/ppermute | solution.py:64
  101.3 3.3 %to_grid.1 = bf16[1,2,24,48,512]{4,3,2,1,0:T(8,128)(2,1)} custom-call(bf16[1008,512]{1,0:T(8,128)(2,1)S(1)} %get-tuple-element.29.edge_ref, bf16[1296,512]{1,0:T(8,128)(2,1)S(1)} %shard_map.101.inner_ref, bf16[320,512]{1,0:T(8,128)(2,1)S(1)} %collective-permute-done.17.lat_ref, bf16[320,512]{1,0:T(8,128)(2,1)S(1)} %collective-permute-done.18.lon_ref, ...), custom_call_target="tpu_custom_call" | custom-call | flops 3000000000 | bytes 8000000 | tf_op jit(solution)/shard_map/to_grid/pallas_call | solution.py:426
  (59 shorter events, 0.5 us)
Async XLA Ops:
  1.5 16.9 %collective-permute-start.5 = (bf16[48,512]{1,0:T(8,128)(2,1)S(1)}, bf16[48,512]{1,0:T(8,128)(2,1)S(1)}, u32[]{:S(2)}, u32[]{:S(2)}) collective-permute-start(bf16[48,512]{1,0:T(8,128)(2,1)S(1)} %get-tuple-element.34), channel_id=1, source_target_pairs={{3,0},{0,1},{1,2},{2,3},{7,4},{4,5},{5,6},{6,7},{11,8},{8,9},{9,10... | collective-permute-start | bytes 147464 | tf_op jit(solution)/shard_map/ppermute | solution.py:40
  3.6 14.8 %collective-permute-start.4 = (bf16[48,512]{1,0:T(8,128)(2,1)S(1)}, bf16[48,512]{1,0:T(8,128)(2,1)S(1)}, u32[]{:S(2)}, u32[]{:S(2)}) collective-permute-start(bf16[48,512]{1,0:T(8,128)(2,1)S(1)} %get-tuple-element.34), channel_id=1, source_target_pairs={{2,0},{3,1},{0,2},{1,3},{6,4},{7,5},{4,6},{5,7},{10,8},{11,9},{8,1... | collective-permute-start | bytes 147464 | tf_op jit(solution)/shard_map/ppermute | solution.py:40
  6.1 11.9 %collective-permute-start.3 = (bf16[48,512]{1,0:T(8,128)(2,1)S(1)}, bf16[48,512]{1,0:T(8,128)(2,1)S(1)}, u32[]{:S(2)}, u32[]{:S(2)}) collective-permute-start(bf16[48,512]{1,0:T(8,128)(2,1)S(1)} %get-tuple-element.34), channel_id=1, source_target_pairs={{1,0},{2,1},{3,2},{0,3},{5,4},{6,5},{7,6},{4,7},{9,8},{10,9},{11,1... | collective-permute-start | bytes 147464 | tf_op jit(solution)/shard_map/ppermute | solution.py:40
  8.9 14.7 %collective-permute-start.2 = (bf16[80,512]{1,0:T(8,128)(2,1)S(1)}, bf16[80,512]{1,0:T(8,128)(2,1)S(1)}, u32[]{:S(2)}, u32[]{:S(2)}) collective-permute-start(bf16[80,512]{1,0:T(8,128)(2,1)S(1)} %fusion.5), channel_id=1, source_target_pairs={{9,0},{10,1},{11,2},{12,3},{13,4},{14,5},{15,6},{8,7},{17,8},{18,9... | collective-permute-start | bytes 245768 | tf_op jit(solution)/shard_map/ppermute | solution.py:64
  16.0 10.1 %collective-permute-start = (bf16[320,512]{1,0:T(8,128)(2,1)S(1)}, bf16[320,512]{1,0:T(8,128)(2,1)}, u32[]{:S(2)}, u32[]{:S(2)}) collective-permute-start(bf16[320,512]{1,0:T(8,128)(2,1)S(1)} %fusion.3), channel_id=1, source_target_pairs={{8,0},{9,1},{10,2},{11,3},{12,4},{13,5},{14,6},{15,7},{16,8},{17,9... | collective-permute-start | bytes 983048 | tf_op jit(solution)/shard_map/ppermute | solution.py:64
  17.9 9.6 %collective-permute-start.1 = (bf16[416,512]{1,0:T(8,128)(2,1)S(1)}, bf16[416,512]{1,0:T(8,128)(2,1)S(1)}, u32[]{:S(2)}, u32[]{:S(2)}) collective-permute-start(bf16[416,512]{1,0:T(8,128)(2,1)S(1)} %fusion.2), channel_id=1, source_target_pairs={{1,0},{2,1},{3,2},{4,3},{5,4},{6,5},{7,6},{0,7},{9,8},{10,9},{11,1... | collective-permute-start | bytes 1277960 | tf_op jit(solution)/shard_map/ppermute | solution.py:64
  18.8 3.4 %collective-permute-start.6 = (bf16[144,512]{1,0:T(8,128)(2,1)S(1)}, bf16[144,512]{1,0:T(8,128)(2,1)S(1)}, u32[]{:S(2)}, u32[]{:S(2)}) collective-permute-start(bf16[144,512]{1,0:T(8,128)(2,1)S(1)} %pad_maximum_fusion.4), channel_id=1, source_target_pairs={{32,0},{33,1},{34,2},{35,3},{36,4},{37,5},{38,6},{39,7},{40,8},{41... | collective-permute-start | bytes 442376 | tf_op jit(solution)/shard_map/ppermute | solution.py:40
  22.2 14.0 %collective-permute-start.9 = (bf16[336,512]{1,0:T(8,128)(2,1)S(1)}, bf16[336,512]{1,0:T(8,128)(2,1)S(1)}, u32[]{:S(2)}, u32[]{:S(2)}) collective-permute-start(bf16[336,512]{1,0:T(8,128)(2,1)S(1)} %constant_dynamic-update-slice_fusion), channel_id=1, source_target_pairs={{68,0},{69,1},{70,2},{71,3},{64,4},{65,5},{66,6},{67,7},{76,8},{77... | collective-permute-start | bytes 1032200 | tf_op jit(solution)/shard_map/ppermute | solution.py:40
  23.6 12.5 %collective-permute-start.8 = (bf16[336,512]{1,0:T(8,128)(2,1)S(1)}, bf16[336,512]{1,0:T(8,128)(2,1)S(1)}, u32[]{:S(2)}, u32[]{:S(2)}) collective-permute-start(bf16[336,512]{1,0:T(8,128)(2,1)S(1)} %constant_dynamic-update-slice_fusion), channel_id=1, source_target_pairs={{4,0},{5,1},{6,2},{7,3},{0,4},{1,5},{2,6},{3,7},{12,8},{13,9},{14,... | collective-permute-start | bytes 1032200 | tf_op jit(solution)/shard_map/ppermute | solution.py:40
  23.6 3.9 %copy-start.6 = (bf16[80,512]{1,0:T(8,128)(2,1)}, bf16[80,512]{1,0:T(8,128)(2,1)S(1)}, u32[]{:S(2)}) copy-start(bf16[80,512]{1,0:T(8,128)(2,1)S(1)} %collective-permute-done.2.both_ref) | copy-start | bytes 245764
  23.6 12.5 %collective-permute-start.7 = (bf16[336,512]{1,0:T(8,128)(2,1)S(1)}, bf16[336,512]{1,0:T(8,128)(2,1)S(1)}, u32[]{:S(2)}, u32[]{:S(2)}) collective-permute-start(bf16[336,512]{1,0:T(8,128)(2,1)S(1)} %constant_dynamic-update-slice_fusion), channel_id=1, source_target_pairs={{64,0},{65,1},{66,2},{67,3},{68,4},{69,5},{70,6},{71,7},{72,8},{73... | collective-permute-start | bytes 1032200 | tf_op jit(solution)/shard_map/ppermute | solution.py:40
  27.5 0.8 copy-start.5
  36.2 14.3 %copy-start.4 = (bf16[336,512]{1,0:T(8,128)(2,1)}, bf16[336,512]{1,0:T(8,128)(2,1)S(1)}, u32[]{:S(2)}) copy-start(bf16[336,512]{1,0:T(8,128)(2,1)S(1)} %collective-permute-done.7) | copy-start | bytes 1032196
  36.3 6.1 %collective-permute-start.11 = (bf16[4,48,512]{2,1,0:T(8,128)(2,1)S(1)}, bf16[4,48,512]{2,1,0:T(8,128)(2,1)S(1)}, u32[]{:S(2)}, u32[]{:S(2)}) collective-permute-start(bf16[4,48,512]{2,1,0:T(8,128)(2,1)S(1)} %get-tuple-element.38), channel_id=1, source_target_pairs={{16,0},{17,1},{18,2},{19,3},{20,4},{21,5},{22,6},{23,7},{24,8},{25... | collective-permute-start | bytes 589832 | tf_op jit(solution)/shard_map/ppermute | solution.py:40
  36.8 6.0 %collective-permute-start.10 = (bf16[4,48,512]{2,1,0:T(8,128)(2,1)S(1)}, bf16[4,48,512]{2,1,0:T(8,128)(2,1)S(1)}, u32[]{:S(2)}, u32[]{:S(2)}) collective-permute-start(bf16[4,48,512]{2,1,0:T(8,128)(2,1)S(1)} %get-tuple-element.38), channel_id=1, source_target_pairs={{8,0},{9,1},{10,2},{11,3},{12,4},{13,5},{14,6},{15,7},{16,8},{17,9... | collective-permute-start | bytes 589832 | tf_op jit(solution)/shard_map/ppermute | solution.py:40
  39.2 6.0 %collective-permute-start.12 = (bf16[4,48,512]{2,1,0:T(8,128)(2,1)S(1)}, bf16[4,48,512]{2,1,0:T(8,128)(2,1)S(1)}, u32[]{:S(2)}, u32[]{:S(2)}) collective-permute-start(bf16[4,48,512]{2,1,0:T(8,128)(2,1)S(1)} %get-tuple-element.38), channel_id=1, source_target_pairs={{24,0},{25,1},{26,2},{27,3},{28,4},{29,5},{30,6},{31,7},{0,8},{1,9... | collective-permute-start | bytes 589832 | tf_op jit(solution)/shard_map/ppermute | solution.py:40
  45.3 9.2 %collective-permute-start.13 = (bf16[4,4,48,512]{3,2,1,0:T(8,128)(2,1)S(1)}, bf16[4,4,48,512]{3,2,1,0:T(8,128)(2,1)S(1)}, u32[]{:S(2)}, u32[]{:S(2)}) collective-permute-start(bf16[4,4,48,512]{3,2,1,0:T(8,128)(2,1)S(1)} %pad_maximum_fusion.1.refs_0_), channel_id=1, source_target_pairs={{32,0},{33,1},{34,2},{35,3},{36,4},{37,5},{38,6},{39,7},{40,8},{41... | collective-permute-start | bytes 2359304 | tf_op jit(solution)/shard_map/ppermute | solution.py:40
  50.5 1.0 slice-start
  51.6 29.3 %collective-permute-start.16 = (bf16[4,2,144,512]{3,2,1,0:T(8,128)(2,1)S(1)}, bf16[4,2,144,512]{3,2,1,0:T(8,128)(2,1)S(1)}, u32[]{:S(2)}, u32[]{:S(2)}) collective-permute-start(bf16[4,2,144,512]{3,2,1,0:T(8,128)(2,1)S(1)} %pad_maximum_fusion.refs_0_), channel_id=1, source_target_pairs={{24,0},{25,1},{26,2},{27,3},{28,4},{29,5},{30,6},{31,7},{0,8},{1,9... | collective-permute-start | bytes 3538952 | tf_op jit(solution)/shard_map/ppermute | solution.py:40
  52.1 28.8 %collective-permute-start.15 = (bf16[4,2,144,512]{3,2,1,0:T(8,128)(2,1)S(1)}, bf16[4,2,144,512]{3,2,1,0:T(8,128)(2,1)S(1)}, u32[]{:S(2)}, u32[]{:S(2)}) collective-permute-start(bf16[4,2,144,512]{3,2,1,0:T(8,128)(2,1)S(1)} %pad_maximum_fusion.refs_0_), channel_id=1, source_target_pairs={{16,0},{17,1},{18,2},{19,3},{20,4},{21,5},{22,6},{23,7},{24,8},{25... | collective-permute-start | bytes 3538952 | tf_op jit(solution)/shard_map/ppermute | solution.py:40
  53.6 27.9 %collective-permute-start.14 = (bf16[4,2,144,512]{3,2,1,0:T(8,128)(2,1)S(1)}, bf16[4,2,144,512]{3,2,1,0:T(8,128)(2,1)S(1)}, u32[]{:S(2)}, u32[]{:S(2)}) collective-permute-start(bf16[4,2,144,512]{3,2,1,0:T(8,128)(2,1)S(1)} %pad_maximum_fusion.refs_0_), channel_id=1, source_target_pairs={{8,0},{9,1},{10,2},{11,3},{12,4},{13,5},{14,6},{15,7},{16,8},{17,9... | collective-permute-start | bytes 3538952 | tf_op jit(solution)/shard_map/ppermute | solution.py:40
  54.6 26.9 %copy-start = (f32[512]{0:T(512)S(1)}, f32[512]{0:T(512)}, u32[]{:S(2)}) copy-start(f32[512]{0:T(512)} %param.15) | copy-start | bytes 6148
  54.6 26.9 %copy-start.1 = (bf16[16,144,512]{2,1,0:T(8,128)(2,1)S(1)}, bf16[16,144,512]{2,1,0:T(8,128)(2,1)}, u32[]{:S(2)}) copy-start(bf16[16,144,512]{2,1,0:T(8,128)(2,1)} %get-tuple-element.21) | copy-start | bytes 7077892
  88.1 8.8 %collective-permute-start.19 = (bf16[48,512]{1,0:T(8,128)(2,1)S(1)}, bf16[48,512]{1,0:T(8,128)(2,1)S(1)}, u32[]{:S(2)}, u32[]{:S(2)}) collective-permute-start(bf16[48,512]{1,0:T(8,128)(2,1)S(1)} %get-tuple-element.32), channel_id=1, source_target_pairs={{31,0},{24,1},{25,2},{26,3},{27,4},{28,5},{29,6},{30,7},{7,8},{0,9... | collective-permute-start | bytes 147464 | tf_op jit(solution)/shard_map/ppermute | solution.py:64
  88.2 9.9 %collective-permute-start.17 = (bf16[320,512]{1,0:T(8,128)(2,1)S(1)}, bf16[320,512]{1,0:T(8,128)(2,1)S(1)}, u32[]{:S(2)}, u32[]{:S(2)}) collective-permute-start(bf16[320,512]{1,0:T(8,128)(2,1)S(1)} %get-tuple-element.30), channel_id=1, source_target_pairs={{24,0},{25,1},{26,2},{27,3},{28,4},{29,5},{30,6},{31,7},{0,8},{1,9... | collective-permute-start | bytes 983048 | tf_op jit(solution)/shard_map/ppermute | solution.py:64
  88.2 13.0 %copy-start.2 = (bf16[576,656]{1,0:T(8,128)(2,1)S(1)}, bf16[576,656]{1,0:T(8,128)(2,1)}, u32[]{:S(2)}) copy-start(bf16[576,656]{1,0:T(8,128)(2,1)} %constant.70.clone.mid_ref) | copy-start | bytes 2267140
  88.2 13.0 %copy-start.3 = (bf16[288,368]{1,0:T(8,128)(2,1)S(1)}, bf16[288,368]{1,0:T(8,128)(2,1)}, u32[]{:S(2)}) copy-start(bf16[288,368]{1,0:T(8,128)(2,1)} %constant.69.clone.top_ref) | copy-start | bytes 635908
  88.3 13.0 %collective-permute-start.18 = (bf16[320,512]{1,0:T(8,128)(2,1)S(1)}, bf16[320,512]{1,0:T(8,128)(2,1)S(1)}, u32[]{:S(2)}, u32[]{:S(2)}) collective-permute-start(bf16[320,512]{1,0:T(8,128)(2,1)S(1)} %get-tuple-element.31), channel_id=1, source_target_pairs={{7,0},{0,1},{1,2},{2,3},{3,4},{4,5},{5,6},{6,7},{15,8},{8,9},{9,10... | collective-permute-start | bytes 983048 | tf_op jit(solution)/shard_map/ppermute | solution.py:64
